TPU v7x, 16 devices: a whole 2x2x2 slice. The times are simulated.
16 devices in a mesh: dp: 4 (over z, y), tp: 4 (over x, core).
Axes of the slice: x: 2, y: 2, z: 2, core: 2. Of those that a mesh axis runs over, the one named last changes fastest.
Arguments:
- hidden: bfloat16 [32768, 4096], P(('dp', 'tp')), parts along dimension 0
- norm_gain: float32 [4096], replicated
- w_query: bfloat16 [4096, 32, 128], P(None, 'tp')
- w_key: bfloat16 [4096, 32, 128], P(None, 'tp')
- w_value: bfloat16 [4096, 32, 128], P(None, 'tp')
Outputs:
- output 1: bfloat16 [32768, 32, 128], P('dp', 'tp'), parts along dimension 0
- output 2: bfloat16 [32768, 32, 128], P('dp', 'tp'), parts along dimension 0
- output 3: bfloat16 [32768, 32, 128], P('dp', 'tp'), parts along dimension 0
There are 4 independent parts. A program takes and returns all parts, laid end to end along the dimension named above; an argument that names none is the same for every part.
All inputs are finite; a program needn't handle non-finite values.
Results may differ from a plain program's by a relative error of at most 0.001.
Values are sent between devices in bfloat16 or wider.
A program may use at most 1 GiB of HBM per device.

v0:
```python
import jax
import jax.numpy as jnp
from jax import lax
from jax.sharding import PartitionSpec as P


def solution(mesh):
    def local_step(hidden_blk, norm_gain, wq_local, wk_local, wv_local):
        hidden_f32 = hidden_blk.astype(jnp.float32)
        mean_sq = jnp.mean(hidden_f32 * hidden_f32, axis=-1, keepdims=True)
        normed = (hidden_f32 * lax.rsqrt(mean_sq + 1e-6) * norm_gain).astype(jnp.bfloat16)
        gathered = lax.all_gather(normed, "tp", axis=0, tiled=True)
        q_out = jnp.einsum("td,dhk->thk", gathered, wq_local, preferred_element_type=jnp.float32).astype(jnp.bfloat16)
        k_out = jnp.einsum("td,dhk->thk", gathered, wk_local, preferred_element_type=jnp.float32).astype(jnp.bfloat16)
        v_out = jnp.einsum("td,dhk->thk", gathered, wv_local, preferred_element_type=jnp.float32).astype(jnp.bfloat16)
        return q_out, k_out, v_out

    row_spec = P(("dp", "tp"), None)
    head_spec = P(None, "tp", None)
    out_spec = P("dp", "tp", None)
    return jax.shard_map(local_step, mesh=mesh, in_specs=(row_spec, P(None), head_spec, head_spec, head_spec), out_specs=(out_spec, out_spec, out_spec), check_vma=False)
```

profile of v0, /device:TPU:0, one launch (start us, length us, event | category | flops | bytes accessed | tf_op | source)
XLA Modules:
  0.0 711.3 jit_solution(7317021036671275030)
XLA Ops:
  7.2 0.0 copy-start.1
  7.2 0.0 all-gather.2.cloned.1.call-start
  7.2 0.0 copy-start
  7.2 7.5 %fusion.6 = f32[2048]{0:T(1024)S(1)} fusion(bf16[2048,4096]{1,0:T(8,128)(2,1)} %param.5), kind=kLoop, calls=%fused_computation.8 | loop fusion | flops 25163776 | bytes 16785408 | tf_op jit(solution)/shard_map/reduce_sum | solution.py:10
  14.7 0.0 copy-done.1
  14.7 3.2 copy-done
  17.9 8.6 %fusion.8 = bf16[2048,4096]{1,0:T(8,128)(2,1)} fusion(bf16[2048,4096]{1,0:T(8,128)(2,1)S(1)} %copy-done, f32[4096]{0:T(1024)S(1)} %copy-done.1, f32[2048]{0:T(1024)S(1)} %add_rsqrt_fusion), kind=kLoop, calls=%fused_computation.10 | loop fusion | flops 33554432 | bytes 33579008 | tf_op jit(solution)/shard_map/convert_element_type | solution.py:11
  26.5 0.0 all-gather.2.cloned.1.call-update
  26.6 393.6 %all-gather.2.cloned.1.call-done = bf16[8192,4096]{1,0:T(8,128)(2,1)} async-done(((bf16[2048,4096]{1,0:T(8,128)(2,1)}), bf16[8192,4096]{1,0:T(8,128)(2,1)}) %all-gather.2.cloned.1.call-update) | async-done | bytes 67108880 | tf_op jit(solution)/shard_map/all_gather | solution.py:12
  420.1 77.6 %fusion.12 = bf16[8192,8,128]{2,0,1:T(8,128)(2,1)} fusion(bf16[8192,4096]{1,0:T(8,128)(2,1)} %all-gather.2.cloned.1.call-done, bf16[4096,8,128]{2,1,0:T(8,128)(2,1)} %param.8), kind=kOutput, calls=%fused_computation.12 | convolution fusion | flops 68727865344 | bytes 92274688 | tf_op jit(solution)/shard_map/td,dhk->thk/dot_general | solution.py:14
  497.7 0.0 copy-start.2
  497.7 18.9 %copy.12 = bf16[8192,8,128]{2,1,0:T(8,128)(2,1)} copy(bf16[8192,8,128]{2,0,1:T(8,128)(2,1)} %fusion.12) | data formatting | bytes 33554432
  516.6 0.0 copy-done.2
  516.6 75.2 %fusion.9 = bf16[8192,8,128]{2,0,1:T(8,128)(2,1)} fusion(bf16[8192,4096]{1,0:T(8,128)(2,1)} %all-gather.2.cloned.1.call-done, bf16[4096,8,128]{2,1,0:T(8,128)(2,1)S(1)} %copy-done.2), kind=kOutput, calls=%fused_computation.11 | convolution fusion | flops 68727865344 | bytes 92274688 | tf_op jit(solution)/shard_map/td,dhk->thk/dot_general | solution.py:13
  591.8 0.0 copy-start.3
  591.8 18.9 %copy.11 = bf16[8192,8,128]{2,1,0:T(8,128)(2,1)} copy(bf16[8192,8,128]{2,0,1:T(8,128)(2,1)} %fusion.9) | data formatting | bytes 33554432
  610.7 0.0 copy-done.3
  610.7 75.2 %fusion.15 = bf16[8192,8,128]{2,0,1:T(8,128)(2,1)} fusion(bf16[8192,4096]{1,0:T(8,128)(2,1)} %all-gather.2.cloned.1.call-done, bf16[4096,8,128]{2,1,0:T(8,128)(2,1)S(1)} %copy-done.3), kind=kOutput, calls=%fused_computation.13 | convolution fusion | flops 68727865344 | bytes 92274688 | tf_op jit(solution)/shard_map/td,dhk->thk/dot_general | solution.py:15
  685.9 18.6 %copy.13 = bf16[8192,8,128]{2,1,0:T(8,128)(2,1)} copy(bf16[8192,8,128]{2,0,1:T(8,128)(2,1)} %fusion.15) | data formatting | bytes 33554432
  (1 shorter events, 0.0 us)
Async XLA Ops:
  7.2 7.5 %copy-start.1 = (f32[4096]{0:T(1024)S(1)}, f32[4096]{0:T(1024)}, u32[]{:S(2)}) copy-start(f32[4096]{0:T(1024)} %param.6) | copy-start | bytes 49156
  7.2 412.9 %all-gather.2.cloned.1.call-start = ((), (), s32[]{:S(2)}) async-start(), calls=%async_computation | async-start | bytes 83886080 | tf_op jit(solution)/shard_map/all_gather | solution.py:12
  7.2 10.7 %copy-start = (bf16[2048,4096]{1,0:T(8,128)(2,1)S(1)}, bf16[2048,4096]{1,0:T(8,128)(2,1)}, u32[]{:S(2)}) copy-start(bf16[2048,4096]{1,0:T(8,128)(2,1)} %param.5) | copy-start | bytes 50331652
  497.7 18.9 %copy-start.2 = (bf16[4096,8,128]{2,1,0:T(8,128)(2,1)S(1)}, bf16[4096,8,128]{2,1,0:T(8,128)(2,1)}, u32[]{:S(2)}) copy-start(bf16[4096,8,128]{2,1,0:T(8,128)(2,1)} %param.7) | copy-start | bytes 25165828
  591.8 18.9 %copy-start.3 = (bf16[4096,8,128]{2,1,0:T(8,128)(2,1)S(1)}, bf16[4096,8,128]{2,1,0:T(8,128)(2,1)}, u32[]{:S(2)}) copy-start(bf16[4096,8,128]{2,1,0:T(8,128)(2,1)} %param.9) | copy-start | bytes 25165828
Sparse Core Ops, SparseCore 0:
  26.7 393.3 all-gather.1
where the time goes:
time: 712 us; the launch traced here: 711 us
  waiting for transfers between devices  394 us (55%)
  matrix products  228 us (32%)
  local copies, waits for them, and re-layouts  59.5 us (8%)
  other arithmetic  16.1 us (2%)
  between operations  14.1 us (2%)
    all_gather x1, waiting for transfers between devices, local_step(): gathered = lax.all_gather(normed, 'tp', axis=0, tiled=True)  394 us
    dot_general x1, matrix products, local_step(): jnp.einsum('td,dhk->thk', gathered, wk_local, preferred_element_type=jnp....  77.6 us
    dot_general x1, matrix products, local_step(): jnp.einsum('td,dhk->thk', gathered, wq_local, preferred_element_type=jnp....  75.2 us
    dot_general x1, matrix products, local_step(): jnp.einsum('td,dhk->thk', gathered, wv_local, preferred_element_type=jnp....  75.2 us
    unnamed x11, local copies, waits for them, and re-layouts  59.5 us
  transfers between devices with their start and end apart: 1, of which 1 were waited for; matrix products, arithmetic and copies ran while one was open for 0% of the time, Pallas kernels for 0%

commit v1 on v0

v1 whole, which is shorter than its diff:
```python
import functools

import jax
import jax.numpy as jnp
from jax import lax
from jax.experimental import pallas as pl
from jax.experimental.pallas import tpu as pltpu
from jax.sharding import PartitionSpec as P


HEADS = 8
HEAD_DIM = 128
COLS = HEADS * HEAD_DIM
MIB = 1024 * 1024
VMEM = 60 * MIB
PROJECT_VMEM = 42 * MIB

CHUNKS = (256, 256, 256, 256, 256, 256, 256, 128, 128)
BIG = 512


def normalize(x, norm_gain, start, rows, step):
    dim = x.shape[1]

    def body(x_ref, g_ref, n_ref):
        def piece(i, carry):
            at = pl.ds(pl.multiple_of(i * 16, 16), 16)
            v = x_ref[at, :].astype(jnp.float32)
            scale = lax.rsqrt(jnp.mean(v * v, axis=-1, keepdims=True) + 1e-6)
            n_ref[at, :] = (v * scale * g_ref[...]).astype(jnp.bfloat16)
            return carry

        lax.fori_loop(0, step // 16, piece, 0)

    return pl.pallas_call(
        body,
        grid=(rows // step,),
        in_specs=[
            pl.BlockSpec((step, dim), lambda i: (start // step + i, 0)),
            pl.BlockSpec((1, dim), lambda i: (0, 0)),
        ],
        out_specs=pl.BlockSpec((step, dim), lambda i: (i, 0)),
        out_shape=jax.ShapeDtypeStruct((rows, dim), jnp.bfloat16),
        compiler_params=pltpu.CompilerParams(vmem_limit_bytes=VMEM),
        cost_estimate=pl.CostEstimate(flops=8 * rows * dim, bytes_accessed=4 * rows * dim, transcendentals=rows),
        name="normalize",
    )(x, norm_gain.reshape(1, dim))


def join_weights(*weights):
    dim = weights[0].shape[0]
    step = 256

    def body(a_ref, b_ref, c_ref, w_ref, flat):
        for index, ref in enumerate((a_ref, b_ref, c_ref)):
            flat[...] = ref[...].astype(jnp.float32).reshape(step * HEADS, HEAD_DIM)
            for head in range(HEADS):
                part = flat[pl.ds(head, step, stride=HEADS), :]
                w_ref[index, :, head * HEAD_DIM : (head + 1) * HEAD_DIM] = part.astype(jnp.bfloat16)

    return pl.pallas_call(
        body,
        grid=(dim // step,),
        in_specs=[pl.BlockSpec((step, HEADS, HEAD_DIM), lambda i: (i, 0, 0))] * 3,
        out_specs=pl.BlockSpec((3, step, COLS), lambda i: (0, i, 0)),
        out_shape=jax.ShapeDtypeStruct((3, dim, COLS), jnp.bfloat16),
        scratch_shapes=[pltpu.VMEM((step * HEADS, HEAD_DIM), jnp.float32)],
        compiler_params=pltpu.CompilerParams(vmem_limit_bytes=VMEM),
        cost_estimate=pl.CostEstimate(flops=6 * dim * COLS, bytes_accessed=12 * dim * COLS, transcendentals=0),
        name="join_weights",
    )(*weights)


def product(n_ref, w_ref, total):
    rows = n_ref.shape[0]

    def pair(i, carry):
        cols = pl.ds(pl.multiple_of(i * 2 * HEAD_DIM, 2 * HEAD_DIM), 2 * HEAD_DIM)
        part = jnp.dot(n_ref[...], w_ref[0, :, cols], preferred_element_type=jnp.float32)
        for side in range(2):
            total[pl.ds(2 * i + side, rows, stride=HEADS), :] = part[:, side * HEAD_DIM : (side + 1) * HEAD_DIM]
        return carry

    lax.fori_loop(0, HEADS // 2, pair, 0)


def emit(total, out_ref):
    rows = out_ref.shape[0]
    step = 32

    def piece(i, carry):
        src = pl.ds(pl.multiple_of(i * step * HEADS, step * HEADS), step * HEADS)
        dst = pl.ds(pl.multiple_of(i * step, step), step)
        out_ref[dst] = total[src, :].reshape(step, HEADS, HEAD_DIM).astype(out_ref.dtype)
        return carry

    lax.fori_loop(0, rows // step, piece, 0)


def project(n, w, owners, which, outs, tokens):
    rows, dim = n.shape
    blocks = rows // BIG

    def body(owners_ref, n_ref, w_ref, *refs):
        q_ref, k_ref, v_ref, total = refs[-4:]
        product(n_ref, w_ref, total)
        j = pl.program_id(1)
        for index, out_ref in enumerate((q_ref, k_ref, v_ref)):
            pl.when(j == index)(functools.partial(emit, total, out_ref))

    out_spec = pl.BlockSpec((BIG, HEADS, HEAD_DIM), lambda r, j, owners: (owners[which] * blocks + r, 0, 0))
    return pl.pallas_call(
        body,
        grid_spec=pltpu.PrefetchScalarGridSpec(
            num_scalar_prefetch=1,
            grid=(blocks, 3),
            in_specs=[
                pl.BlockSpec((BIG, dim), lambda r, j, owners: (r, 0)),
                pl.BlockSpec((1, dim, COLS), lambda r, j, owners: (j, 0, 0)),
            ]
            + [pl.BlockSpec(memory_space=pl.ANY)] * len(outs),
            out_specs=[out_spec] * 3,
            scratch_shapes=[pltpu.VMEM((BIG * HEADS, HEAD_DIM), jnp.float32)],
        ),
        out_shape=[jax.ShapeDtypeStruct((tokens, HEADS, HEAD_DIM), jnp.bfloat16)] * 3,
        input_output_aliases={3 + i: i for i in range(len(outs))},
        compiler_params=pltpu.CompilerParams(vmem_limit_bytes=PROJECT_VMEM),
        cost_estimate=pl.CostEstimate(
            flops=6 * rows * dim * COLS,
            bytes_accessed=2 * (rows * dim + 3 * blocks * dim * COLS + 3 * rows * COLS),
            transcendentals=0,
        ),
        name="project",
    )(owners, n, w, *outs)


def project_two(near, far, w, owners, start, block, outs, tokens):
    rows, dim = near.shape

    def body(owners_ref, near_ref, far_ref, w_ref, *refs):
        q_ref, k_ref, v_ref, total = refs[-4:]
        j, r = pl.program_id(0), pl.program_id(1)
        for index, n_ref in enumerate((near_ref, far_ref)):
            pl.when(r == index)(functools.partial(product, n_ref, w_ref, total))
        for index, out_ref in enumerate((q_ref, k_ref, v_ref)):
            pl.when(j == index)(functools.partial(emit, total, out_ref))

    def out_spec(index):
        def at_step(j, r, owners):
            side = jnp.where(j < index, 0, jnp.where(j > index, 1, r))
            return (owners[2 + side] * (block // rows) + start // rows, 0, 0)

        return pl.BlockSpec((rows, HEADS, HEAD_DIM), at_step)

    whole = pl.BlockSpec((rows, dim), lambda j, r, owners: (0, 0))
    return pl.pallas_call(
        body,
        grid_spec=pltpu.PrefetchScalarGridSpec(
            num_scalar_prefetch=1,
            grid=(3, 2),
            in_specs=[whole, whole, pl.BlockSpec((1, dim, COLS), lambda j, r, owners: (j, 0, 0))]
            + [pl.BlockSpec(memory_space=pl.ANY)] * 3,
            out_specs=[out_spec(i) for i in range(3)],
            scratch_shapes=[pltpu.VMEM((rows * HEADS, HEAD_DIM), jnp.float32)],
        ),
        out_shape=[jax.ShapeDtypeStruct((tokens, HEADS, HEAD_DIM), jnp.bfloat16)] * 3,
        input_output_aliases={4 + i: i for i in range(3)},
        compiler_params=pltpu.CompilerParams(vmem_limit_bytes=PROJECT_VMEM),
        cost_estimate=pl.CostEstimate(
            flops=12 * rows * dim * COLS,
            bytes_accessed=2 * (2 * rows * dim + 3 * dim * COLS + 6 * rows * COLS),
            transcendentals=0,
        ),
        name="project_two",
    )(owners, near, far, w, *outs)


def solution(mesh):
    across = [(0, 2), (1, 3), (2, 0), (3, 1)]
    beside = [(0, 1), (1, 0), (2, 3), (3, 2)]

    def inner(hidden_blk, norm_gain, wq_local, wk_local, wv_local):
        block, _ = hidden_blk.shape
        tokens = 4 * block
        me = lax.axis_index("tp").astype(jnp.int32)
        owners = me ^ jnp.arange(4, dtype=jnp.int32)
        starts = [sum(CHUNKS[:i]) for i in range(len(CHUNKS))]

        x, near = hidden_blk, []
        for s, c in zip(starts, CHUNKS):
            mine = normalize(x, norm_gain, s, c, 128)
            x, mine = lax.optimization_barrier((x, mine))
            near.append(lax.ppermute(mine, "tp", across))
        own = normalize(x, norm_gain, 0, block, 128)
        paired = lax.ppermute(own, "tp", beside)
        w = join_weights(wq_local, wk_local, wv_local)

        far = {}

        def arrive(outs, *chunks):
            got = lax.optimization_barrier((tuple(near[i] for i in chunks), tuple(outs)))
            for i, a in zip(chunks, got[0]):
                near[i] = a
                far[i] = lax.ppermute(a, "tp", beside)
            return got[1]

        outs = project(own, w, owners, 0, (), tokens)
        outs = arrive(outs, 0, 1)
        outs = project(paired, w, owners, 1, outs, tokens)
        outs = arrive(outs, 2)
        after = {0: 3, 3: 4}
        for i, (s, c) in enumerate(zip(starts, CHUNKS)):
            if i > 4:
                outs = arrive(outs, i)
            outs = project_two(near[i], far[i], w, owners, s, block, outs, tokens)
            if i in after:
                outs = arrive(outs, after[i])
        return tuple(outs)

    row_spec = P(("dp", "tp"), None)
    head_spec = P(None, "tp", None)
    out_spec = P("dp", "tp", None)
    return jax.shard_map(inner, mesh=mesh, in_specs=(row_spec, P(None), head_spec, head_spec, head_spec), out_specs=(out_spec, out_spec, out_spec), check_vma=False)
```

time: 712 us -> 597 us (0.84)
  Pallas kernels: 0 us -> 448 us
  waiting for transfers between devices: 394 us -> 130 us
  matrix products: 228 us -> 0 us
  local copies, waits for them, and re-layouts: 59.5 us -> 0.02 us
  other arithmetic: 16.1 us -> 0.01 us
  starting transfers between devices: 0.04 us -> 15.8 us
  between operations: 14.1 us -> 0.69 us
    pallas_call x0 -> x22, Pallas kernels: none -> 448 us  [the longest x9 216 us: project_two(): pl.pallas_call(body, grid_spec=pltpu.PrefetchScalarGridSpec(num_scalar_pr...]
    all_gather x1 -> x0, waiting for transfers between devices: 394 us -> none  [local_step(): gathered = lax.all_gather(normed, 'tp', axis=0, tiled=True)]
    dot_general x3 -> x0, matrix products: 228 us -> none  [the longest x1 77.6 us: local_step(): jnp.einsum('td,dhk->thk', gathered, wk_local, preferred_element_type=jnp....]
    ppermute x0 -> x19, waiting for transfers between devices: none -> 130 us  [the longest x9 120 us: inner(): near.append(lax.ppermute(mine, 'tp', across))]
    unnamed x11 -> x10, local copies, waits for them, and re-layouts: 59.5 us -> 0.02 us
    ppermute x0 -> x19, starting transfers between devices: none -> 15.8 us  [the longest x9 13.9 us: inner(): near.append(lax.ppermute(mine, 'tp', across))]
    convert_element_type x1 -> x0, other arithmetic: 8.65 us -> none  [local_step(): (hidden_f32 * lax.rsqrt(mean_sq + 1e-06) * norm_gain).astype(jnp.bfloat16)]
    reduce_sum x1 -> x0, other arithmetic: 7.46 us -> none  [local_step(): mean_sq = jnp.mean(hidden_f32 * hidden_f32, axis=-1, keepdims=True)]
  transfers between devices with their start and end apart: 1 -> 19, of which waited for: 1 -> 10; matrix products, arithmetic and copies ran while one was open for 0% -> 0% of each run, Pallas kernels for 0% -> 61%
where the time goes in v1:
time: 597 us; the launch traced here: 595 us
  Pallas kernels  448 us (75%)
  waiting for transfers between devices  130 us (22%)
  starting transfers between devices  15.8 us (3%)
    pallas_call x9, Pallas kernels, project_two(): pl.pallas_call(body, grid_spec=pltpu.PrefetchScalarGridSpec(num_scalar_pr...  216 us
    pallas_call x2, Pallas kernels, project(): pl.pallas_call(body, grid_spec=pltpu.PrefetchScalarGridSpec(num_scalar_pr...  142 us
    ppermute x9, waiting for transfers between devices, inner(): near.append(lax.ppermute(mine, 'tp', across))  120 us
    pallas_call x10, Pallas kernels, normalize(): pl.pallas_call(body, grid=(rows // step,), in_specs=[pl.BlockSpec((step,...  63.6 us
    pallas_call x1, Pallas kernels, join_weights(): pl.pallas_call(body, grid=(dim // step,), in_specs=[pl.BlockSpec((step, H...  26.8 us
    ppermute x9, starting transfers between devices, inner(): near.append(lax.ppermute(mine, 'tp', across))  13.9 us
  transfers between devices with their start and end apart: 19, of which 10 were waited for; matrix products, arithmetic and copies ran while one was open for 0% of the time, Pallas kernels for 61%

profile of v1, /device:TPU:0, one launch (start us, length us, event | category | flops | bytes accessed | tf_op | source)
XLA Modules:
  0.0 595.2 jit_solution(8922948715893274867)
XLA Ops:
  0.6 4.6 normalize.10
  5.2 4.6 normalize.11
  9.9 4.6 normalize.12
  14.5 4.6 normalize.13
  19.0 4.6 normalize.14
  23.6 4.6 normalize.15
  28.2 4.6 normalize.16
  39.6 24.6 %normalize.19.n_ref = bf16[2048,4096]{1,0:T(8,128)(2,1)} custom-call(bf16[2048,4096]{1,0:T(8,128)(2,1)} %x_ref.10, f32[1,4096]{1,0:T(1,128)} %bitcast.10), custom_call_target="tpu_custom_call" | custom-call | flops 67108864 | bytes 33554432 | tf_op jit(solution)/shard_map/normalize/pallas_call | solution.py:35
  69.5 26.8 %join_weights.1.w_ref = bf16[3,4096,1024]{2,1,0:T(8,128)(2,1)} custom-call(bf16[4096,8,128]{2,1,0:T(8,128)(2,1)} %a_ref.1, bf16[4096,8,128]{2,1,0:T(8,128)(2,1)} %b_ref.1, bf16[4096,8,128]{2,1,0:T(8,128)(2,1)} %c_ref.1), custom_call_target="tpu_custom_call" | custom-call | flops 25165824 | bytes 50331648 | tf_op jit(solution)/shard_map/join_weights/pallas_call | solution.py:61
  96.3 71.1 %project.2 = (bf16[8192,8,128]{2,1,0:T(8,128)(2,1)}, bf16[8192,8,128]{2,1,0:T(8,128)(2,1)}, bf16[8192,8,128]{2,1,0:T(8,128)(2,1)}) custom-call(s32[4]{0:T(128)S(1)} %iota_xor_fusion.owners_ref, bf16[2048,4096]{1,0:T(8,128)(2,1)} %normalize.19.n_ref, bf16[3,4096,1024]{2,1,0:T(8,128)(2,1)} %join_weights.1.w_ref), custom_call_target="tpu_custom_call" | custom-call | flops 51539607552 | bytes 130023424 | tf_op jit(solution)/shard_map/project/pallas_call | solution.py:112
  167.5 36.7 %collective-permute-done.7.near_ref = bf16[256,4096]{1,0:T(8,128)(2,1)} collective-permute-done((bf16[256,4096]{1,0:T(8,128)(2,1)}, bf16[256,4096]{1,0:T(8,128)(2,1)}, u32[]{:S(2)}, u32[]{:S(2)}) %collective-permute-start.7) | collective-permute-done | bytes 2097184 | tf_op jit(solution)/shard_map/ppermute | solution.py:193
  206.2 42.9 %collective-permute-done.6.near_ref = bf16[256,4096]{1,0:T(8,128)(2,1)} collective-permute-done((bf16[256,4096]{1,0:T(8,128)(2,1)}, bf16[256,4096]{1,0:T(8,128)(2,1)}, u32[]{:S(2)}, u32[]{:S(2)}) %collective-permute-start.6) | collective-permute-done | bytes 2097184 | tf_op jit(solution)/shard_map/ppermute | solution.py:193
  249.6 71.1 %project.3 = (bf16[8192,8,128]{2,1,0:T(8,128)(2,1)}, bf16[8192,8,128]{2,1,0:T(8,128)(2,1)}, bf16[8192,8,128]{2,1,0:T(8,128)(2,1)}) custom-call(s32[4]{0:T(128)S(1)} %iota_xor_fusion.owners_ref, bf16[2048,4096]{1,0:T(8,128)(2,1)} %collective-permute-done.10.n_ref, ...), custom_call_target="tpu_custom_call", output_to_operand_aliasing={{0}: (3, {}), {1}: (4, {}), {2}: (5, {})} | custom-call | flops 51539607552 | bytes 130023424 | tf_op jit(solution)/shard_map/project/pallas_call | solution.py:112
  320.7 25.3 %project_two.9 = (bf16[8192,8,128]{2,1,0:T(8,128)(2,1)}, bf16[8192,8,128]{2,1,0:T(8,128)(2,1)}, bf16[8192,8,128]{2,1,0:T(8,128)(2,1)}) custom-call(s32[4]{0:T(128)S(1)} %iota_xor_fusion.owners_ref, bf16[256,4096]{1,0:T(8,128)(2,1)} %collective-permute-done.6.near_ref, ...), custom_call_target="tpu_custom_call", output_to_operand_aliasing={{0}: (4, {}), {1}: (5, {}), {2}: (6, {})} | custom-call | flops 12884901888 | bytes 32505856 | tf_op jit(solution)/shard_map/project_two/pallas_call | solution.py:156
  346.5 25.3 %project_two.10 = (bf16[8192,8,128]{2,1,0:T(8,128)(2,1)}, bf16[8192,8,128]{2,1,0:T(8,128)(2,1)}, bf16[8192,8,128]{2,1,0:T(8,128)(2,1)}) custom-call(s32[4]{0:T(128)S(1)} %iota_xor_fusion.owners_ref, bf16[256,4096]{1,0:T(8,128)(2,1)} %collective-permute-done.7.near_ref, ...), custom_call_target="tpu_custom_call", output_to_operand_aliasing={{0}: (4, {}), {1}: (5, {}), {2}: (6, {})} | custom-call | flops 12884901888 | bytes 32505856 | tf_op jit(solution)/shard_map/project_two/pallas_call | solution.py:156
  371.8 24.8 %project_two.11 = (bf16[8192,8,128]{2,1,0:T(8,128)(2,1)}, bf16[8192,8,128]{2,1,0:T(8,128)(2,1)}, bf16[8192,8,128]{2,1,0:T(8,128)(2,1)}) custom-call(s32[4]{0:T(128)S(1)} %iota_xor_fusion.owners_ref, bf16[256,4096]{1,0:T(8,128)(2,1)S(1)} %collective-permute-done.9.near_ref, ...), custom_call_target="tpu_custom_call", output_to_operand_aliasing={{0}: (4, {}), {1}: (5, {}), {2}: (6, {})} | custom-call | flops 12884901888 | bytes 32505856 | tf_op jit(solution)/shard_map/project_two/pallas_call | solution.py:156
  396.6 24.8 %project_two.12 = (bf16[8192,8,128]{2,1,0:T(8,128)(2,1)}, bf16[8192,8,128]{2,1,0:T(8,128)(2,1)}, bf16[8192,8,128]{2,1,0:T(8,128)(2,1)}) custom-call(s32[4]{0:T(128)S(1)} %iota_xor_fusion.owners_ref, bf16[256,4096]{1,0:T(8,128)(2,1)S(1)} %collective-permute-done.5.near_ref, ...), custom_call_target="tpu_custom_call", output_to_operand_aliasing={{0}: (4, {}), {1}: (5, {}), {2}: (6, {})} | custom-call | flops 12884901888 | bytes 32505856 | tf_op jit(solution)/shard_map/project_two/pallas_call | solution.py:156
  425.8 25.3 %project_two.13 = (bf16[8192,8,128]{2,1,0:T(8,128)(2,1)}, bf16[8192,8,128]{2,1,0:T(8,128)(2,1)}, bf16[8192,8,128]{2,1,0:T(8,128)(2,1)}) custom-call(s32[4]{0:T(128)S(1)} %iota_xor_fusion.owners_ref, bf16[256,4096]{1,0:T(8,128)(2,1)} %collective-permute-done.4.near_ref, ...), custom_call_target="tpu_custom_call", output_to_operand_aliasing={{0}: (4, {}), {1}: (5, {}), {2}: (6, {})} | custom-call | flops 12884901888 | bytes 32505856 | tf_op jit(solution)/shard_map/project_two/pallas_call | solution.py:156
  451.1 18.6 %collective-permute-done.3.near_ref = bf16[256,4096]{1,0:T(8,128)(2,1)S(1)} collective-permute-done((bf16[256,4096]{1,0:T(8,128)(2,1)S(1)}, bf16[256,4096]{1,0:T(8,128)(2,1)S(1)}, u32[]{:S(2)}, u32[]{:S(2)}) %collective-permute-start.3) | collective-permute-done | bytes 2097184 | tf_op jit(solution)/shard_map/ppermute | solution.py:193
  473.9 25.0 %project_two.14 = (bf16[8192,8,128]{2,1,0:T(8,128)(2,1)}, bf16[8192,8,128]{2,1,0:T(8,128)(2,1)}, bf16[8192,8,128]{2,1,0:T(8,128)(2,1)}) custom-call(s32[4]{0:T(128)S(1)} %iota_xor_fusion.owners_ref, bf16[256,4096]{1,0:T(8,128)(2,1)S(1)} %collective-permute-done.3.near_ref, ...), custom_call_target="tpu_custom_call", output_to_operand_aliasing={{0}: (4, {}), {1}: (5, {}), {2}: (6, {})} | custom-call | flops 12884901888 | bytes 32505856 | tf_op jit(solution)/shard_map/project_two/pallas_call | solution.py:156
  498.9 18.9 %collective-permute-done.2.near_ref = bf16[256,4096]{1,0:T(8,128)(2,1)S(1)} collective-permute-done((bf16[256,4096]{1,0:T(8,128)(2,1)S(1)}, bf16[256,4096]{1,0:T(8,128)(2,1)S(1)}, u32[]{:S(2)}, u32[]{:S(2)}) %collective-permute-start.2) | collective-permute-done | bytes 2097184 | tf_op jit(solution)/shard_map/ppermute | solution.py:193
  522.0 24.8 %project_two.15 = (bf16[8192,8,128]{2,1,0:T(8,128)(2,1)}, bf16[8192,8,128]{2,1,0:T(8,128)(2,1)}, bf16[8192,8,128]{2,1,0:T(8,128)(2,1)}) custom-call(s32[4]{0:T(128)S(1)} %iota_xor_fusion.owners_ref, bf16[256,4096]{1,0:T(8,128)(2,1)S(1)} %collective-permute-done.2.near_ref, ...), custom_call_target="tpu_custom_call", output_to_operand_aliasing={{0}: (4, {}), {1}: (5, {}), {2}: (6, {})} | custom-call | flops 12884901888 | bytes 32505856 | tf_op jit(solution)/shard_map/project_two/pallas_call | solution.py:156
  549.4 20.3 %project_two.16 = (bf16[8192,8,128]{2,1,0:T(8,128)(2,1)}, bf16[8192,8,128]{2,1,0:T(8,128)(2,1)}, bf16[8192,8,128]{2,1,0:T(8,128)(2,1)}) custom-call(s32[4]{0:T(128)S(1)} %iota_xor_fusion.owners_ref, bf16[128,4096]{1,0:T(8,128)(2,1)S(1)} %collective-permute-done.1.near_ref, ...), custom_call_target="tpu_custom_call", output_to_operand_aliasing={{0}: (4, {}), {1}: (5, {}), {2}: (6, {})} | custom-call | flops 6442450944 | bytes 28835840 | tf_op jit(solution)/shard_map/project_two/pallas_call | solution.py:156
  575.0 20.2 %project_two.17 = (bf16[8192,8,128]{2,1,0:T(8,128)(2,1)}, bf16[8192,8,128]{2,1,0:T(8,128)(2,1)}, bf16[8192,8,128]{2,1,0:T(8,128)(2,1)}) custom-call(s32[4]{0:T(128)S(1)} %iota_xor_fusion.owners_ref, bf16[128,4096]{1,0:T(8,128)(2,1)S(1)} %collective-permute-done.near_ref, ...), custom_call_target="tpu_custom_call", output_to_operand_aliasing={{0}: (4, {}), {1}: (5, {}), {2}: (6, {})} | custom-call | flops 6442450944 | bytes 28835840 | tf_op jit(solution)/shard_map/project_two/pallas_call | solution.py:156
  (47 shorter events, 35.9 us)
Async XLA Ops:
  64.3 184.8 %collective-permute-start.10 = (bf16[2048,4096]{1,0:T(8,128)(2,1)}, bf16[2048,4096]{1,0:T(8,128)(2,1)}, u32[]{:S(2)}, u32[]{:S(2)}) collective-permute-start(bf16[2048,4096]{1,0:T(8,128)(2,1)} %normalize.19.n_ref), channel_id=1, source_target_pairs={{0,1},{1,0},{2,3},{3,2},{4,5},{5,4},{6,7},{7,6},{8,9},{9,8},{10,11... | collective-permute-start | bytes 50331656 | tf_op jit(solution)/shard_map/ppermute | solution.py:195
  65.0 356.4 %collective-permute-start.4 = (bf16[256,4096]{1,0:T(8,128)(2,1)}, bf16[256,4096]{1,0:T(8,128)(2,1)}, u32[]{:S(2)}, u32[]{:S(2)}) collective-permute-start(bf16[256,4096]{1,0:T(8,128)(2,1)} %normalize.14), channel_id=1, source_target_pairs={{0,2},{1,3},{2,0},{3,1},{4,6},{5,7},{6,4},{7,5},{8,10},{9,11},{10,... | collective-permute-start | bytes 6291464 | tf_op jit(solution)/shard_map/ppermute | solution.py:193
  67.5 278.5 %collective-permute-start.5 = (bf16[256,4096]{1,0:T(8,128)(2,1)}, bf16[256,4096]{1,0:T(8,128)(2,1)S(1)}, u32[]{:S(2)}, u32[]{:S(2)}) collective-permute-start(bf16[256,4096]{1,0:T(8,128)(2,1)} %normalize.13), channel_id=1, source_target_pairs={{0,2},{1,3},{2,0},{3,1},{4,6},{5,7},{6,4},{7,5},{8,10},{9,11},{10,... | collective-permute-start | bytes 6291464 | tf_op jit(solution)/shard_map/ppermute | solution.py:193
  67.5 136.6 %collective-permute-start.7 = (bf16[256,4096]{1,0:T(8,128)(2,1)}, bf16[256,4096]{1,0:T(8,128)(2,1)}, u32[]{:S(2)}, u32[]{:S(2)}) collective-permute-start(bf16[256,4096]{1,0:T(8,128)(2,1)} %normalize.11), channel_id=1, source_target_pairs={{0,2},{1,3},{2,0},{3,1},{4,6},{5,7},{6,4},{7,5},{8,10},{9,11},{10,... | collective-permute-start | bytes 6291464 | tf_op jit(solution)/shard_map/ppermute | solution.py:193
  69.5 179.6 %collective-permute-start.6 = (bf16[256,4096]{1,0:T(8,128)(2,1)}, bf16[256,4096]{1,0:T(8,128)(2,1)}, u32[]{:S(2)}, u32[]{:S(2)}) collective-permute-start(bf16[256,4096]{1,0:T(8,128)(2,1)} %normalize.10), channel_id=1, source_target_pairs={{0,2},{1,3},{2,0},{3,1},{4,6},{5,7},{6,4},{7,5},{8,10},{9,11},{10,... | collective-permute-start | bytes 6291464 | tf_op jit(solution)/shard_map/ppermute | solution.py:193
  96.3 107.8 %copy-start.2 = (bf16[256,4096]{1,0:T(8,128)(2,1)S(1)}, bf16[256,4096]{1,0:T(8,128)(2,1)}, u32[]{:S(2)}) copy-start(bf16[256,4096]{1,0:T(8,128)(2,1)} %normalize.12) | copy-start | bytes 6291460
  204.2 116.5 %collective-permute-start.9 = (bf16[256,4096]{1,0:T(8,128)(2,1)S(1)}, bf16[256,4096]{1,0:T(8,128)(2,1)S(1)}, u32[]{:S(2)}, u32[]{:S(2)}) collective-permute-start(bf16[256,4096]{1,0:T(8,128)(2,1)S(1)} %copy-done.2), channel_id=1, source_target_pairs={{0,2},{1,3},{2,0},{3,1},{4,6},{5,7},{6,4},{7,5},{8,10},{9,11},{10,... | collective-permute-start | bytes 6291464 | tf_op jit(solution)/shard_map/ppermute | solution.py:193
  249.1 71.6 %collective-permute-start.8 = (bf16[256,4096]{1,0:T(8,128)(2,1)}, bf16[256,4096]{1,0:T(8,128)(2,1)S(1)}, u32[]{:S(2)}, u32[]{:S(2)}) collective-permute-start(bf16[256,4096]{1,0:T(8,128)(2,1)} %collective-permute-done.6.near_ref), channel_id=1, source_target_pairs={{0,1},{1,0},{2,3},{3,2},{4,5},{5,4},{6,7},{7,6},{8,9},{9,8},{10,11... | collective-permute-start | bytes 6291464 | tf_op jit(solution)/shard_map/ppermute | solution.py:204
  249.1 97.4 %collective-permute-start.13 = (bf16[256,4096]{1,0:T(8,128)(2,1)}, bf16[256,4096]{1,0:T(8,128)(2,1)S(1)}, u32[]{:S(2)}, u32[]{:S(2)}) collective-permute-start(bf16[256,4096]{1,0:T(8,128)(2,1)} %collective-permute-done.7.near_ref), channel_id=1, source_target_pairs={{0,1},{1,0},{2,3},{3,2},{4,5},{5,4},{6,7},{7,6},{8,9},{9,8},{10,11... | collective-permute-start | bytes 6291464 | tf_op jit(solution)/shard_map/ppermute | solution.py:204
  320.7 51.1 %collective-permute-start.12 = (bf16[256,4096]{1,0:T(8,128)(2,1)S(1)}, bf16[256,4096]{1,0:T(8,128)(2,1)S(1)}, u32[]{:S(2)}, u32[]{:S(2)}) collective-permute-start(bf16[256,4096]{1,0:T(8,128)(2,1)S(1)} %collective-permute-done.9.near_ref), channel_id=1, source_target_pairs={{0,1},{1,0},{2,3},{3,2},{4,5},{5,4},{6,7},{7,6},{8,9},{9,8},{10,11... | collective-permute-start | bytes 6291464 | tf_op jit(solution)/shard_map/ppermute | solution.py:204
  346.0 50.6 %collective-permute-start.11 = (bf16[256,4096]{1,0:T(8,128)(2,1)S(1)}, bf16[256,4096]{1,0:T(8,128)(2,1)S(1)}, u32[]{:S(2)}, u32[]{:S(2)}) collective-permute-start(bf16[256,4096]{1,0:T(8,128)(2,1)S(1)} %collective-permute-done.5.near_ref), channel_id=1, source_target_pairs={{0,1},{1,0},{2,3},{3,2},{4,5},{5,4},{6,7},{7,6},{8,9},{9,8},{10,11... | collective-permute-start | bytes 6291464 | tf_op jit(solution)/shard_map/ppermute | solution.py:204
  396.6 24.9 %copy-start.1 = (bf16[256,4096]{1,0:T(8,128)(2,1)S(1)}, bf16[256,4096]{1,0:T(8,128)(2,1)}, u32[]{:S(2)}) copy-start(bf16[256,4096]{1,0:T(8,128)(2,1)} %normalize.15) | copy-start | bytes 6291460
  421.4 48.4 %copy-start = (bf16[256,4096]{1,0:T(8,128)(2,1)S(1)}, bf16[256,4096]{1,0:T(8,128)(2,1)}, u32[]{:S(2)}) copy-start(bf16[256,4096]{1,0:T(8,128)(2,1)} %normalize.16) | copy-start | bytes 6291460
  421.4 4.4 collective-permute-start.14
  421.5 48.3 %collective-permute-start.3 = (bf16[256,4096]{1,0:T(8,128)(2,1)S(1)}, bf16[256,4096]{1,0:T(8,128)(2,1)S(1)}, u32[]{:S(2)}, u32[]{:S(2)}) collective-permute-start(bf16[256,4096]{1,0:T(8,128)(2,1)S(1)} %copy-done.1), channel_id=1, source_target_pairs={{0,2},{1,3},{2,0},{3,1},{4,6},{5,7},{6,4},{7,5},{8,10},{9,11},{10,... | collective-permute-start | bytes 6291464 | tf_op jit(solution)/shard_map/ppermute | solution.py:193
  469.8 48.1 %copy-start.4 = (bf16[128,4096]{1,0:T(8,128)(2,1)S(1)}, bf16[128,4096]{1,0:T(8,128)(2,1)}, u32[]{:S(2)}) copy-start(bf16[128,4096]{1,0:T(8,128)(2,1)} %normalize.17) | copy-start | bytes 3145732
  469.8 4.2 collective-permute-start.15
  469.8 48.0 %collective-permute-start.2 = (bf16[256,4096]{1,0:T(8,128)(2,1)S(1)}, bf16[256,4096]{1,0:T(8,128)(2,1)S(1)}, u32[]{:S(2)}, u32[]{:S(2)}) collective-permute-start(bf16[256,4096]{1,0:T(8,128)(2,1)S(1)} %copy-done), channel_id=1, source_target_pairs={{0,2},{1,3},{2,0},{3,1},{4,6},{5,7},{6,4},{7,5},{8,10},{9,11},{10,... | collective-permute-start | bytes 6291464 | tf_op jit(solution)/shard_map/ppermute | solution.py:193
  517.8 29.1 %copy-start.3 = (bf16[128,4096]{1,0:T(8,128)(2,1)S(1)}, bf16[128,4096]{1,0:T(8,128)(2,1)}, u32[]{:S(2)}) copy-start(bf16[128,4096]{1,0:T(8,128)(2,1)} %normalize.18) | copy-start | bytes 3145732
  517.8 4.2 collective-permute-start.16
  517.8 28.9 %collective-permute-start.1 = (bf16[128,4096]{1,0:T(8,128)(2,1)S(1)}, bf16[128,4096]{1,0:T(8,128)(2,1)S(1)}, u32[]{:S(2)}, u32[]{:S(2)}) collective-permute-start(bf16[128,4096]{1,0:T(8,128)(2,1)S(1)} %copy-done.4), channel_id=1, source_target_pairs={{0,2},{1,3},{2,0},{3,1},{4,6},{5,7},{6,4},{7,5},{8,10},{9,11},{10,... | collective-permute-start | bytes 3145736 | tf_op jit(solution)/shard_map/ppermute | solution.py:193
  546.8 2.7 collective-permute-start.17
  546.9 25.4 %collective-permute-start = (bf16[128,4096]{1,0:T(8,128)(2,1)S(1)}, bf16[128,4096]{1,0:T(8,128)(2,1)S(1)}, u32[]{:S(2)}, u32[]{:S(2)}) collective-permute-start(bf16[128,4096]{1,0:T(8,128)(2,1)S(1)} %copy-done.3), channel_id=1, source_target_pairs={{0,2},{1,3},{2,0},{3,1},{4,6},{5,7},{6,4},{7,5},{8,10},{9,11},{10,... | collective-permute-start | bytes 3145736 | tf_op jit(solution)/shard_map/ppermute | solution.py:193
  572.3 2.7 collective-permute-start.18

commit v2 on v0

v2 whole, which is shorter than its diff:
```python
import jax
import jax.numpy as jnp
from jax import lax
from jax.experimental import pallas as pl
from jax.experimental.pallas import tpu as pltpu
from jax.sharding import PartitionSpec as P


HEADS = 8
HEAD_DIM = 128
COLS = HEADS * HEAD_DIM
PIECE = 2 * HEAD_DIM
PIECES = COLS // PIECE
RING = 6
MIB = 1024 * 1024
VMEM = 60 * MIB
PROJECT_VMEM = 42 * MIB

CHUNKS = (256, 256, 256, 256, 256, 256, 256, 128, 128)
BIG = 512
NORM_ROWS = 128


def normalize_rows(x_ref, g_ref, n_ref):
    def piece(i, carry):
        at = pl.ds(pl.multiple_of(i * 32, 32), 32)
        v = x_ref[at, :].astype(jnp.float32)
        scale = lax.rsqrt(jnp.mean(v * v, axis=-1, keepdims=True) + 1e-6)
        n_ref[at, :] = (v * scale * g_ref[...]).astype(jnp.bfloat16)
        return carry

    lax.fori_loop(0, x_ref.shape[0] // 32, piece, 0)


def normalize_first(x, norm_gain, rows):
    dim = x.shape[1]
    step = 64
    return pl.pallas_call(
        normalize_rows,
        grid=(rows // step,),
        in_specs=[pl.BlockSpec((step, dim), lambda i: (i, 0)), pl.BlockSpec((1, dim), lambda i: (0, 0))],
        out_specs=pl.BlockSpec((step, dim), lambda i: (i, 0)),
        out_shape=jax.ShapeDtypeStruct((rows, dim), jnp.bfloat16),
        compiler_params=pltpu.CompilerParams(vmem_limit_bytes=VMEM),
        cost_estimate=pl.CostEstimate(flops=8 * rows * dim, bytes_accessed=4 * rows * dim, transcendentals=rows),
        name="normalize_first",
    )(x, norm_gain)


def normalize_all(x, norm_gain, chunks):
    block, dim = x.shape
    step = NORM_ROWS
    bounds = [sum(chunks[:i]) // step for i in range(len(chunks) + 1)]

    def body(x_ref, g_ref, *refs):
        outs, (held, sem) = refs[:-2], refs[-2:]
        b = pl.program_id(0)
        slot = lax.rem(b, 2)

        def copies(b, slot, do):
            do(pltpu.make_async_copy(held.at[slot], outs[0].at[pl.ds(b * step, step)], sem.at[slot, 0]))
            for i in range(1, len(chunks)):

                @pl.when((b >= bounds[i]) & (b < bounds[i + 1]))
                def _(i=i):
                    to = outs[i].at[pl.ds((b - bounds[i]) * step, step)]
                    do(pltpu.make_async_copy(held.at[slot], to, sem.at[slot, 1]))

        pl.when(b >= 2)(lambda: copies(b - 2, slot, lambda c: c.wait()))
        normalize_rows(x_ref, g_ref, held.at[slot])
        copies(b, slot, lambda c: c.start())

        @pl.when(b == block // step - 1)
        def _():
            copies(b - 1, 1 - slot, lambda c: c.wait())
            copies(b, slot, lambda c: c.wait())

    return pl.pallas_call(
        body,
        grid=(block // step,),
        in_specs=[pl.BlockSpec((step, dim), lambda i: (i, 0)), pl.BlockSpec((1, dim), lambda i: (0, 0))],
        out_specs=[pl.BlockSpec(memory_space=pl.ANY)] * len(chunks),
        out_shape=[jax.ShapeDtypeStruct((rows, dim), jnp.bfloat16) for rows in (block,) + chunks[1:]],
        scratch_shapes=[pltpu.VMEM((2, step, dim), jnp.bfloat16), pltpu.SemaphoreType.DMA((2, 2))],
        compiler_params=pltpu.CompilerParams(vmem_limit_bytes=VMEM),
        cost_estimate=pl.CostEstimate(flops=8 * block * dim, bytes_accessed=6 * block * dim, transcendentals=block),
        name="normalize_all",
    )(x, norm_gain)


def join_weights(*weights):
    dim = weights[0].shape[0]
    step, sub = 256, 64

    def body(a_ref, b_ref, c_ref, w_ref, flat):
        def some(i, carry):
            at = pl.ds(pl.multiple_of(i * sub, sub), sub)
            for index, ref in enumerate((a_ref, b_ref, c_ref)):
                flat[index] = ref[at].astype(jnp.float32).reshape(sub * HEADS, HEAD_DIM)
            for index in range(3):
                for head in range(HEADS):
                    part = flat[index, pl.ds(head, sub, stride=HEADS), :]
                    lanes = slice(head % 2 * HEAD_DIM, (head % 2 + 1) * HEAD_DIM)
                    w_ref[index * PIECES + head // 2, at, lanes] = part.astype(jnp.bfloat16)
            return carry

        lax.fori_loop(0, step // sub, some, 0)

    return pl.pallas_call(
        body,
        grid=(dim // step,),
        in_specs=[pl.BlockSpec((step, HEADS, HEAD_DIM), lambda i: (i, 0, 0))] * 3,
        out_specs=pl.BlockSpec((3 * PIECES, step, PIECE), lambda i: (0, i, 0)),
        out_shape=jax.ShapeDtypeStruct((3 * PIECES, dim, PIECE), jnp.bfloat16),
        scratch_shapes=[pltpu.VMEM((3, sub * HEADS, HEAD_DIM), jnp.float32)],
        compiler_params=pltpu.CompilerParams(vmem_limit_bytes=VMEM),
        cost_estimate=pl.CostEstimate(flops=6 * dim * COLS, bytes_accessed=12 * dim * COLS, transcendentals=0),
        name="join_weights",
    )(*weights)


def project(parts, w, owners, outs, tokens):
    arrays = [p[0] for p in parts]
    dim = w.shape[1]
    sizes = [p[1] for p in parts]
    offsets = [sum(sizes[:i]) for i in range(len(sizes))]
    rows = sum(sizes)
    blocks = arrays[0].shape[0] // sizes[0]
    steps = 3 * blocks
    slots = min(blocks, 2)
    quarter = rows // PIECES

    def body(owners_ref, *refs):
        n_hbm, w_hbm = refs[: len(parts)], refs[len(parts)]
        q_out, k_out, v_out, n_buf, w_buf, total, stage, n_sem, w_sem, o_sem = refs[-10:]

        def fetch(b, do):
            slot = lax.rem(b, slots)
            for i, size in enumerate(sizes):
                src = n_hbm[i].at[pl.ds(pl.multiple_of(b * size, size), size)]
                do(pltpu.make_async_copy(src, n_buf.at[slot, pl.ds(offsets[i], size)], n_sem.at[slot, i]))

        def piece(p, do):
            slot = lax.rem(p, RING)
            do(pltpu.make_async_copy(w_hbm.at[lax.rem(p, 3 * PIECES)], w_buf.at[slot], w_sem.at[slot]))

        def store(s, do):
            b, j = s // 3, lax.rem(s, 3)
            slot = lax.rem(s, 2)
            for index, out in enumerate((q_out, k_out, v_out)):

                @pl.when(j == index)
                def _(out=out):
                    for i, (_, size, which, start) in enumerate(parts):
                        first = owners_ref[which] * (tokens // 4) + start + b * size
                        src = stage.at[slot, pl.ds(offsets[i], size)]
                        do(pltpu.make_async_copy(src, out.at[pl.ds(first, size)], o_sem.at[slot, i]))

        def emit(slot, start, size):
            src = pl.ds(pl.multiple_of(start * HEADS, size * HEADS), size * HEADS)
            got = total[slot, src, :].reshape(size, HEADS, HEAD_DIM).astype(jnp.bfloat16)
            stage[slot, pl.ds(pl.multiple_of(start, size), size)] = got

        def begin(copy):
            copy.start()

        def end(copy):
            copy.wait()

        fetch(0, begin)
        for p in range(RING - 1):
            piece(p, begin)

        def step(s, carry):
            b, j = s // 3, lax.rem(s, 3)
            slot = lax.rem(s, 2)
            pl.when(s >= 3)(lambda: store(s - 3, end))

            @pl.when(j == 0)
            def _():
                fetch(b, end)
                if blocks > 1:
                    pl.when(b + 1 < blocks)(lambda: fetch(b + 1, begin))

            def part(i, carry):
                p = s * PIECES + i
                piece(p, end)
                pl.when(p + RING - 1 < steps * PIECES)(lambda: piece(p + RING - 1, begin))
                emit(1 - slot, i * quarter, quarter)
                got = jnp.dot(n_buf[lax.rem(b, slots)], w_buf[lax.rem(p, RING)], preferred_element_type=jnp.float32)
                for side in range(2):
                    total[slot, pl.ds(2 * i + side, rows, stride=HEADS), :] = got[:, side * HEAD_DIM : (side + 1) * HEAD_DIM]
                return carry

            lax.fori_loop(0, PIECES, part, 0)
            pl.when(s >= 1)(lambda: store(s - 1, begin))
            return carry

        lax.fori_loop(0, steps, step, 0)
        last = steps - 1
        store(last - 2, end)
        lax.fori_loop(0, PIECES, lambda i, carry: (emit(last % 2, i * quarter, quarter), carry)[1], 0)
        store(last, begin)
        store(last - 1, end)
        store(last, end)

    return pl.pallas_call(
        body,
        in_specs=[pl.BlockSpec(memory_space=pltpu.SMEM)] + [pl.BlockSpec(memory_space=pltpu.HBM)] * (len(parts) + 1 + len(outs)),
        out_specs=[pl.BlockSpec(memory_space=pl.ANY)] * 3,
        out_shape=[jax.ShapeDtypeStruct((tokens, HEADS, HEAD_DIM), jnp.bfloat16)] * 3,
        scratch_shapes=[
            pltpu.VMEM((slots, rows, dim), jnp.bfloat16),
            pltpu.VMEM((RING, dim, PIECE), jnp.bfloat16),
            pltpu.VMEM((2, rows * HEADS, HEAD_DIM), jnp.float32),
            pltpu.VMEM((2, rows, HEADS, HEAD_DIM), jnp.bfloat16),
            pltpu.SemaphoreType.DMA((slots, len(parts))),
            pltpu.SemaphoreType.DMA((RING,)),
            pltpu.SemaphoreType.DMA((2, len(parts))),
        ],
        input_output_aliases={len(parts) + 2 + i: i for i in range(len(outs))},
        compiler_params=pltpu.CompilerParams(vmem_limit_bytes=PROJECT_VMEM),
        cost_estimate=pl.CostEstimate(
            flops=6 * blocks * rows * dim * COLS,
            bytes_accessed=2 * blocks * (rows * dim + 3 * dim * COLS + 3 * rows * COLS),
            transcendentals=0,
        ),
        name="project",
    )(owners, *arrays, w, *outs)


def solution(mesh):
    across = [(0, 2), (1, 3), (2, 0), (3, 1)]
    beside = [(0, 1), (1, 0), (2, 3), (3, 2)]

    def inner(hidden_blk, norm_gain, wq_local, wk_local, wv_local):
        block, dim = hidden_blk.shape
        tokens = 4 * block
        me = lax.axis_index("tp").astype(jnp.int32)
        owners = me ^ jnp.arange(4, dtype=jnp.int32)
        starts = [sum(CHUNKS[:i]) for i in range(len(CHUNKS))]

        gain = norm_gain.reshape(1, dim)
        mine = [normalize_first(hidden_blk, gain, CHUNKS[0])]
        near = [lax.ppermute(mine[0], "tp", across)]
        own, *rest = normalize_all(hidden_blk, gain, CHUNKS)
        for m in rest:
            near.append(lax.ppermute(m, "tp", across))
        paired = lax.ppermute(own, "tp", beside)
        w = join_weights(wq_local, wk_local, wv_local)

        far = {}

        def arrive(outs, *chunks):
            got = lax.optimization_barrier((tuple(near[i] for i in chunks), tuple(outs)))
            for i, a in zip(chunks, got[0]):
                near[i] = a
                far[i] = lax.ppermute(a, "tp", beside)
            return got[1]

        outs = project([(own, BIG, 0, 0)], w, owners, (), tokens)
        outs = arrive(outs, 0, 1)
        outs = project([(paired, BIG, 1, 0)], w, owners, outs, tokens)
        outs = arrive(outs, 2)
        after = {1: 3, 3: 4}
        for i, (s, c) in enumerate(zip(starts, CHUNKS)):
            if i > 4:
                outs = arrive(outs, i)
            outs = project([(near[i], c, 2, s), (far[i], c, 3, s)], w, owners, outs, tokens)
            if i in after:
                outs = arrive(outs, after[i])
        return tuple(outs)

    row_spec = P(("dp", "tp"), None)
    head_spec = P(None, "tp", None)
    out_spec = P("dp", "tp", None)
    return jax.shard_map(inner, mesh=mesh, in_specs=(row_spec, P(None), head_spec, head_spec, head_spec), out_specs=(out_spec, out_spec, out_spec), check_vma=False)
```

time: 712 us -> 490 us (0.69)
  Pallas kernels: 0 us -> 355 us
  waiting for transfers between devices: 394 us -> 117 us
  matrix products: 228 us -> 0 us
  local copies, waits for them, and re-layouts: 59.5 us -> 0.02 us
  other arithmetic: 16.1 us -> 0.01 us
  starting transfers between devices: 0.04 us -> 15.5 us
  between operations: 14.1 us -> 0.82 us
    all_gather x1 -> x0, waiting for transfers between devices: 394 us -> none  [local_step(): gathered = lax.all_gather(normed, 'tp', axis=0, tiled=True)]
    pallas_call x0 -> x14, Pallas kernels: none -> 355 us  [the longest x11 300 us: project(): pl.pallas_call(body, in_specs=[pl.BlockSpec(memory_space=pltpu.SMEM)] + [...]
    dot_general x3 -> x0, matrix products: 228 us -> none  [the longest x1 77.6 us: local_step(): jnp.einsum('td,dhk->thk', gathered, wk_local, preferred_element_type=jnp....]
    ppermute x0 -> x19, waiting for transfers between devices: none -> 117 us  [the longest x8 107 us: inner(): near.append(lax.ppermute(m, 'tp', across))]
    unnamed x11 -> x10, local copies, waits for them, and re-layouts: 59.5 us -> 0.02 us
    ppermute x0 -> x19, starting transfers between devices: none -> 15.5 us  [the longest x8 11.1 us: inner(): near.append(lax.ppermute(m, 'tp', across))]
    convert_element_type x1 -> x0, other arithmetic: 8.65 us -> none  [local_step(): (hidden_f32 * lax.rsqrt(mean_sq + 1e-06) * norm_gain).astype(jnp.bfloat16)]
    reduce_sum x1 -> x0, other arithmetic: 7.46 us -> none  [local_step(): mean_sq = jnp.mean(hidden_f32 * hidden_f32, axis=-1, keepdims=True)]
  transfers between devices with their start and end apart: 1 -> 19, of which waited for: 1 -> 11; matrix products, arithmetic and copies ran while one was open for 0% -> 0% of each run, Pallas kernels for 0% -> 65%
where the time goes in v2:
time: 490 us; the launch traced here: 489 us
  Pallas kernels  355 us (72%)
  waiting for transfers between devices  117 us (24%)
  starting transfers between devices  15.5 us (3%)
    pallas_call x11, Pallas kernels, project(): pl.pallas_call(body, in_specs=[pl.BlockSpec(memory_space=pltpu.SMEM)] + [...  300 us
    ppermute x8, waiting for transfers between devices, inner(): near.append(lax.ppermute(m, 'tp', across))  107 us
    pallas_call x1, Pallas kernels, join_weights(): pl.pallas_call(body, grid=(dim // step,), in_specs=[pl.BlockSpec((step, H...  26.9 us
    pallas_call x1, Pallas kernels, normalize_all(): pl.pallas_call(body, grid=(block // step,), in_specs=[pl.BlockSpec((step,...  23.6 us
    ppermute x8, starting transfers between devices, inner(): near.append(lax.ppermute(m, 'tp', across))  11.1 us
    ppermute x9, waiting for transfers between devices, arrive(): far[i] = lax.ppermute(a, 'tp', beside)  10.7 us
  transfers between devices with their start and end apart: 19, of which 11 were waited for; matrix products, arithmetic and copies ran while one was open for 0% of the time, Pallas kernels for 65%

profile of v2, /device:TPU:0, one launch (start us, length us, event | category | flops | bytes accessed | tf_op | source)
XLA Modules:
  0.0 488.6 jit_solution(5347229017428421875)
XLA Ops:
  0.6 23.6 %normalize_all.1 = (bf16[2048,4096]{1,0:T(8,128)(2,1)}, bf16[256,4096]{1,0:T(8,128)(2,1)}, bf16[256,4096]{1,0:T(8,128)(2,1)}, bf16[256,4096]{1,0:T(8,128)(2,1)},...) custom-call(bf16[2048,4096]{1,0:T(8,128)(2,1)} %x_ref.3, ...), custom_call_target="tpu_custom_call" | custom-call | flops 67108864 | bytes 50331648 | tf_op jit(solution)/shard_map/normalize_all/pallas_call | solution.py:78
  24.9 4.5 normalize_first.1
  29.4 2.5 collective-permute-start.6
  34.0 26.9 %join_weights.1.refs_1_.refs_2_ = bf16[12,4096,256]{2,1,0:T(8,128)(2,1)} custom-call(bf16[4096,8,128]{2,1,0:T(8,128)(2,1)} %a_ref.1, bf16[4096,8,128]{2,1,0:T(8,128)(2,1)} %b_ref.1, bf16[4096,8,128]{2,1,0:T(8,128)(2,1)} %c_ref.1), custom_call_target="tpu_custom_call" | custom-call | flops 25165824 | bytes 50331648 | tf_op jit(solution)/shard_map/join_weights/pallas_call | solution.py:109
  60.9 68.7 %project.11 = (bf16[8192,8,128]{2,1,0:T(8,128)(2,1)}, bf16[8192,8,128]{2,1,0:T(8,128)(2,1)}, bf16[8192,8,128]{2,1,0:T(8,128)(2,1)}) custom-call(s32[4]{0:T(128)S(1)} %iota_xor_fusion.owners_ref, bf16[2048,4096]{1,0:T(8,128)(2,1)} %get-tuple-element.82.refs_0_, bf16[12,4096,256]{2,1,0:T(8,128)(2,1)} %join_weights.1.refs_1_.refs_2_), custom_call_target="tpu_custom_call" | custom-call | flops 51539607552 | bytes 130023424 | tf_op jit(solution)/shard_map/project/pallas_call | solution.py:207
  129.7 38.9 %collective-permute-done.7.refs_0_ = bf16[256,4096]{1,0:T(8,128)(2,1)} collective-permute-done((bf16[256,4096]{1,0:T(8,128)(2,1)}, bf16[256,4096]{1,0:T(8,128)(2,1)}, u32[]{:S(2)}, u32[]{:S(2)}) %collective-permute-start.7) | collective-permute-done | bytes 2097184 | tf_op jit(solution)/shard_map/ppermute | solution.py:248
  169.1 68.7 %project.12 = (bf16[8192,8,128]{2,1,0:T(8,128)(2,1)}, bf16[8192,8,128]{2,1,0:T(8,128)(2,1)}, bf16[8192,8,128]{2,1,0:T(8,128)(2,1)}) custom-call(s32[4]{0:T(128)S(1)} %iota_xor_fusion.owners_ref, bf16[2048,4096]{1,0:T(8,128)(2,1)} %collective-permute-done.11.refs_0_, ...), custom_call_target="tpu_custom_call", output_to_operand_aliasing={{0}: (3, {}), {1}: (4, {}), {2}: (5, {})} | custom-call | flops 51539607552 | bytes 130023424 | tf_op jit(solution)/shard_map/project/pallas_call | solution.py:207
  237.9 19.8 %project.13 = (bf16[8192,8,128]{2,1,0:T(8,128)(2,1)}, bf16[8192,8,128]{2,1,0:T(8,128)(2,1)}, bf16[8192,8,128]{2,1,0:T(8,128)(2,1)}) custom-call(s32[4]{0:T(128)S(1)} %iota_xor_fusion.owners_ref, bf16[256,4096]{1,0:T(8,128)(2,1)} %collective-permute-done.6.refs_0_, ...), custom_call_target="tpu_custom_call", output_to_operand_aliasing={{0}: (4, {}), {1}: (5, {}), {2}: (6, {})} | custom-call | flops 12884901888 | bytes 32505856 | tf_op jit(solution)/shard_map/project/pallas_call | solution.py:207
  257.8 19.9 %project.14 = (bf16[8192,8,128]{2,1,0:T(8,128)(2,1)}, bf16[8192,8,128]{2,1,0:T(8,128)(2,1)}, bf16[8192,8,128]{2,1,0:T(8,128)(2,1)}) custom-call(s32[4]{0:T(128)S(1)} %iota_xor_fusion.owners_ref, bf16[256,4096]{1,0:T(8,128)(2,1)} %collective-permute-done.7.refs_0_, ...), custom_call_target="tpu_custom_call", output_to_operand_aliasing={{0}: (4, {}), {1}: (5, {}), {2}: (6, {})} | custom-call | flops 12884901888 | bytes 32505856 | tf_op jit(solution)/shard_map/project/pallas_call | solution.py:207
  280.3 19.5 %project.15 = (bf16[8192,8,128]{2,1,0:T(8,128)(2,1)}, bf16[8192,8,128]{2,1,0:T(8,128)(2,1)}, bf16[8192,8,128]{2,1,0:T(8,128)(2,1)}) custom-call(s32[4]{0:T(128)S(1)} %iota_xor_fusion.owners_ref, bf16[256,4096]{1,0:T(8,128)(2,1)S(1)} %collective-permute-done.10.refs_0_, ...), custom_call_target="tpu_custom_call", output_to_operand_aliasing={{0}: (4, {}), {1}: (5, {}), {2}: (6, {})} | custom-call | flops 12884901888 | bytes 32505856 | tf_op jit(solution)/shard_map/project/pallas_call | solution.py:207
  299.7 19.9 %project.16 = (bf16[8192,8,128]{2,1,0:T(8,128)(2,1)}, bf16[8192,8,128]{2,1,0:T(8,128)(2,1)}, bf16[8192,8,128]{2,1,0:T(8,128)(2,1)}) custom-call(s32[4]{0:T(128)S(1)} %iota_xor_fusion.owners_ref, bf16[256,4096]{1,0:T(8,128)(2,1)} %collective-permute-done.5.refs_0_, ...), custom_call_target="tpu_custom_call", output_to_operand_aliasing={{0}: (4, {}), {1}: (5, {}), {2}: (6, {})} | custom-call | flops 12884901888 | bytes 32505856 | tf_op jit(solution)/shard_map/project/pallas_call | solution.py:207
  319.7 6.4 %collective-permute-done.4.refs_0_ = bf16[256,4096]{1,0:T(8,128)(2,1)S(1)} collective-permute-done((bf16[256,4096]{1,0:T(8,128)(2,1)S(1)}, bf16[256,4096]{1,0:T(8,128)(2,1)S(1)}, u32[]{:S(2)}, u32[]{:S(2)}) %collective-permute-start.4) | collective-permute-done | bytes 2097184 | tf_op jit(solution)/shard_map/ppermute | solution.py:248
  327.9 2.4 collective-permute-done.14.refs_1_
  330.3 19.5 %project.17 = (bf16[8192,8,128]{2,1,0:T(8,128)(2,1)}, bf16[8192,8,128]{2,1,0:T(8,128)(2,1)}, bf16[8192,8,128]{2,1,0:T(8,128)(2,1)}) custom-call(s32[4]{0:T(128)S(1)} %iota_xor_fusion.owners_ref, bf16[256,4096]{1,0:T(8,128)(2,1)S(1)} %collective-permute-done.4.refs_0_, ...), custom_call_target="tpu_custom_call", output_to_operand_aliasing={{0}: (4, {}), {1}: (5, {}), {2}: (6, {})} | custom-call | flops 12884901888 | bytes 32505856 | tf_op jit(solution)/shard_map/project/pallas_call | solution.py:207
  349.7 24.4 %collective-permute-done.3.refs_0_ = bf16[256,4096]{1,0:T(8,128)(2,1)S(1)} collective-permute-done((bf16[256,4096]{1,0:T(8,128)(2,1)S(1)}, bf16[256,4096]{1,0:T(8,128)(2,1)S(1)}, u32[]{:S(2)}, u32[]{:S(2)}) %collective-permute-start.3) | collective-permute-done | bytes 2097184 | tf_op jit(solution)/shard_map/ppermute | solution.py:248
  375.9 2.4 collective-permute-done.15.refs_1_
  378.3 19.5 %project.18 = (bf16[8192,8,128]{2,1,0:T(8,128)(2,1)}, bf16[8192,8,128]{2,1,0:T(8,128)(2,1)}, bf16[8192,8,128]{2,1,0:T(8,128)(2,1)}) custom-call(s32[4]{0:T(128)S(1)} %iota_xor_fusion.owners_ref, bf16[256,4096]{1,0:T(8,128)(2,1)S(1)} %collective-permute-done.3.refs_0_, ...), custom_call_target="tpu_custom_call", output_to_operand_aliasing={{0}: (4, {}), {1}: (5, {}), {2}: (6, {})} | custom-call | flops 12884901888 | bytes 32505856 | tf_op jit(solution)/shard_map/project/pallas_call | solution.py:207
  397.8 24.4 %collective-permute-done.2.refs_0_ = bf16[256,4096]{1,0:T(8,128)(2,1)S(1)} collective-permute-done((bf16[256,4096]{1,0:T(8,128)(2,1)S(1)}, bf16[256,4096]{1,0:T(8,128)(2,1)S(1)}, u32[]{:S(2)}, u32[]{:S(2)}) %collective-permute-start.2) | collective-permute-done | bytes 2097184 | tf_op jit(solution)/shard_map/ppermute | solution.py:248
  424.0 2.4 collective-permute-done.16.refs_1_
  426.4 19.5 %project.19 = (bf16[8192,8,128]{2,1,0:T(8,128)(2,1)}, bf16[8192,8,128]{2,1,0:T(8,128)(2,1)}, bf16[8192,8,128]{2,1,0:T(8,128)(2,1)}) custom-call(s32[4]{0:T(128)S(1)} %iota_xor_fusion.owners_ref, bf16[256,4096]{1,0:T(8,128)(2,1)S(1)} %collective-permute-done.2.refs_0_, ...), custom_call_target="tpu_custom_call", output_to_operand_aliasing={{0}: (4, {}), {1}: (5, {}), {2}: (6, {})} | custom-call | flops 12884901888 | bytes 32505856 | tf_op jit(solution)/shard_map/project/pallas_call | solution.py:207
  450.4 12.5 %project.20 = (bf16[8192,8,128]{2,1,0:T(8,128)(2,1)}, bf16[8192,8,128]{2,1,0:T(8,128)(2,1)}, bf16[8192,8,128]{2,1,0:T(8,128)(2,1)}) custom-call(s32[4]{0:T(128)S(1)} %iota_xor_fusion.owners_ref, bf16[128,4096]{1,0:T(8,128)(2,1)S(1)} %collective-permute-done.1.refs_0_, ...), custom_call_target="tpu_custom_call", output_to_operand_aliasing={{0}: (4, {}), {1}: (5, {}), {2}: (6, {})} | custom-call | flops 6442450944 | bytes 28835840 | tf_op jit(solution)/shard_map/project/pallas_call | solution.py:207
  463.0 10.4 %collective-permute-done.refs_0_ = bf16[128,4096]{1,0:T(8,128)(2,1)S(1)} collective-permute-done((bf16[128,4096]{1,0:T(8,128)(2,1)S(1)}, bf16[128,4096]{1,0:T(8,128)(2,1)S(1)}, u32[]{:S(2)}, u32[]{:S(2)}) %collective-permute-start) | collective-permute-done | bytes 1048608 | tf_op jit(solution)/shard_map/ppermute | solution.py:248
  473.4 2.7 collective-permute-done.18.refs_1_
  476.0 12.6 %project.21 = (bf16[8192,8,128]{2,1,0:T(8,128)(2,1)}, bf16[8192,8,128]{2,1,0:T(8,128)(2,1)}, bf16[8192,8,128]{2,1,0:T(8,128)(2,1)}) custom-call(s32[4]{0:T(128)S(1)} %iota_xor_fusion.owners_ref, bf16[128,4096]{1,0:T(8,128)(2,1)S(1)} %collective-permute-done.refs_0_, ...), custom_call_target="tpu_custom_call", output_to_operand_aliasing={{0}: (4, {}), {1}: (5, {}), {2}: (6, {})} | custom-call | flops 6442450944 | bytes 28835840 | tf_op jit(solution)/shard_map/project/pallas_call | solution.py:207
  (39 shorter events, 15.9 us)
Async XLA Ops:
  24.2 144.9 %collective-permute-start.11 = (bf16[2048,4096]{1,0:T(8,128)(2,1)}, bf16[2048,4096]{1,0:T(8,128)(2,1)}, u32[]{:S(2)}, u32[]{:S(2)}) collective-permute-start(bf16[2048,4096]{1,0:T(8,128)(2,1)} %get-tuple-element.82.refs_0_), channel_id=1, source_target_pairs={{0,1},{1,0},{2,3},{3,2},{4,5},{5,4},{6,7},{7,6},{8,9},{9,8},{10,11... | collective-permute-start | bytes 50331656 | tf_op jit(solution)/shard_map/ppermute | solution.py:249
  29.4 100.2 %collective-permute-start.6 = (bf16[256,4096]{1,0:T(8,128)(2,1)}, bf16[256,4096]{1,0:T(8,128)(2,1)}, u32[]{:S(2)}, u32[]{:S(2)}) collective-permute-start(bf16[256,4096]{1,0:T(8,128)(2,1)} %normalize_first.1), channel_id=1, source_target_pairs={{0,2},{1,3},{2,0},{3,1},{4,6},{5,7},{6,4},{7,5},{8,10},{9,11},{10,... | collective-permute-start | bytes 6291464 | tf_op jit(solution)/shard_map/ppermute | solution.py:245
  31.9 245.8 %collective-permute-start.5 = (bf16[256,4096]{1,0:T(8,128)(2,1)}, bf16[256,4096]{1,0:T(8,128)(2,1)}, u32[]{:S(2)}, u32[]{:S(2)}) collective-permute-start(bf16[256,4096]{1,0:T(8,128)(2,1)} %get-tuple-element.80), channel_id=1, source_target_pairs={{0,2},{1,3},{2,0},{3,1},{4,6},{5,7},{6,4},{7,5},{8,10},{9,11},{10,... | collective-permute-start | bytes 6291464 | tf_op jit(solution)/shard_map/ppermute | solution.py:248
  31.9 136.7 %collective-permute-start.7 = (bf16[256,4096]{1,0:T(8,128)(2,1)}, bf16[256,4096]{1,0:T(8,128)(2,1)}, u32[]{:S(2)}, u32[]{:S(2)}) collective-permute-start(bf16[256,4096]{1,0:T(8,128)(2,1)} %get-tuple-element.81), channel_id=1, source_target_pairs={{0,2},{1,3},{2,0},{3,1},{4,6},{5,7},{6,4},{7,5},{8,10},{9,11},{10,... | collective-permute-start | bytes 6291464 | tf_op jit(solution)/shard_map/ppermute | solution.py:248
  34.0 203.9 %collective-permute-start.10 = (bf16[256,4096]{1,0:T(8,128)(2,1)}, bf16[256,4096]{1,0:T(8,128)(2,1)S(1)}, u32[]{:S(2)}, u32[]{:S(2)}) collective-permute-start(bf16[256,4096]{1,0:T(8,128)(2,1)} %get-tuple-element.88), channel_id=1, source_target_pairs={{0,2},{1,3},{2,0},{3,1},{4,6},{5,7},{6,4},{7,5},{8,10},{9,11},{10,... | collective-permute-start | bytes 6291464 | tf_op jit(solution)/shard_map/ppermute | solution.py:248
  168.6 89.2 %collective-permute-start.8 = (bf16[256,4096]{1,0:T(8,128)(2,1)}, bf16[256,4096]{1,0:T(8,128)(2,1)S(1)}, u32[]{:S(2)}, u32[]{:S(2)}) collective-permute-start(bf16[256,4096]{1,0:T(8,128)(2,1)} %collective-permute-done.7.refs_0_), channel_id=1, source_target_pairs={{0,1},{1,0},{2,3},{3,2},{4,5},{5,4},{6,7},{7,6},{8,9},{9,8},{10,11... | collective-permute-start | bytes 6291464 | tf_op jit(solution)/shard_map/ppermute | solution.py:258
  168.6 69.3 %collective-permute-start.9 = (bf16[256,4096]{1,0:T(8,128)(2,1)}, bf16[256,4096]{1,0:T(8,128)(2,1)S(1)}, u32[]{:S(2)}, u32[]{:S(2)}) collective-permute-start(bf16[256,4096]{1,0:T(8,128)(2,1)} %collective-permute-done.6.refs_0_), channel_id=1, source_target_pairs={{0,1},{1,0},{2,3},{3,2},{4,5},{5,4},{6,7},{7,6},{8,9},{9,8},{10,11... | collective-permute-start | bytes 6291464 | tf_op jit(solution)/shard_map/ppermute | solution.py:258
  237.8 42.4 %collective-permute-start.13 = (bf16[256,4096]{1,0:T(8,128)(2,1)S(1)}, bf16[256,4096]{1,0:T(8,128)(2,1)S(1)}, u32[]{:S(2)}, u32[]{:S(2)}) collective-permute-start(bf16[256,4096]{1,0:T(8,128)(2,1)S(1)} %collective-permute-done.10.refs_0_), channel_id=1, source_target_pairs={{0,1},{1,0},{2,3},{3,2},{4,5},{5,4},{6,7},{7,6},{8,9},{9,8},{10,11... | collective-permute-start | bytes 6291464 | tf_op jit(solution)/shard_map/ppermute | solution.py:258
  257.8 20.5 %copy-start.2 = (bf16[256,4096]{1,0:T(8,128)(2,1)S(1)}, bf16[256,4096]{1,0:T(8,128)(2,1)}, u32[]{:S(2)}) copy-start(bf16[256,4096]{1,0:T(8,128)(2,1)} %get-tuple-element.79) | copy-start | bytes 6291460
  277.7 22.0 %collective-permute-start.12 = (bf16[256,4096]{1,0:T(8,128)(2,1)}, bf16[256,4096]{1,0:T(8,128)(2,1)S(1)}, u32[]{:S(2)}, u32[]{:S(2)}) collective-permute-start(bf16[256,4096]{1,0:T(8,128)(2,1)} %collective-permute-done.5.refs_0_), channel_id=1, source_target_pairs={{0,1},{1,0},{2,3},{3,2},{4,5},{5,4},{6,7},{7,6},{8,9},{9,8},{10,11... | collective-permute-start | bytes 6291464 | tf_op jit(solution)/shard_map/ppermute | solution.py:258
  278.2 47.9 %collective-permute-start.4 = (bf16[256,4096]{1,0:T(8,128)(2,1)S(1)}, bf16[256,4096]{1,0:T(8,128)(2,1)S(1)}, u32[]{:S(2)}, u32[]{:S(2)}) collective-permute-start(bf16[256,4096]{1,0:T(8,128)(2,1)S(1)} %copy-done.2), channel_id=1, source_target_pairs={{0,2},{1,3},{2,0},{3,1},{4,6},{5,7},{6,4},{7,5},{8,10},{9,11},{10,... | collective-permute-start | bytes 6291464 | tf_op jit(solution)/shard_map/ppermute | solution.py:248
  299.7 26.4 %copy-start.1 = (bf16[256,4096]{1,0:T(8,128)(2,1)S(1)}, bf16[256,4096]{1,0:T(8,128)(2,1)}, u32[]{:S(2)}) copy-start(bf16[256,4096]{1,0:T(8,128)(2,1)} %get-tuple-element.78) | copy-start | bytes 6291460
  326.1 4.2 collective-permute-start.14
  326.1 48.0 %copy-start = (bf16[256,4096]{1,0:T(8,128)(2,1)S(1)}, bf16[256,4096]{1,0:T(8,128)(2,1)}, u32[]{:S(2)}) copy-start(bf16[256,4096]{1,0:T(8,128)(2,1)} %get-tuple-element.77) | copy-start | bytes 6291460
  326.1 48.0 %collective-permute-start.3 = (bf16[256,4096]{1,0:T(8,128)(2,1)S(1)}, bf16[256,4096]{1,0:T(8,128)(2,1)S(1)}, u32[]{:S(2)}, u32[]{:S(2)}) collective-permute-start(bf16[256,4096]{1,0:T(8,128)(2,1)S(1)} %copy-done.1), channel_id=1, source_target_pairs={{0,2},{1,3},{2,0},{3,1},{4,6},{5,7},{6,4},{7,5},{8,10},{9,11},{10,... | collective-permute-start | bytes 6291464 | tf_op jit(solution)/shard_map/ppermute | solution.py:248
  374.1 4.2 collective-permute-start.15
  374.2 48.0 %copy-start.4 = (bf16[128,4096]{1,0:T(8,128)(2,1)S(1)}, bf16[128,4096]{1,0:T(8,128)(2,1)}, u32[]{:S(2)}) copy-start(bf16[128,4096]{1,0:T(8,128)(2,1)} %get-tuple-element.76) | copy-start | bytes 3145732
  374.2 48.0 %collective-permute-start.2 = (bf16[256,4096]{1,0:T(8,128)(2,1)S(1)}, bf16[256,4096]{1,0:T(8,128)(2,1)S(1)}, u32[]{:S(2)}, u32[]{:S(2)}) collective-permute-start(bf16[256,4096]{1,0:T(8,128)(2,1)S(1)} %copy-done), channel_id=1, source_target_pairs={{0,2},{1,3},{2,0},{3,1},{4,6},{5,7},{6,4},{7,5},{8,10},{9,11},{10,... | collective-permute-start | bytes 6291464 | tf_op jit(solution)/shard_map/ppermute | solution.py:248
  422.2 4.2 collective-permute-start.16
  422.2 25.6 %copy-start.3 = (bf16[128,4096]{1,0:T(8,128)(2,1)S(1)}, bf16[128,4096]{1,0:T(8,128)(2,1)}, u32[]{:S(2)}) copy-start(bf16[128,4096]{1,0:T(8,128)(2,1)} %get-tuple-element.75) | copy-start | bytes 3145732
  422.2 25.6 %collective-permute-start.1 = (bf16[128,4096]{1,0:T(8,128)(2,1)S(1)}, bf16[128,4096]{1,0:T(8,128)(2,1)S(1)}, u32[]{:S(2)}, u32[]{:S(2)}) collective-permute-start(bf16[128,4096]{1,0:T(8,128)(2,1)S(1)} %copy-done.4), channel_id=1, source_target_pairs={{0,2},{1,3},{2,0},{3,1},{4,6},{5,7},{6,4},{7,5},{8,10},{9,11},{10,... | collective-permute-start | bytes 3145736 | tf_op jit(solution)/shard_map/ppermute | solution.py:248
  447.8 2.7 collective-permute-start.17
  447.8 25.6 %collective-permute-start = (bf16[128,4096]{1,0:T(8,128)(2,1)S(1)}, bf16[128,4096]{1,0:T(8,128)(2,1)S(1)}, u32[]{:S(2)}, u32[]{:S(2)}) collective-permute-start(bf16[128,4096]{1,0:T(8,128)(2,1)S(1)} %copy-done.3), channel_id=1, source_target_pairs={{0,2},{1,3},{2,0},{3,1},{4,6},{5,7},{6,4},{7,5},{8,10},{9,11},{10,... | collective-permute-start | bytes 3145736 | tf_op jit(solution)/shard_map/ppermute | solution.py:248
  473.4 2.7 collective-permute-start.18

commit v3 on v2

--- a/solution.py
+++ b/solution.py
@@ -9,9 +9,10 @@
 HEADS = 8
 HEAD_DIM = 128
 COLS = HEADS * HEAD_DIM
-PIECE = 2 * HEAD_DIM
+SIDES = 4
+PIECE = SIDES * HEAD_DIM
 PIECES = COLS // PIECE
-RING = 6
+RING = 4
 MIB = 1024 * 1024
 VMEM = 60 * MIB
 PROJECT_VMEM = 42 * MIB
@@ -22,14 +23,23 @@
 
 
 def normalize_rows(x_ref, g_ref, n_ref):
+    sub, lanes = 32, 128
+    dim = x_ref.shape[1]
+
     def piece(i, carry):
-        at = pl.ds(pl.multiple_of(i * 32, 32), 32)
-        v = x_ref[at, :].astype(jnp.float32)
-        scale = lax.rsqrt(jnp.mean(v * v, axis=-1, keepdims=True) + 1e-6)
-        n_ref[at, :] = (v * scale * g_ref[...]).astype(jnp.bfloat16)
+        at = pl.ds(pl.multiple_of(i * sub, sub), sub)
+        squares = [jnp.zeros((sub, lanes), jnp.float32) for _ in range(2)]
+        for k in range(dim // lanes):
+            v = x_ref[at, k * lanes : (k + 1) * lanes].astype(jnp.float32)
+            squares[k % 2] += v * v
+        mean = jnp.sum(squares[0] + squares[1], axis=-1, keepdims=True) / dim
+        scale = jnp.broadcast_to(lax.rsqrt(mean + 1e-6), (sub, lanes))
+        for k in range(dim // lanes):
+            cols = slice(k * lanes, (k + 1) * lanes)
+            n_ref[at, cols] = (x_ref[at, cols].astype(jnp.float32) * scale * g_ref[:, cols]).astype(jnp.bfloat16)
         return carry
 
-    lax.fori_loop(0, x_ref.shape[0] // 32, piece, 0)
+    lax.fori_loop(0, x_ref.shape[0] // sub, piece, 0)
 
 
 def normalize_first(x, norm_gain, rows):
@@ -90,7 +100,7 @@
 
 def join_weights(*weights):
     dim = weights[0].shape[0]
-    step, sub = 256, 64
+    step, sub = 512, 64
 
     def body(a_ref, b_ref, c_ref, w_ref, flat):
         def some(i, carry):
@@ -100,8 +110,8 @@
             for index in range(3):
                 for head in range(HEADS):
                     part = flat[index, pl.ds(head, sub, stride=HEADS), :]
-                    lanes = slice(head % 2 * HEAD_DIM, (head % 2 + 1) * HEAD_DIM)
-                    w_ref[index * PIECES + head // 2, at, lanes] = part.astype(jnp.bfloat16)
+                    lanes = slice(head % SIDES * HEAD_DIM, (head % SIDES + 1) * HEAD_DIM)
+                    w_ref[index * PIECES + head // SIDES, at, lanes] = part.astype(jnp.bfloat16)
             return carry
 
         lax.fori_loop(0, step // sub, some, 0)
@@ -188,8 +198,8 @@
                 pl.when(p + RING - 1 < steps * PIECES)(lambda: piece(p + RING - 1, begin))
                 emit(1 - slot, i * quarter, quarter)
                 got = jnp.dot(n_buf[lax.rem(b, slots)], w_buf[lax.rem(p, RING)], preferred_element_type=jnp.float32)
-                for side in range(2):
-                    total[slot, pl.ds(2 * i + side, rows, stride=HEADS), :] = got[:, side * HEAD_DIM : (side + 1) * HEAD_DIM]
+                for side in range(SIDES):
+                    total[slot, pl.ds(SIDES * i + side, rows, stride=HEADS), :] = got[:, side * HEAD_DIM : (side + 1) * HEAD_DIM]
                 return carry
 
             lax.fori_loop(0, PIECES, part, 0)

time: 490 us -> 486 us (level)
  Pallas kernels: 355 us -> 345 us
  waiting for transfers between devices: 117 us -> 124 us
    pallas_call x11, Pallas kernels: 300 us -> 293 us  [project(): pl.pallas_call(body, in_specs=[pl.BlockSpec(memory_space=pltpu.SMEM)] + [...]
    ppermute x8, waiting for transfers between devices: 107 us -> 113 us  [inner(): near.append(lax.ppermute(m, 'tp', across))]
  transfers between devices with their start and end apart: 19 -> 19, of which waited for: 11 -> 11; matrix products, arithmetic and copies ran while one was open for 0% -> 0% of each run, Pallas kernels for 65% -> 64%
where the time goes in v3:
time: 486 us; the launch traced here: 485 us
  Pallas kernels  345 us (71%)
  waiting for transfers between devices  124 us (26%)
  starting transfers between devices  15.5 us (3%)
    pallas_call x11, Pallas kernels, project(): pl.pallas_call(body, in_specs=[pl.BlockSpec(memory_space=pltpu.SMEM)] + [...  293 us
    ppermute x8, waiting for transfers between devices, inner(): near.append(lax.ppermute(m, 'tp', across))  113 us
    pallas_call x1, Pallas kernels, join_weights(): pl.pallas_call(body, grid=(dim // step,), in_specs=[pl.BlockSpec((step, H...  24 us
    pallas_call x1, Pallas kernels, normalize_all(): pl.pallas_call(body, grid=(block // step,), in_specs=[pl.BlockSpec((step,...  23.5 us
    ppermute x8, starting transfers between devices, inner(): near.append(lax.ppermute(m, 'tp', across))  11.1 us
    ppermute x9, waiting for transfers between devices, arrive(): far[i] = lax.ppermute(a, 'tp', beside)  10.7 us
  transfers between devices with their start and end apart: 19, of which 11 were waited for; matrix products, arithmetic and copies ran while one was open for 0% of the time, Pallas kernels for 64%

profile of v3, /device:TPU:0, one launch (start us, length us, event | category | flops | bytes accessed | tf_op | source)
XLA Modules:
  0.0 485.2 jit_solution(14231317173185395603)
XLA Ops:
  0.6 23.5 %normalize_all.1 = (bf16[2048,4096]{1,0:T(8,128)(2,1)}, bf16[256,4096]{1,0:T(8,128)(2,1)}, bf16[256,4096]{1,0:T(8,128)(2,1)}, bf16[256,4096]{1,0:T(8,128)(2,1)},...) custom-call(bf16[2048,4096]{1,0:T(8,128)(2,1)} %x_ref.3, ...), custom_call_target="tpu_custom_call" | custom-call | flops 67108864 | bytes 50331648 | tf_op jit(solution)/shard_map/normalize_all/pallas_call | solution.py:88
  24.9 4.5 normalize_first.1
  29.4 2.5 collective-permute-start.6
  33.9 24.0 %join_weights.1.refs_1_.refs_2_ = bf16[6,4096,512]{2,1,0:T(8,128)(2,1)} custom-call(bf16[4096,8,128]{2,1,0:T(8,128)(2,1)} %a_ref.1, bf16[4096,8,128]{2,1,0:T(8,128)(2,1)} %b_ref.1, bf16[4096,8,128]{2,1,0:T(8,128)(2,1)} %c_ref.1), custom_call_target="tpu_custom_call" | custom-call | flops 25165824 | bytes 50331648 | tf_op jit(solution)/shard_map/join_weights/pallas_call | solution.py:119
  58.0 65.7 %project.11 = (bf16[8192,8,128]{2,1,0:T(8,128)(2,1)}, bf16[8192,8,128]{2,1,0:T(8,128)(2,1)}, bf16[8192,8,128]{2,1,0:T(8,128)(2,1)}) custom-call(s32[4]{0:T(128)S(1)} %iota_xor_fusion.owners_ref, bf16[2048,4096]{1,0:T(8,128)(2,1)} %get-tuple-element.82.refs_0_, bf16[6,4096,512]{2,1,0:T(8,128)(2,1)} %join_weights.1.refs_1_.refs_2_), custom_call_target="tpu_custom_call" | custom-call | flops 51539607552 | bytes 130023424 | tf_op jit(solution)/shard_map/project/pallas_call | solution.py:217
  123.7 44.9 %collective-permute-done.7.refs_0_ = bf16[256,4096]{1,0:T(8,128)(2,1)} collective-permute-done((bf16[256,4096]{1,0:T(8,128)(2,1)}, bf16[256,4096]{1,0:T(8,128)(2,1)}, u32[]{:S(2)}, u32[]{:S(2)}) %collective-permute-start.7) | collective-permute-done | bytes 2097184 | tf_op jit(solution)/shard_map/ppermute | solution.py:258
  169.1 65.7 %project.12 = (bf16[8192,8,128]{2,1,0:T(8,128)(2,1)}, bf16[8192,8,128]{2,1,0:T(8,128)(2,1)}, bf16[8192,8,128]{2,1,0:T(8,128)(2,1)}) custom-call(s32[4]{0:T(128)S(1)} %iota_xor_fusion.owners_ref, bf16[2048,4096]{1,0:T(8,128)(2,1)} %collective-permute-done.11.refs_0_, ...), custom_call_target="tpu_custom_call", output_to_operand_aliasing={{0}: (3, {}), {1}: (4, {}), {2}: (5, {})} | custom-call | flops 51539607552 | bytes 130023424 | tf_op jit(solution)/shard_map/project/pallas_call | solution.py:217
  234.9 19.8 %project.13 = (bf16[8192,8,128]{2,1,0:T(8,128)(2,1)}, bf16[8192,8,128]{2,1,0:T(8,128)(2,1)}, bf16[8192,8,128]{2,1,0:T(8,128)(2,1)}) custom-call(s32[4]{0:T(128)S(1)} %iota_xor_fusion.owners_ref, bf16[256,4096]{1,0:T(8,128)(2,1)} %collective-permute-done.6.refs_0_, ...), custom_call_target="tpu_custom_call", output_to_operand_aliasing={{0}: (4, {}), {1}: (5, {}), {2}: (6, {})} | custom-call | flops 12884901888 | bytes 32505856 | tf_op jit(solution)/shard_map/project/pallas_call | solution.py:217
  254.7 19.8 %project.14 = (bf16[8192,8,128]{2,1,0:T(8,128)(2,1)}, bf16[8192,8,128]{2,1,0:T(8,128)(2,1)}, bf16[8192,8,128]{2,1,0:T(8,128)(2,1)}) custom-call(s32[4]{0:T(128)S(1)} %iota_xor_fusion.owners_ref, bf16[256,4096]{1,0:T(8,128)(2,1)} %collective-permute-done.7.refs_0_, ...), custom_call_target="tpu_custom_call", output_to_operand_aliasing={{0}: (4, {}), {1}: (5, {}), {2}: (6, {})} | custom-call | flops 12884901888 | bytes 32505856 | tf_op jit(solution)/shard_map/project/pallas_call | solution.py:217
  277.1 19.4 %project.15 = (bf16[8192,8,128]{2,1,0:T(8,128)(2,1)}, bf16[8192,8,128]{2,1,0:T(8,128)(2,1)}, bf16[8192,8,128]{2,1,0:T(8,128)(2,1)}) custom-call(s32[4]{0:T(128)S(1)} %iota_xor_fusion.owners_ref, bf16[256,4096]{1,0:T(8,128)(2,1)S(1)} %collective-permute-done.10.refs_0_, ...), custom_call_target="tpu_custom_call", output_to_operand_aliasing={{0}: (4, {}), {1}: (5, {}), {2}: (6, {})} | custom-call | flops 12884901888 | bytes 32505856 | tf_op jit(solution)/shard_map/project/pallas_call | solution.py:217
  296.5 19.8 %project.16 = (bf16[8192,8,128]{2,1,0:T(8,128)(2,1)}, bf16[8192,8,128]{2,1,0:T(8,128)(2,1)}, bf16[8192,8,128]{2,1,0:T(8,128)(2,1)}) custom-call(s32[4]{0:T(128)S(1)} %iota_xor_fusion.owners_ref, bf16[256,4096]{1,0:T(8,128)(2,1)} %collective-permute-done.5.refs_0_, ...), custom_call_target="tpu_custom_call", output_to_operand_aliasing={{0}: (4, {}), {1}: (5, {}), {2}: (6, {})} | custom-call | flops 12884901888 | bytes 32505856 | tf_op jit(solution)/shard_map/project/pallas_call | solution.py:217
  316.3 6.6 %collective-permute-done.4.refs_0_ = bf16[256,4096]{1,0:T(8,128)(2,1)S(1)} collective-permute-done((bf16[256,4096]{1,0:T(8,128)(2,1)S(1)}, bf16[256,4096]{1,0:T(8,128)(2,1)S(1)}, u32[]{:S(2)}, u32[]{:S(2)}) %collective-permute-start.4) | collective-permute-done | bytes 2097184 | tf_op jit(solution)/shard_map/ppermute | solution.py:258
  324.7 2.4 collective-permute-done.14.refs_1_
  327.1 19.4 %project.17 = (bf16[8192,8,128]{2,1,0:T(8,128)(2,1)}, bf16[8192,8,128]{2,1,0:T(8,128)(2,1)}, bf16[8192,8,128]{2,1,0:T(8,128)(2,1)}) custom-call(s32[4]{0:T(128)S(1)} %iota_xor_fusion.owners_ref, bf16[256,4096]{1,0:T(8,128)(2,1)S(1)} %collective-permute-done.4.refs_0_, ...), custom_call_target="tpu_custom_call", output_to_operand_aliasing={{0}: (4, {}), {1}: (5, {}), {2}: (6, {})} | custom-call | flops 12884901888 | bytes 32505856 | tf_op jit(solution)/shard_map/project/pallas_call | solution.py:217
  346.5 24.5 %collective-permute-done.3.refs_0_ = bf16[256,4096]{1,0:T(8,128)(2,1)S(1)} collective-permute-done((bf16[256,4096]{1,0:T(8,128)(2,1)S(1)}, bf16[256,4096]{1,0:T(8,128)(2,1)S(1)}, u32[]{:S(2)}, u32[]{:S(2)}) %collective-permute-start.3) | collective-permute-done | bytes 2097184 | tf_op jit(solution)/shard_map/ppermute | solution.py:258
  372.7 2.4 collective-permute-done.15.refs_1_
  375.1 19.4 %project.18 = (bf16[8192,8,128]{2,1,0:T(8,128)(2,1)}, bf16[8192,8,128]{2,1,0:T(8,128)(2,1)}, bf16[8192,8,128]{2,1,0:T(8,128)(2,1)}) custom-call(s32[4]{0:T(128)S(1)} %iota_xor_fusion.owners_ref, bf16[256,4096]{1,0:T(8,128)(2,1)S(1)} %collective-permute-done.3.refs_0_, ...), custom_call_target="tpu_custom_call", output_to_operand_aliasing={{0}: (4, {}), {1}: (5, {}), {2}: (6, {})} | custom-call | flops 12884901888 | bytes 32505856 | tf_op jit(solution)/shard_map/project/pallas_call | solution.py:217
  394.5 24.5 %collective-permute-done.2.refs_0_ = bf16[256,4096]{1,0:T(8,128)(2,1)S(1)} collective-permute-done((bf16[256,4096]{1,0:T(8,128)(2,1)S(1)}, bf16[256,4096]{1,0:T(8,128)(2,1)S(1)}, u32[]{:S(2)}, u32[]{:S(2)}) %collective-permute-start.2) | collective-permute-done | bytes 2097184 | tf_op jit(solution)/shard_map/ppermute | solution.py:258
  420.8 2.4 collective-permute-done.16.refs_1_
  423.2 19.4 %project.19 = (bf16[8192,8,128]{2,1,0:T(8,128)(2,1)}, bf16[8192,8,128]{2,1,0:T(8,128)(2,1)}, bf16[8192,8,128]{2,1,0:T(8,128)(2,1)}) custom-call(s32[4]{0:T(128)S(1)} %iota_xor_fusion.owners_ref, bf16[256,4096]{1,0:T(8,128)(2,1)S(1)} %collective-permute-done.2.refs_0_, ...), custom_call_target="tpu_custom_call", output_to_operand_aliasing={{0}: (4, {}), {1}: (5, {}), {2}: (6, {})} | custom-call | flops 12884901888 | bytes 32505856 | tf_op jit(solution)/shard_map/project/pallas_call | solution.py:217
  447.2 12.2 %project.20 = (bf16[8192,8,128]{2,1,0:T(8,128)(2,1)}, bf16[8192,8,128]{2,1,0:T(8,128)(2,1)}, bf16[8192,8,128]{2,1,0:T(8,128)(2,1)}) custom-call(s32[4]{0:T(128)S(1)} %iota_xor_fusion.owners_ref, bf16[128,4096]{1,0:T(8,128)(2,1)S(1)} %collective-permute-done.1.refs_0_, ...), custom_call_target="tpu_custom_call", output_to_operand_aliasing={{0}: (4, {}), {1}: (5, {}), {2}: (6, {})} | custom-call | flops 6442450944 | bytes 28835840 | tf_op jit(solution)/shard_map/project/pallas_call | solution.py:217
  459.5 10.7 %collective-permute-done.refs_0_ = bf16[128,4096]{1,0:T(8,128)(2,1)S(1)} collective-permute-done((bf16[128,4096]{1,0:T(8,128)(2,1)S(1)}, bf16[128,4096]{1,0:T(8,128)(2,1)S(1)}, u32[]{:S(2)}, u32[]{:S(2)}) %collective-permute-start) | collective-permute-done | bytes 1048608 | tf_op jit(solution)/shard_map/ppermute | solution.py:258
  470.2 2.7 collective-permute-done.18.refs_1_
  472.8 12.2 %project.21 = (bf16[8192,8,128]{2,1,0:T(8,128)(2,1)}, bf16[8192,8,128]{2,1,0:T(8,128)(2,1)}, bf16[8192,8,128]{2,1,0:T(8,128)(2,1)}) custom-call(s32[4]{0:T(128)S(1)} %iota_xor_fusion.owners_ref, bf16[128,4096]{1,0:T(8,128)(2,1)S(1)} %collective-permute-done.refs_0_, ...), custom_call_target="tpu_custom_call", output_to_operand_aliasing={{0}: (4, {}), {1}: (5, {}), {2}: (6, {})} | custom-call | flops 6442450944 | bytes 28835840 | tf_op jit(solution)/shard_map/project/pallas_call | solution.py:217
  (39 shorter events, 16.0 us)
Async XLA Ops:
  24.1 144.9 %collective-permute-start.11 = (bf16[2048,4096]{1,0:T(8,128)(2,1)}, bf16[2048,4096]{1,0:T(8,128)(2,1)}, u32[]{:S(2)}, u32[]{:S(2)}) collective-permute-start(bf16[2048,4096]{1,0:T(8,128)(2,1)} %get-tuple-element.82.refs_0_), channel_id=1, source_target_pairs={{0,1},{1,0},{2,3},{3,2},{4,5},{5,4},{6,7},{7,6},{8,9},{9,8},{10,11... | collective-permute-start | bytes 50331656 | tf_op jit(solution)/shard_map/ppermute | solution.py:259
  29.4 94.3 %collective-permute-start.6 = (bf16[256,4096]{1,0:T(8,128)(2,1)}, bf16[256,4096]{1,0:T(8,128)(2,1)}, u32[]{:S(2)}, u32[]{:S(2)}) collective-permute-start(bf16[256,4096]{1,0:T(8,128)(2,1)} %normalize_first.1), channel_id=1, source_target_pairs={{0,2},{1,3},{2,0},{3,1},{4,6},{5,7},{6,4},{7,5},{8,10},{9,11},{10,... | collective-permute-start | bytes 6291464 | tf_op jit(solution)/shard_map/ppermute | solution.py:255
  31.9 242.6 %collective-permute-start.5 = (bf16[256,4096]{1,0:T(8,128)(2,1)}, bf16[256,4096]{1,0:T(8,128)(2,1)}, u32[]{:S(2)}, u32[]{:S(2)}) collective-permute-start(bf16[256,4096]{1,0:T(8,128)(2,1)} %get-tuple-element.80), channel_id=1, source_target_pairs={{0,2},{1,3},{2,0},{3,1},{4,6},{5,7},{6,4},{7,5},{8,10},{9,11},{10,... | collective-permute-start | bytes 6291464 | tf_op jit(solution)/shard_map/ppermute | solution.py:258
  31.9 136.7 %collective-permute-start.7 = (bf16[256,4096]{1,0:T(8,128)(2,1)}, bf16[256,4096]{1,0:T(8,128)(2,1)}, u32[]{:S(2)}, u32[]{:S(2)}) collective-permute-start(bf16[256,4096]{1,0:T(8,128)(2,1)} %get-tuple-element.81), channel_id=1, source_target_pairs={{0,2},{1,3},{2,0},{3,1},{4,6},{5,7},{6,4},{7,5},{8,10},{9,11},{10,... | collective-permute-start | bytes 6291464 | tf_op jit(solution)/shard_map/ppermute | solution.py:258
  33.9 200.9 %collective-permute-start.10 = (bf16[256,4096]{1,0:T(8,128)(2,1)}, bf16[256,4096]{1,0:T(8,128)(2,1)S(1)}, u32[]{:S(2)}, u32[]{:S(2)}) collective-permute-start(bf16[256,4096]{1,0:T(8,128)(2,1)} %get-tuple-element.88), channel_id=1, source_target_pairs={{0,2},{1,3},{2,0},{3,1},{4,6},{5,7},{6,4},{7,5},{8,10},{9,11},{10,... | collective-permute-start | bytes 6291464 | tf_op jit(solution)/shard_map/ppermute | solution.py:258
  168.5 86.1 %collective-permute-start.8 = (bf16[256,4096]{1,0:T(8,128)(2,1)}, bf16[256,4096]{1,0:T(8,128)(2,1)S(1)}, u32[]{:S(2)}, u32[]{:S(2)}) collective-permute-start(bf16[256,4096]{1,0:T(8,128)(2,1)} %collective-permute-done.7.refs_0_), channel_id=1, source_target_pairs={{0,1},{1,0},{2,3},{3,2},{4,5},{5,4},{6,7},{7,6},{8,9},{9,8},{10,11... | collective-permute-start | bytes 6291464 | tf_op jit(solution)/shard_map/ppermute | solution.py:268
  168.6 66.3 %collective-permute-start.9 = (bf16[256,4096]{1,0:T(8,128)(2,1)}, bf16[256,4096]{1,0:T(8,128)(2,1)S(1)}, u32[]{:S(2)}, u32[]{:S(2)}) collective-permute-start(bf16[256,4096]{1,0:T(8,128)(2,1)} %collective-permute-done.6.refs_0_), channel_id=1, source_target_pairs={{0,1},{1,0},{2,3},{3,2},{4,5},{5,4},{6,7},{7,6},{8,9},{9,8},{10,11... | collective-permute-start | bytes 6291464 | tf_op jit(solution)/shard_map/ppermute | solution.py:268
  234.8 42.3 %collective-permute-start.13 = (bf16[256,4096]{1,0:T(8,128)(2,1)S(1)}, bf16[256,4096]{1,0:T(8,128)(2,1)S(1)}, u32[]{:S(2)}, u32[]{:S(2)}) collective-permute-start(bf16[256,4096]{1,0:T(8,128)(2,1)S(1)} %collective-permute-done.10.refs_0_), channel_id=1, source_target_pairs={{0,1},{1,0},{2,3},{3,2},{4,5},{5,4},{6,7},{7,6},{8,9},{9,8},{10,11... | collective-permute-start | bytes 6291464 | tf_op jit(solution)/shard_map/ppermute | solution.py:268
  254.6 20.4 %copy-start.2 = (bf16[256,4096]{1,0:T(8,128)(2,1)S(1)}, bf16[256,4096]{1,0:T(8,128)(2,1)}, u32[]{:S(2)}) copy-start(bf16[256,4096]{1,0:T(8,128)(2,1)} %get-tuple-element.79) | copy-start | bytes 6291460
  274.5 21.9 %collective-permute-start.12 = (bf16[256,4096]{1,0:T(8,128)(2,1)}, bf16[256,4096]{1,0:T(8,128)(2,1)S(1)}, u32[]{:S(2)}, u32[]{:S(2)}) collective-permute-start(bf16[256,4096]{1,0:T(8,128)(2,1)} %collective-permute-done.5.refs_0_), channel_id=1, source_target_pairs={{0,1},{1,0},{2,3},{3,2},{4,5},{5,4},{6,7},{7,6},{8,9},{9,8},{10,11... | collective-permute-start | bytes 6291464 | tf_op jit(solution)/shard_map/ppermute | solution.py:268
  275.0 47.9 %collective-permute-start.4 = (bf16[256,4096]{1,0:T(8,128)(2,1)S(1)}, bf16[256,4096]{1,0:T(8,128)(2,1)S(1)}, u32[]{:S(2)}, u32[]{:S(2)}) collective-permute-start(bf16[256,4096]{1,0:T(8,128)(2,1)S(1)} %copy-done.2), channel_id=1, source_target_pairs={{0,2},{1,3},{2,0},{3,1},{4,6},{5,7},{6,4},{7,5},{8,10},{9,11},{10,... | collective-permute-start | bytes 6291464 | tf_op jit(solution)/shard_map/ppermute | solution.py:258
  296.5 26.4 %copy-start.1 = (bf16[256,4096]{1,0:T(8,128)(2,1)S(1)}, bf16[256,4096]{1,0:T(8,128)(2,1)}, u32[]{:S(2)}) copy-start(bf16[256,4096]{1,0:T(8,128)(2,1)} %get-tuple-element.78) | copy-start | bytes 6291460
  322.9 4.2 collective-permute-start.14
  322.9 48.0 %copy-start = (bf16[256,4096]{1,0:T(8,128)(2,1)S(1)}, bf16[256,4096]{1,0:T(8,128)(2,1)}, u32[]{:S(2)}) copy-start(bf16[256,4096]{1,0:T(8,128)(2,1)} %get-tuple-element.77) | copy-start | bytes 6291460
  322.9 48.0 %collective-permute-start.3 = (bf16[256,4096]{1,0:T(8,128)(2,1)S(1)}, bf16[256,4096]{1,0:T(8,128)(2,1)S(1)}, u32[]{:S(2)}, u32[]{:S(2)}) collective-permute-start(bf16[256,4096]{1,0:T(8,128)(2,1)S(1)} %copy-done.1), channel_id=1, source_target_pairs={{0,2},{1,3},{2,0},{3,1},{4,6},{5,7},{6,4},{7,5},{8,10},{9,11},{10,... | collective-permute-start | bytes 6291464 | tf_op jit(solution)/shard_map/ppermute | solution.py:258
  371.0 4.2 collective-permute-start.15
  371.0 48.0 %copy-start.4 = (bf16[128,4096]{1,0:T(8,128)(2,1)S(1)}, bf16[128,4096]{1,0:T(8,128)(2,1)}, u32[]{:S(2)}) copy-start(bf16[128,4096]{1,0:T(8,128)(2,1)} %get-tuple-element.76) | copy-start | bytes 3145732
  371.0 48.0 %collective-permute-start.2 = (bf16[256,4096]{1,0:T(8,128)(2,1)S(1)}, bf16[256,4096]{1,0:T(8,128)(2,1)S(1)}, u32[]{:S(2)}, u32[]{:S(2)}) collective-permute-start(bf16[256,4096]{1,0:T(8,128)(2,1)S(1)} %copy-done), channel_id=1, source_target_pairs={{0,2},{1,3},{2,0},{3,1},{4,6},{5,7},{6,4},{7,5},{8,10},{9,11},{10,... | collective-permute-start | bytes 6291464 | tf_op jit(solution)/shard_map/ppermute | solution.py:258
  419.0 4.2 collective-permute-start.16
  419.0 25.6 %copy-start.3 = (bf16[128,4096]{1,0:T(8,128)(2,1)S(1)}, bf16[128,4096]{1,0:T(8,128)(2,1)}, u32[]{:S(2)}) copy-start(bf16[128,4096]{1,0:T(8,128)(2,1)} %get-tuple-element.75) | copy-start | bytes 3145732
  419.0 25.6 %collective-permute-start.1 = (bf16[128,4096]{1,0:T(8,128)(2,1)S(1)}, bf16[128,4096]{1,0:T(8,128)(2,1)S(1)}, u32[]{:S(2)}, u32[]{:S(2)}) collective-permute-start(bf16[128,4096]{1,0:T(8,128)(2,1)S(1)} %copy-done.4), channel_id=1, source_target_pairs={{0,2},{1,3},{2,0},{3,1},{4,6},{5,7},{6,4},{7,5},{8,10},{9,11},{10,... | collective-permute-start | bytes 3145736 | tf_op jit(solution)/shard_map/ppermute | solution.py:258
  444.6 2.7 collective-permute-start.17
  444.6 25.6 %collective-permute-start = (bf16[128,4096]{1,0:T(8,128)(2,1)S(1)}, bf16[128,4096]{1,0:T(8,128)(2,1)S(1)}, u32[]{:S(2)}, u32[]{:S(2)}) collective-permute-start(bf16[128,4096]{1,0:T(8,128)(2,1)S(1)} %copy-done.3), channel_id=1, source_target_pairs={{0,2},{1,3},{2,0},{3,1},{4,6},{5,7},{6,4},{7,5},{8,10},{9,11},{10,... | collective-permute-start | bytes 3145736 | tf_op jit(solution)/shard_map/ppermute | solution.py:258
  470.2 2.7 collective-permute-start.18

commit v4 on v3

v4 whole, which is shorter than its diff:
```python
import jax
import jax.numpy as jnp
from jax import lax
from jax.experimental import pallas as pl
from jax.experimental.pallas import tpu as pltpu
from jax.sharding import PartitionSpec as P


HEADS = 8
HEAD_DIM = 128
COLS = HEADS * HEAD_DIM
SIDES = 4
PIECE = SIDES * HEAD_DIM
PIECES = COLS // PIECE
MIB = 1024 * 1024
VMEM = 60 * MIB
PROJECT_VMEM = 24 * MIB
JOIN_VMEM = 24 * MIB

CHUNKS = (64, 192, 256, 256, 256, 256, 256, 256, 128, 96, 32)
EARLY = 2
BIG = 512
NORM_ROWS = 128


def normalize_rows(x_ref, g_ref, n_ref):
    sub, lanes = 32, 128
    dim = x_ref.shape[1]

    def piece(i, carry):
        at = pl.ds(pl.multiple_of(i * sub, sub), sub)
        squares = [jnp.zeros((sub, lanes), jnp.float32) for _ in range(2)]
        for k in range(dim // lanes):
            v = x_ref[at, k * lanes : (k + 1) * lanes].astype(jnp.float32)
            squares[k % 2] += v * v
        mean = jnp.sum(squares[0] + squares[1], axis=-1, keepdims=True) / dim
        scale = jnp.broadcast_to(lax.rsqrt(mean + 1e-6), (sub, lanes))
        for k in range(dim // lanes):
            cols = slice(k * lanes, (k + 1) * lanes)
            n_ref[at, cols] = (x_ref[at, cols].astype(jnp.float32) * scale * g_ref[:, cols]).astype(jnp.bfloat16)
        return carry

    lax.fori_loop(0, x_ref.shape[0] // sub, piece, 0)


def normalize_some(x, norm_gain, start, rows):
    dim = x.shape[1]
    step = 64
    return pl.pallas_call(
        normalize_rows,
        grid=(rows // step,),
        in_specs=[pl.BlockSpec((step, dim), lambda i: (start // step + i, 0)), pl.BlockSpec((1, dim), lambda i: (0, 0))],
        out_specs=pl.BlockSpec((step, dim), lambda i: (i, 0)),
        out_shape=jax.ShapeDtypeStruct((rows, dim), jnp.bfloat16),
        compiler_params=pltpu.CompilerParams(vmem_limit_bytes=VMEM),
        cost_estimate=pl.CostEstimate(flops=8 * rows * dim, bytes_accessed=4 * rows * dim, transcendentals=rows),
        name="normalize_some",
    )(x, norm_gain)


def normalize_all(x, norm_gain, chunks, early):
    block, dim = x.shape
    step = NORM_ROWS
    starts = [sum(chunks[:i]) for i in range(len(chunks))]

    def body(x_ref, g_ref, *refs):
        outs, (held, sem) = refs[:-2], refs[-2:]
        b = pl.program_id(0)
        slot = lax.rem(b, 2)

        def copies(b, slot, do):
            do(pltpu.make_async_copy(held.at[slot], outs[0].at[pl.ds(b * step, step)], sem.at[slot, 0]))
            for k in range(block // step):

                @pl.when(b == k)
                def _(k=k):
                    count = 1
                    for i in range(early, len(chunks)):
                        low, high = max(k * step, starts[i]), min((k + 1) * step, starts[i] + chunks[i])
                        if low < high:
                            src = held.at[slot, pl.ds(low - k * step, high - low)]
                            dst = outs[1 + i - early].at[pl.ds(low - starts[i], high - low)]
                            do(pltpu.make_async_copy(src, dst, sem.at[slot, count]))
                            count += 1

        pl.when(b >= 2)(lambda: copies(b - 2, slot, lambda c: c.wait()))
        normalize_rows(x_ref, g_ref, held.at[slot])
        copies(b, slot, lambda c: c.start())

        @pl.when(b == block // step - 1)
        def _():
            copies(b - 1, 1 - slot, lambda c: c.wait())
            copies(b, slot, lambda c: c.wait())

    return pl.pallas_call(
        body,
        grid=(block // step,),
        in_specs=[pl.BlockSpec((step, dim), lambda i: (i, 0)), pl.BlockSpec((1, dim), lambda i: (0, 0))],
        out_specs=[pl.BlockSpec(memory_space=pl.ANY)] * (1 + len(chunks) - early),
        out_shape=[jax.ShapeDtypeStruct((rows, dim), jnp.bfloat16) for rows in (block,) + chunks[early:]],
        scratch_shapes=[pltpu.VMEM((2, step, dim), jnp.bfloat16), pltpu.SemaphoreType.DMA((2, 4))],
        compiler_params=pltpu.CompilerParams(vmem_limit_bytes=VMEM),
        cost_estimate=pl.CostEstimate(flops=8 * block * dim, bytes_accessed=6 * block * dim, transcendentals=block),
        name="normalize_all",
    )(x, norm_gain)


def join_weights(*weights):
    dim = weights[0].shape[0]
    step, sub = 512, 64
    steps = dim // step

    def body(a_ref, b_ref, c_ref, w_ref, held, flat, sem):
        def fetch(i, do):
            slot = lax.rem(i, 2)
            for index, ref in enumerate((a_ref, b_ref, c_ref)):
                src = ref.at[pl.ds(pl.multiple_of(i * step, step), step)]
                do(pltpu.make_async_copy(src, held.at[slot, index], sem.at[slot, index]))

        def block(i, carry):
            pl.when(i + 1 < steps)(lambda: fetch(i + 1, lambda copy: copy.start()))
            fetch(i, lambda copy: copy.wait())
            slot = lax.rem(i, 2)

            def some(k, carry):
                at = pl.ds(pl.multiple_of(k * sub, sub), sub)
                to = pl.ds(pl.multiple_of(i * step + k * sub, sub), sub)
                for index in range(3):
                    flat[index] = held[slot, index, at].astype(jnp.float32).reshape(sub * HEADS, HEAD_DIM)
                for index in range(3):
                    for head in range(HEADS):
                        part = flat[index, pl.ds(head, sub, stride=HEADS), :]
                        lanes = slice(head % SIDES * HEAD_DIM, (head % SIDES + 1) * HEAD_DIM)
                        w_ref[index * PIECES + head // SIDES, to, lanes] = part.astype(jnp.bfloat16)
                return carry

            return lax.fori_loop(0, step // sub, some, carry)

        fetch(0, lambda copy: copy.start())
        lax.fori_loop(0, steps, block, 0)

    return pl.pallas_call(
        body,
        in_specs=[pl.BlockSpec(memory_space=pl.ANY)] * 3,
        out_specs=pl.BlockSpec(memory_space=pltpu.VMEM),
        out_shape=pltpu.VMEM((3 * PIECES, dim, PIECE), jnp.bfloat16),
        scratch_shapes=[
            pltpu.VMEM((2, 3, step, HEADS, HEAD_DIM), jnp.bfloat16),
            pltpu.VMEM((3, sub * HEADS, HEAD_DIM), jnp.float32),
            pltpu.SemaphoreType.DMA((2, 3)),
        ],
        compiler_params=pltpu.CompilerParams(vmem_limit_bytes=JOIN_VMEM),
        cost_estimate=pl.CostEstimate(flops=6 * dim * COLS, bytes_accessed=6 * dim * COLS, transcendentals=0),
        name="join_weights",
    )(*weights)


def project(parts, w, owners, outs, tokens):
    arrays = [p[0] for p in parts]
    dim = w.shape[1]
    sizes = [p[1] for p in parts]
    offsets = [sum(sizes[:i]) for i in range(len(sizes))]
    rows = sum(sizes)
    blocks = arrays[0].shape[0] // sizes[0]
    steps = 3 * blocks
    slots = min(blocks, 2)
    quarter = rows // PIECES

    def body(owners_ref, *refs):
        n_hbm, w_ref = refs[: len(parts)], refs[len(parts)]
        q_out, k_out, v_out, n_buf, total, stage, n_sem, o_sem = refs[-8:]

        def fetch(b, do):
            slot = lax.rem(b, slots)
            for i, size in enumerate(sizes):
                src = n_hbm[i].at[pl.ds(pl.multiple_of(b * size, size), size)]
                do(pltpu.make_async_copy(src, n_buf.at[slot, pl.ds(offsets[i], size)], n_sem.at[slot, i]))

        def store(s, do):
            b, j = s // 3, lax.rem(s, 3)
            slot = lax.rem(s, 2)
            for index, out in enumerate((q_out, k_out, v_out)):

                @pl.when(j == index)
                def _(out=out):
                    for i, (_, size, which, start) in enumerate(parts):
                        first = owners_ref[which] * (tokens // 4) + start + b * size
                        src = stage.at[slot, pl.ds(offsets[i], size)]
                        do(pltpu.make_async_copy(src, out.at[pl.ds(first, size)], o_sem.at[slot, i]))

        def emit(slot, start, size):
            src = pl.ds(pl.multiple_of(start * HEADS, size * HEADS), size * HEADS)
            got = total[slot, src, :].reshape(size, HEADS, HEAD_DIM).astype(jnp.bfloat16)
            stage[slot, pl.ds(pl.multiple_of(start, size), size)] = got

        def begin(copy):
            copy.start()

        def end(copy):
            copy.wait()

        fetch(0, begin)

        def step(s, carry):
            b, j = s // 3, lax.rem(s, 3)
            slot = lax.rem(s, 2)
            pl.when(s >= 3)(lambda: store(s - 3, end))

            @pl.when(j == 0)
            def _():
                fetch(b, end)
                if blocks > 1:
                    pl.when(b + 1 < blocks)(lambda: fetch(b + 1, begin))

            def part(i, carry):
                emit(1 - slot, i * quarter, quarter)
                got = jnp.dot(n_buf[lax.rem(b, slots)], w_ref[j * PIECES + i], preferred_element_type=jnp.float32)
                for side in range(SIDES):
                    total[slot, pl.ds(SIDES * i + side, rows, stride=HEADS), :] = got[:, side * HEAD_DIM : (side + 1) * HEAD_DIM]
                return carry

            lax.fori_loop(0, PIECES, part, 0)
            pl.when(s >= 1)(lambda: store(s - 1, begin))
            return carry

        lax.fori_loop(0, steps, step, 0)
        last = steps - 1
        store(last - 2, end)
        lax.fori_loop(0, PIECES, lambda i, carry: (emit(last % 2, i * quarter, quarter), carry)[1], 0)
        store(last, begin)
        store(last - 1, end)
        store(last, end)

    return pl.pallas_call(
        body,
        in_specs=[pl.BlockSpec(memory_space=pltpu.SMEM)]
        + [pl.BlockSpec(memory_space=pl.ANY)] * len(parts)
        + [pl.BlockSpec(memory_space=pltpu.VMEM)]
        + [pl.BlockSpec(memory_space=pl.ANY)] * len(outs),
        out_specs=[pl.BlockSpec(memory_space=pl.ANY)] * 3,
        out_shape=[jax.ShapeDtypeStruct((tokens, HEADS, HEAD_DIM), jnp.bfloat16)] * 3,
        scratch_shapes=[
            pltpu.VMEM((slots, rows, dim), jnp.bfloat16),
            pltpu.VMEM((2, rows * HEADS, HEAD_DIM), jnp.float32),
            pltpu.VMEM((2, rows, HEADS, HEAD_DIM), jnp.bfloat16),
            pltpu.SemaphoreType.DMA((slots, len(parts))),
            pltpu.SemaphoreType.DMA((2, len(parts))),
        ],
        input_output_aliases={len(parts) + 2 + i: i for i in range(len(outs))},
        compiler_params=pltpu.CompilerParams(vmem_limit_bytes=PROJECT_VMEM),
        cost_estimate=pl.CostEstimate(
            flops=6 * blocks * rows * dim * COLS,
            bytes_accessed=2 * blocks * (rows * dim + 3 * rows * COLS),
            transcendentals=0,
        ),
        name="project",
    )(owners, *arrays, pltpu.with_memory_space_constraint(w, pltpu.VMEM), *outs)


def solution(mesh):
    across = [(0, 2), (1, 3), (2, 0), (3, 1)]
    beside = [(0, 1), (1, 0), (2, 3), (3, 2)]

    def inner(hidden_blk, norm_gain, wq_local, wk_local, wv_local):
        block, dim = hidden_blk.shape
        tokens = 4 * block
        me = lax.axis_index("tp").astype(jnp.int32)
        owners = me ^ jnp.arange(4, dtype=jnp.int32)
        starts = [sum(CHUNKS[:i]) for i in range(len(CHUNKS))]

        gain = norm_gain.reshape(1, dim)
        near = []
        for i in range(EARLY):
            m = normalize_some(hidden_blk, gain, starts[i], CHUNKS[i])
            near.append(lax.ppermute(m, "tp", across))
        own, *rest = normalize_all(hidden_blk, gain, CHUNKS, EARLY)
        for m in rest:
            near.append(lax.ppermute(m, "tp", across))
        paired = lax.ppermute(own, "tp", beside)
        w = join_weights(wq_local, wk_local, wv_local)

        far = {}

        def arrive(outs, *chunks):
            got = lax.optimization_barrier((tuple(near[i] for i in chunks), tuple(outs)))
            for i, a in zip(chunks, got[0]):
                near[i] = a
                far[i] = lax.ppermute(a, "tp", beside)
            return got[1]

        outs = project([(own, BIG, 0, 0)], w, owners, (), tokens)
        outs = arrive(outs, 0, 1, 2)
        outs = project([(paired, BIG, 1, 0)], w, owners, outs, tokens)
        outs = arrive(outs, 3)
        before = {5: (5,), 6: (6,), 7: (7,), 8: (8,), 9: (9, 10)}
        after = {2: (4,)}
        for group in ((0, 1), (2,), (3,), (4,), (5,), (6,), (7,), (8,), (9, 10)):
            for i in before.get(group[0], ()):
                outs = arrive(outs, i)
            parts = [(near[i], CHUNKS[i], 2, starts[i]) for i in group] + [(far[i], CHUNKS[i], 3, starts[i]) for i in group]
            outs = project(parts, w, owners, outs, tokens)
            for i in after.get(group[0], ()):
                outs = arrive(outs, i)
        return tuple(outs)

    row_spec = P(("dp", "tp"), None)
    head_spec = P(None, "tp", None)
    out_spec = P("dp", "tp", None)
    return jax.shard_map(inner, mesh=mesh, in_specs=(row_spec, P(None), head_spec, head_spec, head_spec), out_specs=(out_spec, out_spec, out_spec), check_vma=False)
```

time: 486 us -> 476 us (0.979)
  Pallas kernels: 345 us -> 310 us
  waiting for transfers between devices: 124 us -> 145 us
    pallas_call x11, Pallas kernels: 293 us -> 265 us  [project(): pl.pallas_call(body, in_specs=[pl.BlockSpec(memory_space=pltpu.SMEM)] + [...]
    ppermute x8 -> x11, waiting for transfers between devices: 113 us -> 135 us  [inner(): near.append(lax.ppermute(m, 'tp', across))]
    pallas_call x2 -> x3, Pallas kernels: 28.5 us -> 21.7 us  [the longest x1 15.7 us: join_weights(): pl.pallas_call(body, in_specs=[pl.BlockSpec(memory_space=pl.ANY)] * 3, ou...]
    ppermute x8 -> x11, starting transfers between devices: 11.1 us -> 17.5 us  [inner(): near.append(lax.ppermute(m, 'tp', across))]
    ppermute x9 -> x11, waiting for transfers between devices: 10.7 us -> 9.53 us  [arrive(): far[i] = lax.ppermute(a, 'tp', beside)]
  transfers between devices with their start and end apart: 19 -> 23, of which waited for: 11 -> 12; matrix products, arithmetic and copies ran while one was open for 0% -> 0% of each run, Pallas kernels for 64% -> 58%
where the time goes in v4:
time: 476 us; the launch traced here: 475 us
  Pallas kernels  310 us (65%)
  waiting for transfers between devices  145 us (30%)
  starting transfers between devices  19.4 us (4%)
    pallas_call x11, Pallas kernels, project(): pl.pallas_call(body, in_specs=[pl.BlockSpec(memory_space=pltpu.SMEM)] + [...  265 us
    ppermute x11, waiting for transfers between devices, inner(): near.append(lax.ppermute(m, 'tp', across))  135 us
    pallas_call x1, Pallas kernels, normalize_all(): pl.pallas_call(body, grid=(block // step,), in_specs=[pl.BlockSpec((step,...  23.5 us
    ppermute x11, starting transfers between devices, inner(): near.append(lax.ppermute(m, 'tp', across))  17.5 us
    pallas_call x1, Pallas kernels, join_weights(): pl.pallas_call(body, in_specs=[pl.BlockSpec(memory_space=pl.ANY)] * 3, ou...  15.7 us
    ppermute x11, waiting for transfers between devices, arrive(): far[i] = lax.ppermute(a, 'tp', beside)  9.53 us
  transfers between devices with their start and end apart: 23, of which 12 were waited for; matrix products, arithmetic and copies ran while one was open for 0% of the time, Pallas kernels for 58%

profile of v4, /device:TPU:0, one launch (start us, length us, event | category | flops | bytes accessed | tf_op | source)
XLA Modules:
  0.0 474.9 jit_solution(6314681838396234759)
XLA Ops:
  0.6 23.5 %normalize_all.1 = (bf16[2048,4096]{1,0:T(8,128)(2,1)}, bf16[256,4096]{1,0:T(8,128)(2,1)}, bf16[256,4096]{1,0:T(8,128)(2,1)}, bf16[256,4096]{1,0:T(8,128)(2,1)},...) custom-call(bf16[2048,4096]{1,0:T(8,128)(2,1)} %x_ref.5, ...), custom_call_target="tpu_custom_call" | custom-call | flops 67108864 | bytes 50331648 | tf_op jit(solution)/shard_map/normalize_all/pallas_call | solution.py:95
  27.1 2.5 collective-permute-start.6
  29.6 3.8 normalize_some.3
  35.4 15.7 %join_weights.1.refs_1_.refs_4_.refs_2_ = bf16[6,4096,512]{2,1,0:T(8,128)(2,1)S(1)} custom-call(bf16[4096,8,128]{2,1,0:T(8,128)(2,1)} %a_ref.1, bf16[4096,8,128]{2,1,0:T(8,128)(2,1)} %b_ref.1, bf16[4096,8,128]{2,1,0:T(8,128)(2,1)} %c_ref.1), custom_call_target="tpu_custom_call" | custom-call | flops 25165824 | bytes 25165824 | tf_op jit(solution)/shard_map/join_weights/pallas_call | solution.py:142
  51.1 62.7 %project.11 = (bf16[8192,8,128]{2,1,0:T(8,128)(2,1)}, bf16[8192,8,128]{2,1,0:T(8,128)(2,1)}, bf16[8192,8,128]{2,1,0:T(8,128)(2,1)}) custom-call(s32[4]{0:T(128)S(1)} %iota_xor_fusion.owners_ref, bf16[2048,4096]{1,0:T(8,128)(2,1)} %get-tuple-element.88.refs_0_, bf16[6,4096,512]{2,1,0:T(8,128)(2,1)S(1)} %join_weights.1.refs_1_.refs_4_.refs_2_), custom_call_target="tpu_custom_call" | custom-call | flops 51539607552 | bytes 29360128 | tf_op jit(solution)/shard_map/project/pallas_call | solution.py:234
  115.9 50.2 %collective-permute-done.8.refs_0_ = bf16[256,4096]{1,0:T(8,128)(2,1)S(1)} collective-permute-done((bf16[256,4096]{1,0:T(8,128)(2,1)}, bf16[256,4096]{1,0:T(8,128)(2,1)S(1)}, u32[]{:S(2)}, u32[]{:S(2)}) %collective-permute-start.8) | collective-permute-done | bytes 2097184 | tf_op jit(solution)/shard_map/ppermute | solution.py:278
  166.7 62.7 %project.12 = (bf16[8192,8,128]{2,1,0:T(8,128)(2,1)}, bf16[8192,8,128]{2,1,0:T(8,128)(2,1)}, bf16[8192,8,128]{2,1,0:T(8,128)(2,1)}) custom-call(s32[4]{0:T(128)S(1)} %iota_xor_fusion.owners_ref, bf16[2048,4096]{1,0:T(8,128)(2,1)} %collective-permute-done.13.refs_0_, ...), custom_call_target="tpu_custom_call", output_to_operand_aliasing={{0}: (3, {}), {1}: (4, {}), {2}: (5, {})} | custom-call | flops 51539607552 | bytes 29360128 | tf_op jit(solution)/shard_map/project/pallas_call | solution.py:234
  229.9 18.0 %project.13 = (bf16[8192,8,128]{2,1,0:T(8,128)(2,1)}, bf16[8192,8,128]{2,1,0:T(8,128)(2,1)}, bf16[8192,8,128]{2,1,0:T(8,128)(2,1)}) custom-call(s32[4]{0:T(128)S(1)} %iota_xor_fusion.owners_ref, bf16[64,4096]{1,0:T(8,128)(2,1)S(1)} %collective-permute-done.6.refs_0_, ...), custom_call_target="tpu_custom_call", output_to_operand_aliasing={{0}: (6, {}), {1}: (7, {}), {2}: (8, {})} | custom-call | flops 12884901888 | bytes 7340032 | tf_op jit(solution)/shard_map/project/pallas_call | solution.py:234
  247.9 16.8 %project.14 = (bf16[8192,8,128]{2,1,0:T(8,128)(2,1)}, bf16[8192,8,128]{2,1,0:T(8,128)(2,1)}, bf16[8192,8,128]{2,1,0:T(8,128)(2,1)}) custom-call(s32[4]{0:T(128)S(1)} %iota_xor_fusion.owners_ref, bf16[256,4096]{1,0:T(8,128)(2,1)S(1)} %collective-permute-done.8.refs_0_, ...), custom_call_target="tpu_custom_call", output_to_operand_aliasing={{0}: (4, {}), {1}: (5, {}), {2}: (6, {})} | custom-call | flops 12884901888 | bytes 7340032 | tf_op jit(solution)/shard_map/project/pallas_call | solution.py:234
  266.8 16.8 %project.15 = (bf16[8192,8,128]{2,1,0:T(8,128)(2,1)}, bf16[8192,8,128]{2,1,0:T(8,128)(2,1)}, bf16[8192,8,128]{2,1,0:T(8,128)(2,1)}) custom-call(s32[4]{0:T(128)S(1)} %iota_xor_fusion.owners_ref, bf16[256,4096]{1,0:T(8,128)(2,1)S(1)} %collective-permute-done.12.refs_0_, ...), custom_call_target="tpu_custom_call", output_to_operand_aliasing={{0}: (4, {}), {1}: (5, {}), {2}: (6, {})} | custom-call | flops 12884901888 | bytes 7340032 | tf_op jit(solution)/shard_map/project/pallas_call | solution.py:234
  283.6 18.1 %project.16 = (bf16[8192,8,128]{2,1,0:T(8,128)(2,1)}, bf16[8192,8,128]{2,1,0:T(8,128)(2,1)}, bf16[8192,8,128]{2,1,0:T(8,128)(2,1)}) custom-call(s32[4]{0:T(128)S(1)} %iota_xor_fusion.owners_ref, bf16[256,4096]{1,0:T(8,128)(2,1)} %collective-permute-done.5.refs_0_, ...), custom_call_target="tpu_custom_call", output_to_operand_aliasing={{0}: (4, {}), {1}: (5, {}), {2}: (6, {})} | custom-call | flops 12884901888 | bytes 7340032 | tf_op jit(solution)/shard_map/project/pallas_call | solution.py:234
  301.8 11.5 %collective-permute-done.4.refs_0_ = bf16[256,4096]{1,0:T(8,128)(2,1)S(1)} collective-permute-done((bf16[256,4096]{1,0:T(8,128)(2,1)}, bf16[256,4096]{1,0:T(8,128)(2,1)S(1)}, u32[]{:S(2)}, u32[]{:S(2)}) %collective-permute-start.4) | collective-permute-done | bytes 2097184 | tf_op jit(solution)/shard_map/ppermute | solution.py:278
  317.4 16.8 %project.17 = (bf16[8192,8,128]{2,1,0:T(8,128)(2,1)}, bf16[8192,8,128]{2,1,0:T(8,128)(2,1)}, bf16[8192,8,128]{2,1,0:T(8,128)(2,1)}) custom-call(s32[4]{0:T(128)S(1)} %iota_xor_fusion.owners_ref, bf16[256,4096]{1,0:T(8,128)(2,1)S(1)} %collective-permute-done.4.refs_0_, ...), custom_call_target="tpu_custom_call", output_to_operand_aliasing={{0}: (4, {}), {1}: (5, {}), {2}: (6, {})} | custom-call | flops 12884901888 | bytes 7340032 | tf_op jit(solution)/shard_map/project/pallas_call | solution.py:234
  334.2 27.1 %collective-permute-done.3.refs_0_ = bf16[256,4096]{1,0:T(8,128)(2,1)S(1)} collective-permute-done((bf16[256,4096]{1,0:T(8,128)(2,1)S(1)}, bf16[256,4096]{1,0:T(8,128)(2,1)S(1)}, u32[]{:S(2)}, u32[]{:S(2)}) %collective-permute-start.3) | collective-permute-done | bytes 2097184 | tf_op jit(solution)/shard_map/ppermute | solution.py:278
  363.1 2.4 collective-permute-done.17.refs_1_
  365.5 17.0 %project.18 = (bf16[8192,8,128]{2,1,0:T(8,128)(2,1)}, bf16[8192,8,128]{2,1,0:T(8,128)(2,1)}, bf16[8192,8,128]{2,1,0:T(8,128)(2,1)}) custom-call(s32[4]{0:T(128)S(1)} %iota_xor_fusion.owners_ref, bf16[256,4096]{1,0:T(8,128)(2,1)S(1)} %collective-permute-done.3.refs_0_, ...), custom_call_target="tpu_custom_call", output_to_operand_aliasing={{0}: (4, {}), {1}: (5, {}), {2}: (6, {})} | custom-call | flops 12884901888 | bytes 7340032 | tf_op jit(solution)/shard_map/project/pallas_call | solution.py:234
  382.4 26.9 %collective-permute-done.2.refs_0_ = bf16[256,4096]{1,0:T(8,128)(2,1)S(1)} collective-permute-done((bf16[256,4096]{1,0:T(8,128)(2,1)S(1)}, bf16[256,4096]{1,0:T(8,128)(2,1)S(1)}, u32[]{:S(2)}, u32[]{:S(2)}) %collective-permute-start.2) | collective-permute-done | bytes 2097184 | tf_op jit(solution)/shard_map/ppermute | solution.py:278
  411.2 2.4 collective-permute-done.18.refs_1_
  413.5 16.8 %project.19 = (bf16[8192,8,128]{2,1,0:T(8,128)(2,1)}, bf16[8192,8,128]{2,1,0:T(8,128)(2,1)}, bf16[8192,8,128]{2,1,0:T(8,128)(2,1)}) custom-call(s32[4]{0:T(128)S(1)} %iota_xor_fusion.owners_ref, bf16[256,4096]{1,0:T(8,128)(2,1)S(1)} %collective-permute-done.2.refs_0_, ...), custom_call_target="tpu_custom_call", output_to_operand_aliasing={{0}: (4, {}), {1}: (5, {}), {2}: (6, {})} | custom-call | flops 12884901888 | bytes 7340032 | tf_op jit(solution)/shard_map/project/pallas_call | solution.py:234
  430.3 4.6 collective-permute-done.1.refs_0_
  437.6 9.5 %project.20 = (bf16[8192,8,128]{2,1,0:T(8,128)(2,1)}, bf16[8192,8,128]{2,1,0:T(8,128)(2,1)}, bf16[8192,8,128]{2,1,0:T(8,128)(2,1)}) custom-call(s32[4]{0:T(128)S(1)} %iota_xor_fusion.owners_ref, bf16[128,4096]{1,0:T(8,128)(2,1)S(1)} %collective-permute-done.1.refs_0_, ...), custom_call_target="tpu_custom_call", output_to_operand_aliasing={{0}: (4, {}), {1}: (5, {}), {2}: (6, {})} | custom-call | flops 6442450944 | bytes 3670016 | tf_op jit(solution)/shard_map/project/pallas_call | solution.py:234
  447.1 7.8 %collective-permute-done.refs_0_ = bf16[96,4096]{1,0:T(8,128)(2,1)S(1)} collective-permute-done((bf16[96,4096]{1,0:T(8,128)(2,1)S(1)}, bf16[96,4096]{1,0:T(8,128)(2,1)S(1)}, u32[]{:S(2)}, u32[]{:S(2)}) %collective-permute-start) | collective-permute-done | bytes 786464 | tf_op jit(solution)/shard_map/ppermute | solution.py:278
  456.7 7.0 %collective-permute-done.20.refs_1_ = bf16[32,4096]{1,0:T(8,128)(2,1)S(1)} collective-permute-done((bf16[32,4096]{1,0:T(8,128)(2,1)S(1)}, bf16[32,4096]{1,0:T(8,128)(2,1)S(1)}, u32[]{:S(2)}, u32[]{:S(2)}) %collective-permute-start.20) | collective-permute-done | bytes 262176 | tf_op jit(solution)/shard_map/ppermute | solution.py:278
  465.2 9.6 %project.21 = (bf16[8192,8,128]{2,1,0:T(8,128)(2,1)}, bf16[8192,8,128]{2,1,0:T(8,128)(2,1)}, bf16[8192,8,128]{2,1,0:T(8,128)(2,1)}) custom-call(s32[4]{0:T(128)S(1)} %iota_xor_fusion.owners_ref, bf16[96,4096]{1,0:T(8,128)(2,1)S(1)} %collective-permute-done.refs_0_, ...), custom_call_target="tpu_custom_call", output_to_operand_aliasing={{0}: (6, {}), {1}: (7, {}), {2}: (8, {})} | custom-call | flops 6442450944 | bytes 3670016 | tf_op jit(solution)/shard_map/project/pallas_call | solution.py:234
  (50 shorter events, 23.9 us)
Async XLA Ops:
  24.1 142.5 %collective-permute-start.13 = (bf16[2048,4096]{1,0:T(8,128)(2,1)}, bf16[2048,4096]{1,0:T(8,128)(2,1)}, u32[]{:S(2)}, u32[]{:S(2)}) collective-permute-start(bf16[2048,4096]{1,0:T(8,128)(2,1)} %get-tuple-element.88.refs_0_), channel_id=1, source_target_pairs={{0,1},{1,0},{2,3},{3,2},{4,5},{5,4},{6,7},{7,6},{8,9},{9,8},{10,11... | collective-permute-start | bytes 50331656 | tf_op jit(solution)/shard_map/ppermute | solution.py:279
  27.1 86.8 %collective-permute-start.6 = (bf16[64,4096]{1,0:T(8,128)(2,1)}, bf16[64,4096]{1,0:T(8,128)(2,1)S(1)}, u32[]{:S(2)}, u32[]{:S(2)}) collective-permute-start(bf16[64,4096]{1,0:T(8,128)(2,1)} %normalize_some.2), channel_id=1, source_target_pairs={{0,2},{1,3},{2,0},{3,1},{4,6},{5,7},{6,4},{7,5},{8,10},{9,11},{10,... | collective-permute-start | bytes 1572872 | tf_op jit(solution)/shard_map/ppermute | solution.py:275
  33.4 82.6 %collective-permute-start.7 = (bf16[192,4096]{1,0:T(8,128)(2,1)}, bf16[192,4096]{1,0:T(8,128)(2,1)}, u32[]{:S(2)}, u32[]{:S(2)}) collective-permute-start(bf16[192,4096]{1,0:T(8,128)(2,1)} %normalize_some.3), channel_id=1, source_target_pairs={{0,2},{1,3},{2,0},{3,1},{4,6},{5,7},{6,4},{7,5},{8,10},{9,11},{10,... | collective-permute-start | bytes 4718600 | tf_op jit(solution)/shard_map/ppermute | solution.py:275
  33.4 231.3 %collective-permute-start.5 = (bf16[256,4096]{1,0:T(8,128)(2,1)}, bf16[256,4096]{1,0:T(8,128)(2,1)}, u32[]{:S(2)}, u32[]{:S(2)}) collective-permute-start(bf16[256,4096]{1,0:T(8,128)(2,1)} %get-tuple-element.86), channel_id=1, source_target_pairs={{0,2},{1,3},{2,0},{3,1},{4,6},{5,7},{6,4},{7,5},{8,10},{9,11},{10,... | collective-permute-start | bytes 6291464 | tf_op jit(solution)/shard_map/ppermute | solution.py:278
  35.4 130.8 %collective-permute-start.8 = (bf16[256,4096]{1,0:T(8,128)(2,1)}, bf16[256,4096]{1,0:T(8,128)(2,1)S(1)}, u32[]{:S(2)}, u32[]{:S(2)}) collective-permute-start(bf16[256,4096]{1,0:T(8,128)(2,1)} %get-tuple-element.87), channel_id=1, source_target_pairs={{0,2},{1,3},{2,0},{3,1},{4,6},{5,7},{6,4},{7,5},{8,10},{9,11},{10,... | collective-permute-start | bytes 6291464 | tf_op jit(solution)/shard_map/ppermute | solution.py:278
  51.1 62.8 %copy-start.2 = (bf16[256,4096]{1,0:T(8,128)(2,1)S(1)}, bf16[256,4096]{1,0:T(8,128)(2,1)}, u32[]{:S(2)}) copy-start(bf16[256,4096]{1,0:T(8,128)(2,1)} %get-tuple-element.95) | copy-start | bytes 6291460
  113.9 115.4 %collective-permute-start.12 = (bf16[256,4096]{1,0:T(8,128)(2,1)S(1)}, bf16[256,4096]{1,0:T(8,128)(2,1)S(1)}, u32[]{:S(2)}, u32[]{:S(2)}) collective-permute-start(bf16[256,4096]{1,0:T(8,128)(2,1)S(1)} %copy-done.2), channel_id=1, source_target_pairs={{0,2},{1,3},{2,0},{3,1},{4,6},{5,7},{6,4},{7,5},{8,10},{9,11},{10,... | collective-permute-start | bytes 6291464 | tf_op jit(solution)/shard_map/ppermute | solution.py:278
  166.1 63.7 %collective-permute-start.10 = (bf16[64,4096]{1,0:T(8,128)(2,1)S(1)}, bf16[64,4096]{1,0:T(8,128)(2,1)S(1)}, u32[]{:S(2)}, u32[]{:S(2)}) collective-permute-start(bf16[64,4096]{1,0:T(8,128)(2,1)S(1)} %collective-permute-done.6.refs_0_), channel_id=1, source_target_pairs={{0,1},{1,0},{2,3},{3,2},{4,5},{5,4},{6,7},{7,6},{8,9},{9,8},{10,11... | collective-permute-start | bytes 1572872 | tf_op jit(solution)/shard_map/ppermute | solution.py:288
  166.1 63.7 %collective-permute-start.11 = (bf16[192,4096]{1,0:T(8,128)(2,1)}, bf16[192,4096]{1,0:T(8,128)(2,1)S(1)}, u32[]{:S(2)}, u32[]{:S(2)}) collective-permute-start(bf16[192,4096]{1,0:T(8,128)(2,1)} %collective-permute-done.7.refs_1_), channel_id=1, source_target_pairs={{0,1},{1,0},{2,3},{3,2},{4,5},{5,4},{6,7},{7,6},{8,9},{9,8},{10,11... | collective-permute-start | bytes 4718600 | tf_op jit(solution)/shard_map/ppermute | solution.py:288
  166.7 81.2 %collective-permute-start.9 = (bf16[256,4096]{1,0:T(8,128)(2,1)S(1)}, bf16[256,4096]{1,0:T(8,128)(2,1)S(1)}, u32[]{:S(2)}, u32[]{:S(2)}) collective-permute-start(bf16[256,4096]{1,0:T(8,128)(2,1)S(1)} %collective-permute-done.8.refs_0_), channel_id=1, source_target_pairs={{0,1},{1,0},{2,3},{3,2},{4,5},{5,4},{6,7},{7,6},{8,9},{9,8},{10,11... | collective-permute-start | bytes 6291464 | tf_op jit(solution)/shard_map/ppermute | solution.py:288
  229.3 37.5 %collective-permute-start.15 = (bf16[256,4096]{1,0:T(8,128)(2,1)S(1)}, bf16[256,4096]{1,0:T(8,128)(2,1)S(1)}, u32[]{:S(2)}, u32[]{:S(2)}) collective-permute-start(bf16[256,4096]{1,0:T(8,128)(2,1)S(1)} %collective-permute-done.12.refs_0_), channel_id=1, source_target_pairs={{0,1},{1,0},{2,3},{3,2},{4,5},{5,4},{6,7},{7,6},{8,9},{9,8},{10,11... | collective-permute-start | bytes 6291464 | tf_op jit(solution)/shard_map/ppermute | solution.py:288
  264.7 18.9 %collective-permute-start.14 = (bf16[256,4096]{1,0:T(8,128)(2,1)}, bf16[256,4096]{1,0:T(8,128)(2,1)S(1)}, u32[]{:S(2)}, u32[]{:S(2)}) collective-permute-start(bf16[256,4096]{1,0:T(8,128)(2,1)} %collective-permute-done.5.refs_0_), channel_id=1, source_target_pairs={{0,1},{1,0},{2,3},{3,2},{4,5},{5,4},{6,7},{7,6},{8,9},{9,8},{10,11... | collective-permute-start | bytes 6291464 | tf_op jit(solution)/shard_map/ppermute | solution.py:288
  264.8 48.5 %collective-permute-start.4 = (bf16[256,4096]{1,0:T(8,128)(2,1)}, bf16[256,4096]{1,0:T(8,128)(2,1)S(1)}, u32[]{:S(2)}, u32[]{:S(2)}) collective-permute-start(bf16[256,4096]{1,0:T(8,128)(2,1)} %get-tuple-element.85), channel_id=1, source_target_pairs={{0,2},{1,3},{2,0},{3,1},{4,6},{5,7},{6,4},{7,5},{8,10},{9,11},{10,... | collective-permute-start | bytes 6291464 | tf_op jit(solution)/shard_map/ppermute | solution.py:278
  313.3 4.2 collective-permute-start.16
  313.3 48.0 %collective-permute-start.3 = (bf16[256,4096]{1,0:T(8,128)(2,1)S(1)}, bf16[256,4096]{1,0:T(8,128)(2,1)S(1)}, u32[]{:S(2)}, u32[]{:S(2)}) collective-permute-start(bf16[256,4096]{1,0:T(8,128)(2,1)S(1)} %copy-done.1), channel_id=1, source_target_pairs={{0,2},{1,3},{2,0},{3,1},{4,6},{5,7},{6,4},{7,5},{8,10},{9,11},{10,... | collective-permute-start | bytes 6291464 | tf_op jit(solution)/shard_map/ppermute | solution.py:278
  361.3 4.2 collective-permute-start.17
  361.3 48.0 %collective-permute-start.2 = (bf16[256,4096]{1,0:T(8,128)(2,1)S(1)}, bf16[256,4096]{1,0:T(8,128)(2,1)S(1)}, u32[]{:S(2)}, u32[]{:S(2)}) collective-permute-start(bf16[256,4096]{1,0:T(8,128)(2,1)S(1)} %copy-done), channel_id=1, source_target_pairs={{0,2},{1,3},{2,0},{3,1},{4,6},{5,7},{6,4},{7,5},{8,10},{9,11},{10,... | collective-permute-start | bytes 6291464 | tf_op jit(solution)/shard_map/ppermute | solution.py:278
  409.4 4.2 collective-permute-start.18
  409.4 25.6 %collective-permute-start.1 = (bf16[128,4096]{1,0:T(8,128)(2,1)S(1)}, bf16[128,4096]{1,0:T(8,128)(2,1)S(1)}, u32[]{:S(2)}, u32[]{:S(2)}) collective-permute-start(bf16[128,4096]{1,0:T(8,128)(2,1)S(1)} %copy-done.3), channel_id=1, source_target_pairs={{0,2},{1,3},{2,0},{3,1},{4,6},{5,7},{6,4},{7,5},{8,10},{9,11},{10,... | collective-permute-start | bytes 3145736 | tf_op jit(solution)/shard_map/ppermute | solution.py:278
  435.0 2.7 collective-permute-start.19
  435.0 20.0 %collective-permute-start = (bf16[96,4096]{1,0:T(8,128)(2,1)S(1)}, bf16[96,4096]{1,0:T(8,128)(2,1)S(1)}, u32[]{:S(2)}, u32[]{:S(2)}) collective-permute-start(bf16[96,4096]{1,0:T(8,128)(2,1)S(1)} %copy-done.4), channel_id=1, source_target_pairs={{0,2},{1,3},{2,0},{3,1},{4,6},{5,7},{6,4},{7,5},{8,10},{9,11},{10,... | collective-permute-start | bytes 2359304 | tf_op jit(solution)/shard_map/ppermute | solution.py:278
  454.9 10.3 %collective-permute-start.21 = (bf16[96,4096]{1,0:T(8,128)(2,1)S(1)}, bf16[96,4096]{1,0:T(8,128)(2,1)S(1)}, u32[]{:S(2)}, u32[]{:S(2)}) collective-permute-start(bf16[96,4096]{1,0:T(8,128)(2,1)S(1)} %collective-permute-done.refs_0_), channel_id=1, source_target_pairs={{0,1},{1,0},{2,3},{3,2},{4,5},{5,4},{6,7},{7,6},{8,9},{9,8},{10,11... | collective-permute-start | bytes 2359304 | tf_op jit(solution)/shard_map/ppermute | solution.py:288
  454.9 8.7 %collective-permute-start.20 = (bf16[32,4096]{1,0:T(8,128)(2,1)S(1)}, bf16[32,4096]{1,0:T(8,128)(2,1)S(1)}, u32[]{:S(2)}, u32[]{:S(2)}) collective-permute-start(bf16[32,4096]{1,0:T(8,128)(2,1)S(1)} %copy-done.5), channel_id=1, source_target_pairs={{0,2},{1,3},{2,0},{3,1},{4,6},{5,7},{6,4},{7,5},{8,10},{9,11},{10,... | collective-permute-start | bytes 786440 | tf_op jit(solution)/shard_map/ppermute | solution.py:278
  463.6 1.5 collective-permute-start.22
  (5 other events, 171.3 us)

commit v5 on v4

--- a/solution.py
+++ b/solution.py
@@ -13,34 +13,69 @@
 PIECE = SIDES * HEAD_DIM
 PIECES = COLS // PIECE
 MIB = 1024 * 1024
-VMEM = 60 * MIB
+VMEM = 48 * MIB
 PROJECT_VMEM = 24 * MIB
 JOIN_VMEM = 24 * MIB
 
-CHUNKS = (64, 192, 256, 256, 256, 256, 256, 256, 128, 96, 32)
+CHUNKS = (64, 192, 256, 256, 256, 256, 256, 240, 128, 80, 64)
 EARLY = 2
 BIG = 512
 NORM_ROWS = 128
 
 
+def normalize_piece(x_ref, g_ref, n_ref, at):
+    lanes = 128
+    dim = x_ref.shape[1]
+    squares = [jnp.zeros((at.size, lanes), jnp.float32) for _ in range(2)]
+    for k in range(dim // lanes):
+        v = x_ref[at, k * lanes : (k + 1) * lanes].astype(jnp.float32)
+        squares[k % 2] += v * v
+    mean = jnp.sum(squares[0] + squares[1], axis=-1, keepdims=True) / dim
+    scale = jnp.broadcast_to(lax.rsqrt(mean + 1e-6), (at.size, lanes))
+    for k in range(dim // lanes):
+        cols = slice(k * lanes, (k + 1) * lanes)
+        n_ref[at, cols] = (x_ref[at, cols].astype(jnp.float32) * scale * g_ref[:, cols]).astype(jnp.bfloat16)
+
+
 def normalize_rows(x_ref, g_ref, n_ref):
-    sub, lanes = 32, 128
-    dim = x_ref.shape[1]
+    sub = 32
 
     def piece(i, carry):
-        at = pl.ds(pl.multiple_of(i * sub, sub), sub)
-        squares = [jnp.zeros((sub, lanes), jnp.float32) for _ in range(2)]
-        for k in range(dim // lanes):
-            v = x_ref[at, k * lanes : (k + 1) * lanes].astype(jnp.float32)
-            squares[k % 2] += v * v
-        mean = jnp.sum(squares[0] + squares[1], axis=-1, keepdims=True) / dim
-        scale = jnp.broadcast_to(lax.rsqrt(mean + 1e-6), (sub, lanes))
-        for k in range(dim // lanes):
-            cols = slice(k * lanes, (k + 1) * lanes)
-            n_ref[at, cols] = (x_ref[at, cols].astype(jnp.float32) * scale * g_ref[:, cols]).astype(jnp.bfloat16)
+        normalize_piece(x_ref, g_ref, n_ref, pl.ds(pl.multiple_of(i * sub, sub), sub))
         return carry
 
     lax.fori_loop(0, x_ref.shape[0] // sub, piece, 0)
+
+
+def normalize_first(x, norm_gain, rows):
+    dim = x.shape[1]
+    sub = 32
+
+    def body(x_hbm, g_hbm, n_ref, x_buf, g_buf, sem):
+        gain = pltpu.make_async_copy(g_hbm, g_buf, sem.at[0])
+        pieces = [pl.ds(i * sub, sub) for i in range(rows // sub)]
+        copies = [pltpu.make_async_copy(x_hbm.at[at], x_buf.at[at], sem.at[1 + i]) for i, at in enumerate(pieces)]
+        for copy in [gain] + copies:
+            copy.start()
+        gain.wait()
+        for at, copy in zip(pieces, copies):
+            copy.wait()
+            normalize_piece(x_buf, g_buf, n_ref, at)
+
+    return pl.pallas_call(
+        body,
+        in_specs=[pl.BlockSpec(memory_space=pl.ANY)] * 2,
+        out_specs=pl.BlockSpec(memory_space=pltpu.VMEM),
+        out_shape=pltpu.VMEM((rows, dim), jnp.bfloat16),
+        scratch_shapes=[
+            pltpu.VMEM((rows, dim), jnp.bfloat16),
+            pltpu.VMEM((1, dim), jnp.float32),
+            pltpu.SemaphoreType.DMA((1 + rows // sub,)),
+        ],
+        compiler_params=pltpu.CompilerParams(vmem_limit_bytes=VMEM),
+        cost_estimate=pl.CostEstimate(flops=8 * rows * dim, bytes_accessed=2 * rows * dim, transcendentals=rows),
+        name="normalize_first",
+    )(x, norm_gain)
 
 
 def normalize_some(x, norm_gain, start, rows):
@@ -155,8 +190,25 @@
     )(*weights)
 
 
-def project(parts, w, owners, outs, tokens):
-    arrays = [p[0] for p in parts]
+def to_vmem(n):
+    def body(n_ref, out_ref, sem):
+        pltpu.make_async_copy(n_ref, out_ref, sem).start()
+        pltpu.make_async_copy(n_ref, out_ref, sem).wait()
+
+    return pl.pallas_call(
+        body,
+        in_specs=[pl.BlockSpec(memory_space=pl.ANY)],
+        out_specs=pl.BlockSpec(memory_space=pltpu.VMEM),
+        out_shape=pltpu.VMEM(n.shape, n.dtype),
+        scratch_shapes=[pltpu.SemaphoreType.DMA],
+        compiler_params=pltpu.CompilerParams(vmem_limit_bytes=MIB),
+        cost_estimate=pl.CostEstimate(flops=n.size, bytes_accessed=4 * n.size, transcendentals=0),
+        name="to_vmem",
+    )(n)
+
+
+def project(parts, w, owners, outs, tokens, resident=False):
+    arrays = [pltpu.with_memory_space_constraint(p[0], pltpu.VMEM) if resident else p[0] for p in parts]
     dim = w.shape[1]
     sizes = [p[1] for p in parts]
     offsets = [sum(sizes[:i]) for i in range(len(sizes))]
@@ -171,6 +223,11 @@
         q_out, k_out, v_out, n_buf, total, stage, n_sem, o_sem = refs[-8:]
 
         def fetch(b, do):
+            if resident:
+                if do is end:
+                    for i, size in enumerate(sizes):
+                        n_buf[0, offsets[i] : offsets[i] + size, :] = n_hbm[i][...]
+                return
             slot = lax.rem(b, slots)
             for i, size in enumerate(sizes):
                 src = n_hbm[i].at[pl.ds(pl.multiple_of(b * size, size), size)]
@@ -234,7 +291,7 @@
     return pl.pallas_call(
         body,
         in_specs=[pl.BlockSpec(memory_space=pltpu.SMEM)]
-        + [pl.BlockSpec(memory_space=pl.ANY)] * len(parts)
+        + [pl.BlockSpec(memory_space=pltpu.VMEM if resident else pl.ANY)] * len(parts)
         + [pl.BlockSpec(memory_space=pltpu.VMEM)]
         + [pl.BlockSpec(memory_space=pl.ANY)] * len(outs),
         out_specs=[pl.BlockSpec(memory_space=pl.ANY)] * 3,
@@ -268,10 +325,10 @@
         owners = me ^ jnp.arange(4, dtype=jnp.int32)
         starts = [sum(CHUNKS[:i]) for i in range(len(CHUNKS))]
 
-        gain = norm_gain.reshape(1, dim)
+        gain = pltpu.with_memory_space_constraint(norm_gain.reshape(1, dim), pltpu.HBM)
         near = []
         for i in range(EARLY):
-            m = normalize_some(hidden_blk, gain, starts[i], CHUNKS[i])
+            m = normalize_some(hidden_blk, gain, starts[i], CHUNKS[i]) if i else normalize_first(hidden_blk, gain, CHUNKS[i])
             near.append(lax.ppermute(m, "tp", across))
         own, *rest = normalize_all(hidden_blk, gain, CHUNKS, EARLY)
         for m in rest:
@@ -286,19 +343,21 @@
             for i, a in zip(chunks, got[0]):
                 near[i] = a
                 far[i] = lax.ppermute(a, "tp", beside)
+                if i == len(CHUNKS) - 1:
+                    near[i] = to_vmem(a)
             return got[1]
 
         outs = project([(own, BIG, 0, 0)], w, owners, (), tokens)
         outs = arrive(outs, 0, 1, 2)
         outs = project([(paired, BIG, 1, 0)], w, owners, outs, tokens)
         outs = arrive(outs, 3)
-        before = {5: (5,), 6: (6,), 7: (7,), 8: (8,), 9: (9, 10)}
+        before = {5: (5,), 6: (6,), 7: (7,), 8: (8,), 9: (9,), 10: (10,)}
         after = {2: (4,)}
-        for group in ((0, 1), (2,), (3,), (4,), (5,), (6,), (7,), (8,), (9, 10)):
+        for group in ((0, 1), (2,), (3,), (4,), (5,), (6,), (7,), (8,), (9,), (10,)):
             for i in before.get(group[0], ()):
                 outs = arrive(outs, i)
             parts = [(near[i], CHUNKS[i], 2, starts[i]) for i in group] + [(far[i], CHUNKS[i], 3, starts[i]) for i in group]
-            outs = project(parts, w, owners, outs, tokens)
+            outs = project(parts, w, owners, outs, tokens, resident=group[-1] == len(CHUNKS) - 1)
             for i in after.get(group[0], ()):
                 outs = arrive(outs, i)
         return tuple(outs)

time: 476 us -> 480 us (level)
  waiting for transfers between devices: 145 us -> 133 us
  local copies, waits for them, and re-layouts: 0.02 us -> 9.52 us
  Pallas kernels: 310 us -> 316 us
    ppermute x11, waiting for transfers between devices: 135 us -> 123 us  [inner(): near.append(lax.ppermute(m, 'tp', across))]
    unnamed x12 -> x26, local copies, waits for them, and re-layouts: 0.02 us -> 9.52 us
    pallas_call x11 -> x12, Pallas kernels: 265 us -> 272 us  [project(): pl.pallas_call(body, in_specs=[pl.BlockSpec(memory_space=pltpu.SMEM)] + [...]
  transfers between devices with their start and end apart: 23 -> 23, of which waited for: 12 -> 13; matrix products, arithmetic and copies ran while one was open for 0% -> 0% of each run, Pallas kernels for 58% -> 60%
where the time goes in v5:
time: 480 us; the launch traced here: 479 us
  Pallas kernels  316 us (66%)
  waiting for transfers between devices  133 us (28%)
  starting transfers between devices  19.7 us (4%)
  local copies, waits for them, and re-layouts  9.52 us (2%)
    pallas_call x12, Pallas kernels, project(): pl.pallas_call(body, in_specs=[pl.BlockSpec(memory_space=pltpu.SMEM)] + [...  272 us
    ppermute x11, waiting for transfers between devices, inner(): near.append(lax.ppermute(m, 'tp', across))  123 us
    pallas_call x1, Pallas kernels, normalize_all(): pl.pallas_call(body, grid=(block // step,), in_specs=[pl.BlockSpec((step,...  22.7 us
    ppermute x11, starting transfers between devices, inner(): near.append(lax.ppermute(m, 'tp', across))  17.9 us
    pallas_call x1, Pallas kernels, join_weights(): pl.pallas_call(body, in_specs=[pl.BlockSpec(memory_space=pl.ANY)] * 3, ou...  15.7 us
    ppermute x11, waiting for transfers between devices, arrive(): far[i] = lax.ppermute(a, 'tp', beside)  10 us
  transfers between devices with their start and end apart: 23, of which 13 were waited for; matrix products, arithmetic and copies ran while one was open for 0% of the time, Pallas kernels for 60%

profile of v5, /device:TPU:0, one launch (start us, length us, event | category | flops | bytes accessed | tf_op | source)
XLA Modules:
  0.0 479.5 jit_solution(5815505296719269478)
XLA Ops:
  0.6 22.7 %normalize_all.1 = (bf16[2048,4096]{1,0:T(8,128)(2,1)}, bf16[256,4096]{1,0:T(8,128)(2,1)}, bf16[256,4096]{1,0:T(8,128)(2,1)}, bf16[256,4096]{1,0:T(8,128)(2,1)},...) custom-call(bf16[2048,4096]{1,0:T(8,128)(2,1)} %x_ref.3, ...), custom_call_target="tpu_custom_call" | custom-call | flops 67108864 | bytes 50331648 | tf_op jit(solution)/shard_map/normalize_all/pallas_call | solution.py:130
  26.8 2.8 collective-permute-start.7
  29.6 3.8 normalize_some.1
  35.5 15.7 %join_weights.1.refs_1_.refs_4_.refs_2_ = bf16[6,4096,512]{2,1,0:T(8,128)(2,1)S(1)} custom-call(bf16[4096,8,128]{2,1,0:T(8,128)(2,1)} %a_ref.1, bf16[4096,8,128]{2,1,0:T(8,128)(2,1)} %b_ref.1, bf16[4096,8,128]{2,1,0:T(8,128)(2,1)} %c_ref.1), custom_call_target="tpu_custom_call" | custom-call | flops 25165824 | bytes 25165824 | tf_op jit(solution)/shard_map/join_weights/pallas_call | solution.py:177
  51.2 67.5 %project.12 = (bf16[8192,8,128]{2,1,0:T(8,128)(2,1)}, bf16[8192,8,128]{2,1,0:T(8,128)(2,1)}, bf16[8192,8,128]{2,1,0:T(8,128)(2,1)}) custom-call(s32[4]{0:T(128)S(1)} %iota_xor_fusion.owners_ref, bf16[2048,4096]{1,0:T(8,128)(2,1)} %get-tuple-element.92.refs_0_, bf16[6,4096,512]{2,1,0:T(8,128)(2,1)S(1)} %join_weights.1.refs_1_.refs_4_.refs_2_), custom_call_target="tpu_custom_call" | custom-call | flops 51539607552 | bytes 29360128 | tf_op jit(solution)/shard_map/project/pallas_call | solution.py:291
  120.8 45.2 %collective-permute-done.9.refs_0_ = bf16[256,4096]{1,0:T(8,128)(2,1)S(1)} collective-permute-done((bf16[256,4096]{1,0:T(8,128)(2,1)}, bf16[256,4096]{1,0:T(8,128)(2,1)S(1)}, u32[]{:S(2)}, u32[]{:S(2)}) %collective-permute-start.9) | collective-permute-done | bytes 2097184 | tf_op jit(solution)/shard_map/ppermute | solution.py:335
  166.5 62.6 %project.13 = (bf16[8192,8,128]{2,1,0:T(8,128)(2,1)}, bf16[8192,8,128]{2,1,0:T(8,128)(2,1)}, bf16[8192,8,128]{2,1,0:T(8,128)(2,1)}) custom-call(s32[4]{0:T(128)S(1)} %iota_xor_fusion.owners_ref, bf16[2048,4096]{1,0:T(8,128)(2,1)} %collective-permute-done.14.refs_0_, ...), custom_call_target="tpu_custom_call", output_to_operand_aliasing={{0}: (3, {}), {1}: (4, {}), {2}: (5, {})} | custom-call | flops 51539607552 | bytes 29360128 | tf_op jit(solution)/shard_map/project/pallas_call | solution.py:291
  229.7 18.0 %project.14 = (bf16[8192,8,128]{2,1,0:T(8,128)(2,1)}, bf16[8192,8,128]{2,1,0:T(8,128)(2,1)}, bf16[8192,8,128]{2,1,0:T(8,128)(2,1)}) custom-call(s32[4]{0:T(128)S(1)} %iota_xor_fusion.owners_ref, bf16[64,4096]{1,0:T(8,128)(2,1)S(1)} %collective-permute-done.7.refs_0_, ...), custom_call_target="tpu_custom_call", output_to_operand_aliasing={{0}: (6, {}), {1}: (7, {}), {2}: (8, {})} | custom-call | flops 12884901888 | bytes 7340032 | tf_op jit(solution)/shard_map/project/pallas_call | solution.py:291
  247.8 16.8 %project.15 = (bf16[8192,8,128]{2,1,0:T(8,128)(2,1)}, bf16[8192,8,128]{2,1,0:T(8,128)(2,1)}, bf16[8192,8,128]{2,1,0:T(8,128)(2,1)}) custom-call(s32[4]{0:T(128)S(1)} %iota_xor_fusion.owners_ref, bf16[256,4096]{1,0:T(8,128)(2,1)S(1)} %collective-permute-done.9.refs_0_, ...), custom_call_target="tpu_custom_call", output_to_operand_aliasing={{0}: (4, {}), {1}: (5, {}), {2}: (6, {})} | custom-call | flops 12884901888 | bytes 7340032 | tf_op jit(solution)/shard_map/project/pallas_call | solution.py:291
  266.7 16.8 %project.16 = (bf16[8192,8,128]{2,1,0:T(8,128)(2,1)}, bf16[8192,8,128]{2,1,0:T(8,128)(2,1)}, bf16[8192,8,128]{2,1,0:T(8,128)(2,1)}) custom-call(s32[4]{0:T(128)S(1)} %iota_xor_fusion.owners_ref, bf16[256,4096]{1,0:T(8,128)(2,1)S(1)} %collective-permute-done.13.refs_0_, ...), custom_call_target="tpu_custom_call", output_to_operand_aliasing={{0}: (4, {}), {1}: (5, {}), {2}: (6, {})} | custom-call | flops 12884901888 | bytes 7340032 | tf_op jit(solution)/shard_map/project/pallas_call | solution.py:291
  283.5 18.1 %project.17 = (bf16[8192,8,128]{2,1,0:T(8,128)(2,1)}, bf16[8192,8,128]{2,1,0:T(8,128)(2,1)}, bf16[8192,8,128]{2,1,0:T(8,128)(2,1)}) custom-call(s32[4]{0:T(128)S(1)} %iota_xor_fusion.owners_ref, bf16[256,4096]{1,0:T(8,128)(2,1)} %collective-permute-done.6.refs_0_, ...), custom_call_target="tpu_custom_call", output_to_operand_aliasing={{0}: (4, {}), {1}: (5, {}), {2}: (6, {})} | custom-call | flops 12884901888 | bytes 7340032 | tf_op jit(solution)/shard_map/project/pallas_call | solution.py:291
  301.6 11.3 %collective-permute-done.5.refs_0_ = bf16[256,4096]{1,0:T(8,128)(2,1)S(1)} collective-permute-done((bf16[256,4096]{1,0:T(8,128)(2,1)S(1)}, bf16[256,4096]{1,0:T(8,128)(2,1)S(1)}, u32[]{:S(2)}, u32[]{:S(2)}) %collective-permute-start.5) | collective-permute-done | bytes 2097184 | tf_op jit(solution)/shard_map/ppermute | solution.py:335
  317.1 16.8 %project.18 = (bf16[8192,8,128]{2,1,0:T(8,128)(2,1)}, bf16[8192,8,128]{2,1,0:T(8,128)(2,1)}, bf16[8192,8,128]{2,1,0:T(8,128)(2,1)}) custom-call(s32[4]{0:T(128)S(1)} %iota_xor_fusion.owners_ref, bf16[256,4096]{1,0:T(8,128)(2,1)S(1)} %collective-permute-done.5.refs_0_, ...), custom_call_target="tpu_custom_call", output_to_operand_aliasing={{0}: (4, {}), {1}: (5, {}), {2}: (6, {})} | custom-call | flops 12884901888 | bytes 7340032 | tf_op jit(solution)/shard_map/project/pallas_call | solution.py:291
  333.9 27.1 %collective-permute-done.4.refs_0_ = bf16[256,4096]{1,0:T(8,128)(2,1)S(1)} collective-permute-done((bf16[256,4096]{1,0:T(8,128)(2,1)S(1)}, bf16[256,4096]{1,0:T(8,128)(2,1)S(1)}, u32[]{:S(2)}, u32[]{:S(2)}) %collective-permute-start.4) | collective-permute-done | bytes 2097184 | tf_op jit(solution)/shard_map/ppermute | solution.py:335
  365.1 17.0 %project.19 = (bf16[8192,8,128]{2,1,0:T(8,128)(2,1)}, bf16[8192,8,128]{2,1,0:T(8,128)(2,1)}, bf16[8192,8,128]{2,1,0:T(8,128)(2,1)}) custom-call(s32[4]{0:T(128)S(1)} %iota_xor_fusion.owners_ref, bf16[256,4096]{1,0:T(8,128)(2,1)S(1)} %collective-permute-done.4.refs_0_, ...), custom_call_target="tpu_custom_call", output_to_operand_aliasing={{0}: (4, {}), {1}: (5, {}), {2}: (6, {})} | custom-call | flops 12884901888 | bytes 7340032 | tf_op jit(solution)/shard_map/project/pallas_call | solution.py:291
  382.1 24.1 %collective-permute-done.3.refs_0_ = bf16[240,4096]{1,0:T(8,128)(2,1)S(1)} collective-permute-done((bf16[240,4096]{1,0:T(8,128)(2,1)S(1)}, bf16[240,4096]{1,0:T(8,128)(2,1)S(1)}, u32[]{:S(2)}, u32[]{:S(2)}) %collective-permute-start.3) | collective-permute-done | bytes 1966112 | tf_op jit(solution)/shard_map/ppermute | solution.py:335
  410.2 16.2 %project.20 = (bf16[8192,8,128]{2,1,0:T(8,128)(2,1)}, bf16[8192,8,128]{2,1,0:T(8,128)(2,1)}, bf16[8192,8,128]{2,1,0:T(8,128)(2,1)}) custom-call(s32[4]{0:T(128)S(1)} %iota_xor_fusion.owners_ref, bf16[240,4096]{1,0:T(8,128)(2,1)S(1)} %collective-permute-done.3.refs_0_, ...), custom_call_target="tpu_custom_call", output_to_operand_aliasing={{0}: (4, {}), {1}: (5, {}), {2}: (6, {})} | custom-call | flops 12079595520 | bytes 6881280 | tf_op jit(solution)/shard_map/project/pallas_call | solution.py:291
  426.4 5.4 %collective-permute-done.2.refs_0_ = bf16[128,4096]{1,0:T(8,128)(2,1)S(1)} collective-permute-done((bf16[128,4096]{1,0:T(8,128)(2,1)S(1)}, bf16[128,4096]{1,0:T(8,128)(2,1)S(1)}, u32[]{:S(2)}, u32[]{:S(2)}) %collective-permute-start.2) | collective-permute-done | bytes 1048608 | tf_op jit(solution)/shard_map/ppermute | solution.py:335
  434.5 9.5 %project.21 = (bf16[8192,8,128]{2,1,0:T(8,128)(2,1)}, bf16[8192,8,128]{2,1,0:T(8,128)(2,1)}, bf16[8192,8,128]{2,1,0:T(8,128)(2,1)}) custom-call(s32[4]{0:T(128)S(1)} %iota_xor_fusion.owners_ref, bf16[128,4096]{1,0:T(8,128)(2,1)S(1)} %collective-permute-done.2.refs_0_, ...), custom_call_target="tpu_custom_call", output_to_operand_aliasing={{0}: (4, {}), {1}: (5, {}), {2}: (6, {})} | custom-call | flops 6442450944 | bytes 3670016 | tf_op jit(solution)/shard_map/project/pallas_call | solution.py:291
  443.9 5.0 %collective-permute-done.1.refs_0_ = bf16[80,4096]{1,0:T(8,128)(2,1)S(1)} collective-permute-done((bf16[80,4096]{1,0:T(8,128)(2,1)S(1)}, bf16[80,4096]{1,0:T(8,128)(2,1)S(1)}, u32[]{:S(2)}, u32[]{:S(2)}) %collective-permute-start.1) | collective-permute-done | bytes 655392 | tf_op jit(solution)/shard_map/ppermute | solution.py:335
  451.1 7.2 %project.22 = (bf16[8192,8,128]{2,1,0:T(8,128)(2,1)}, bf16[8192,8,128]{2,1,0:T(8,128)(2,1)}, bf16[8192,8,128]{2,1,0:T(8,128)(2,1)}) custom-call(s32[4]{0:T(128)S(1)} %iota_xor_fusion.owners_ref, bf16[80,4096]{1,0:T(8,128)(2,1)S(1)} %collective-permute-done.1.refs_0_, ...), custom_call_target="tpu_custom_call", output_to_operand_aliasing={{0}: (4, {}), {1}: (5, {}), {2}: (6, {})} | custom-call | flops 4026531840 | bytes 2293760 | tf_op jit(solution)/shard_map/project/pallas_call | solution.py:291
  458.2 5.1 %collective-permute-done.n_ref = bf16[64,4096]{1,0:T(8,128)(2,1)S(1)} collective-permute-done((bf16[64,4096]{1,0:T(8,128)(2,1)S(1)}, bf16[64,4096]{1,0:T(8,128)(2,1)S(1)}, u32[]{:S(2)}, u32[]{:S(2)}) %collective-permute-start) | collective-permute-done | bytes 524320 | tf_op jit(solution)/shard_map/ppermute | solution.py:335
  465.2 8.2 %copy-done.1 = bf16[6,4096,512]{2,1,0:T(8,128)(2,1)S(1)} copy-done((bf16[6,4096,512]{2,1,0:T(8,128)(2,1)S(1)}, bf16[6,4096,512]{2,1,0:T(8,128)(2,1)}, u32[]{:S(2)}) %copy-start.1) | copy-done | bytes 25165848
  473.4 6.0 %project.23 = (bf16[8192,8,128]{2,1,0:T(8,128)(2,1)}, bf16[8192,8,128]{2,1,0:T(8,128)(2,1)}, bf16[8192,8,128]{2,1,0:T(8,128)(2,1)}) custom-call(s32[4]{0:T(128)S(1)} %iota_xor_fusion.owners_ref, bf16[64,4096]{1,0:T(8,128)(2,1)S(1)} %to_vmem.1.refs_0_, ...), custom_call_target="tpu_custom_call", output_to_operand_aliasing={{0}: (4, {}), {1}: (5, {}), {2}: (6, {})} | custom-call | flops 3221225472 | bytes 1835008 | tf_op jit(solution)/shard_map/project/pallas_call | solution.py:291
  (66 shorter events, 29.7 us)
Async XLA Ops:
  24.7 141.8 %collective-permute-start.14 = (bf16[2048,4096]{1,0:T(8,128)(2,1)}, bf16[2048,4096]{1,0:T(8,128)(2,1)}, u32[]{:S(2)}, u32[]{:S(2)}) collective-permute-start(bf16[2048,4096]{1,0:T(8,128)(2,1)} %get-tuple-element.92.refs_0_), channel_id=1, source_target_pairs={{0,1},{1,0},{2,3},{3,2},{4,5},{5,4},{6,7},{7,6},{8,9},{9,8},{10,11... | collective-permute-start | bytes 50331656 | tf_op jit(solution)/shard_map/ppermute | solution.py:336
  26.8 91.9 %collective-permute-start.7 = (bf16[64,4096]{1,0:T(8,128)(2,1)S(1)}, bf16[64,4096]{1,0:T(8,128)(2,1)S(1)}, u32[]{:S(2)}, u32[]{:S(2)}) collective-permute-start(bf16[64,4096]{1,0:T(8,128)(2,1)S(1)} %normalize_first.1), channel_id=1, source_target_pairs={{0,2},{1,3},{2,0},{3,1},{4,6},{5,7},{6,4},{7,5},{8,10},{9,11},{10,... | collective-permute-start | bytes 1572872 | tf_op jit(solution)/shard_map/ppermute | solution.py:332
  33.4 87.4 %collective-permute-start.8 = (bf16[192,4096]{1,0:T(8,128)(2,1)}, bf16[192,4096]{1,0:T(8,128)(2,1)}, u32[]{:S(2)}, u32[]{:S(2)}) collective-permute-start(bf16[192,4096]{1,0:T(8,128)(2,1)} %normalize_some.1), channel_id=1, source_target_pairs={{0,2},{1,3},{2,0},{3,1},{4,6},{5,7},{6,4},{7,5},{8,10},{9,11},{10,... | collective-permute-start | bytes 4718600 | tf_op jit(solution)/shard_map/ppermute | solution.py:332
  33.5 231.1 %collective-permute-start.6 = (bf16[256,4096]{1,0:T(8,128)(2,1)}, bf16[256,4096]{1,0:T(8,128)(2,1)}, u32[]{:S(2)}, u32[]{:S(2)}) collective-permute-start(bf16[256,4096]{1,0:T(8,128)(2,1)} %get-tuple-element.90), channel_id=1, source_target_pairs={{0,2},{1,3},{2,0},{3,1},{4,6},{5,7},{6,4},{7,5},{8,10},{9,11},{10,... | collective-permute-start | bytes 6291464 | tf_op jit(solution)/shard_map/ppermute | solution.py:335
  35.5 130.5 %collective-permute-start.9 = (bf16[256,4096]{1,0:T(8,128)(2,1)}, bf16[256,4096]{1,0:T(8,128)(2,1)S(1)}, u32[]{:S(2)}, u32[]{:S(2)}) collective-permute-start(bf16[256,4096]{1,0:T(8,128)(2,1)} %get-tuple-element.91), channel_id=1, source_target_pairs={{0,2},{1,3},{2,0},{3,1},{4,6},{5,7},{6,4},{7,5},{8,10},{9,11},{10,... | collective-permute-start | bytes 6291464 | tf_op jit(solution)/shard_map/ppermute | solution.py:335
  51.2 399.8 %copy-start = (bf16[6,4096,512]{2,1,0:T(8,128)(2,1)}, bf16[6,4096,512]{2,1,0:T(8,128)(2,1)S(1)}, u32[]{:S(2)}) copy-start(bf16[6,4096,512]{2,1,0:T(8,128)(2,1)S(1)} %join_weights.1.refs_1_.refs_4_.refs_2_) | copy-start | bytes 75497472
  118.7 110.4 %collective-permute-start.13 = (bf16[256,4096]{1,0:T(8,128)(2,1)S(1)}, bf16[256,4096]{1,0:T(8,128)(2,1)S(1)}, u32[]{:S(2)}, u32[]{:S(2)}) collective-permute-start(bf16[256,4096]{1,0:T(8,128)(2,1)S(1)} %copy-done.12), channel_id=1, source_target_pairs={{0,2},{1,3},{2,0},{3,1},{4,6},{5,7},{6,4},{7,5},{8,10},{9,11},{10,... | collective-permute-start | bytes 6291464 | tf_op jit(solution)/shard_map/ppermute | solution.py:335
  166.0 63.7 %collective-permute-start.11 = (bf16[64,4096]{1,0:T(8,128)(2,1)S(1)}, bf16[64,4096]{1,0:T(8,128)(2,1)S(1)}, u32[]{:S(2)}, u32[]{:S(2)}) collective-permute-start(bf16[64,4096]{1,0:T(8,128)(2,1)S(1)} %collective-permute-done.7.refs_0_), channel_id=1, source_target_pairs={{0,1},{1,0},{2,3},{3,2},{4,5},{5,4},{6,7},{7,6},{8,9},{9,8},{10,11... | collective-permute-start | bytes 1572872 | tf_op jit(solution)/shard_map/ppermute | solution.py:345
  166.0 63.7 %collective-permute-start.12 = (bf16[192,4096]{1,0:T(8,128)(2,1)}, bf16[192,4096]{1,0:T(8,128)(2,1)S(1)}, u32[]{:S(2)}, u32[]{:S(2)}) collective-permute-start(bf16[192,4096]{1,0:T(8,128)(2,1)} %collective-permute-done.8.refs_1_), channel_id=1, source_target_pairs={{0,1},{1,0},{2,3},{3,2},{4,5},{5,4},{6,7},{7,6},{8,9},{9,8},{10,11... | collective-permute-start | bytes 4718600 | tf_op jit(solution)/shard_map/ppermute | solution.py:345
  166.5 81.2 %collective-permute-start.10 = (bf16[256,4096]{1,0:T(8,128)(2,1)S(1)}, bf16[256,4096]{1,0:T(8,128)(2,1)S(1)}, u32[]{:S(2)}, u32[]{:S(2)}) collective-permute-start(bf16[256,4096]{1,0:T(8,128)(2,1)S(1)} %collective-permute-done.9.refs_0_), channel_id=1, source_target_pairs={{0,1},{1,0},{2,3},{3,2},{4,5},{5,4},{6,7},{7,6},{8,9},{9,8},{10,11... | collective-permute-start | bytes 6291464 | tf_op jit(solution)/shard_map/ppermute | solution.py:345
  229.2 37.5 %collective-permute-start.16 = (bf16[256,4096]{1,0:T(8,128)(2,1)S(1)}, bf16[256,4096]{1,0:T(8,128)(2,1)S(1)}, u32[]{:S(2)}, u32[]{:S(2)}) collective-permute-start(bf16[256,4096]{1,0:T(8,128)(2,1)S(1)} %collective-permute-done.13.refs_0_), channel_id=1, source_target_pairs={{0,1},{1,0},{2,3},{3,2},{4,5},{5,4},{6,7},{7,6},{8,9},{9,8},{10,11... | collective-permute-start | bytes 6291464 | tf_op jit(solution)/shard_map/ppermute | solution.py:345
  264.6 18.9 %collective-permute-start.15 = (bf16[256,4096]{1,0:T(8,128)(2,1)}, bf16[256,4096]{1,0:T(8,128)(2,1)S(1)}, u32[]{:S(2)}, u32[]{:S(2)}) collective-permute-start(bf16[256,4096]{1,0:T(8,128)(2,1)} %collective-permute-done.6.refs_0_), channel_id=1, source_target_pairs={{0,1},{1,0},{2,3},{3,2},{4,5},{5,4},{6,7},{7,6},{8,9},{9,8},{10,11... | collective-permute-start | bytes 6291464 | tf_op jit(solution)/shard_map/ppermute | solution.py:345
  264.6 48.3 %collective-permute-start.5 = (bf16[256,4096]{1,0:T(8,128)(2,1)S(1)}, bf16[256,4096]{1,0:T(8,128)(2,1)S(1)}, u32[]{:S(2)}, u32[]{:S(2)}) collective-permute-start(bf16[256,4096]{1,0:T(8,128)(2,1)S(1)} %copy-done.11), channel_id=1, source_target_pairs={{0,2},{1,3},{2,0},{3,1},{4,6},{5,7},{6,4},{7,5},{8,10},{9,11},{10,... | collective-permute-start | bytes 6291464 | tf_op jit(solution)/shard_map/ppermute | solution.py:335
  312.9 4.2 collective-permute-start.17
  312.9 48.0 %collective-permute-start.4 = (bf16[256,4096]{1,0:T(8,128)(2,1)S(1)}, bf16[256,4096]{1,0:T(8,128)(2,1)S(1)}, u32[]{:S(2)}, u32[]{:S(2)}) collective-permute-start(bf16[256,4096]{1,0:T(8,128)(2,1)S(1)} %copy-done.10), channel_id=1, source_target_pairs={{0,2},{1,3},{2,0},{3,1},{4,6},{5,7},{6,4},{7,5},{8,10},{9,11},{10,... | collective-permute-start | bytes 6291464 | tf_op jit(solution)/shard_map/ppermute | solution.py:335
  361.0 4.2 collective-permute-start.18
  361.0 45.2 %collective-permute-start.3 = (bf16[240,4096]{1,0:T(8,128)(2,1)S(1)}, bf16[240,4096]{1,0:T(8,128)(2,1)S(1)}, u32[]{:S(2)}, u32[]{:S(2)}) collective-permute-start(bf16[240,4096]{1,0:T(8,128)(2,1)S(1)} %copy-done.3), channel_id=1, source_target_pairs={{0,2},{1,3},{2,0},{3,1},{4,6},{5,7},{6,4},{7,5},{8,10},{9,11},{10,... | collective-permute-start | bytes 5898248 | tf_op jit(solution)/shard_map/ppermute | solution.py:335
  406.2 4.0 collective-permute-start.19
  406.2 25.6 %collective-permute-start.2 = (bf16[128,4096]{1,0:T(8,128)(2,1)S(1)}, bf16[128,4096]{1,0:T(8,128)(2,1)S(1)}, u32[]{:S(2)}, u32[]{:S(2)}) collective-permute-start(bf16[128,4096]{1,0:T(8,128)(2,1)S(1)} %copy-done.5), channel_id=1, source_target_pairs={{0,2},{1,3},{2,0},{3,1},{4,6},{5,7},{6,4},{7,5},{8,10},{9,11},{10,... | collective-permute-start | bytes 3145736 | tf_op jit(solution)/shard_map/ppermute | solution.py:335
  431.8 2.7 collective-permute-start.20
  431.8 17.1 %collective-permute-start.1 = (bf16[80,4096]{1,0:T(8,128)(2,1)S(1)}, bf16[80,4096]{1,0:T(8,128)(2,1)S(1)}, u32[]{:S(2)}, u32[]{:S(2)}) collective-permute-start(bf16[80,4096]{1,0:T(8,128)(2,1)S(1)} %copy-done.7), channel_id=1, source_target_pairs={{0,2},{1,3},{2,0},{3,1},{4,6},{5,7},{6,4},{7,5},{8,10},{9,11},{10,... | collective-permute-start | bytes 1966088 | tf_op jit(solution)/shard_map/ppermute | solution.py:335
  449.0 2.1 collective-permute-start.21
  449.0 14.3 %collective-permute-start = (bf16[64,4096]{1,0:T(8,128)(2,1)S(1)}, bf16[64,4096]{1,0:T(8,128)(2,1)S(1)}, u32[]{:S(2)}, u32[]{:S(2)}) collective-permute-start(bf16[64,4096]{1,0:T(8,128)(2,1)S(1)} %copy-done.9), channel_id=1, source_target_pairs={{0,2},{1,3},{2,0},{3,1},{4,6},{5,7},{6,4},{7,5},{8,10},{9,11},{10,... | collective-permute-start | bytes 1572872 | tf_op jit(solution)/shard_map/ppermute | solution.py:335
  463.3 1.9 collective-permute-start.22
  (12 other events, 285.4 us)

commit v6 on v5

--- a/solution.py
+++ b/solution.py
@@ -188,23 +188,6 @@
         cost_estimate=pl.CostEstimate(flops=6 * dim * COLS, bytes_accessed=6 * dim * COLS, transcendentals=0),
         name="join_weights",
     )(*weights)
-
-
-def to_vmem(n):
-    def body(n_ref, out_ref, sem):
-        pltpu.make_async_copy(n_ref, out_ref, sem).start()
-        pltpu.make_async_copy(n_ref, out_ref, sem).wait()
-
-    return pl.pallas_call(
-        body,
-        in_specs=[pl.BlockSpec(memory_space=pl.ANY)],
-        out_specs=pl.BlockSpec(memory_space=pltpu.VMEM),
-        out_shape=pltpu.VMEM(n.shape, n.dtype),
-        scratch_shapes=[pltpu.SemaphoreType.DMA],
-        compiler_params=pltpu.CompilerParams(vmem_limit_bytes=MIB),
-        cost_estimate=pl.CostEstimate(flops=n.size, bytes_accessed=4 * n.size, transcendentals=0),
-        name="to_vmem",
-    )(n)
 
 
 def project(parts, w, owners, outs, tokens, resident=False):
@@ -343,8 +326,6 @@
             for i, a in zip(chunks, got[0]):
                 near[i] = a
                 far[i] = lax.ppermute(a, "tp", beside)
-                if i == len(CHUNKS) - 1:
-                    near[i] = to_vmem(a)
             return got[1]
 
         outs = project([(own, BIG, 0, 0)], w, owners, (), tokens)

time: 480 us -> 472 us (0.983)
  local copies, waits for them, and re-layouts: 9.52 us -> 1.34 us
  Pallas kernels: 316 us -> 311 us
  waiting for transfers between devices: 133 us -> 138 us
    unnamed x26 -> x22, local copies, waits for them, and re-layouts: 9.52 us -> 1.34 us
where the time goes in v6:
time: 472 us; the launch traced here: 471 us
  Pallas kernels  311 us (66%)
  waiting for transfers between devices  138 us (29%)
  starting transfers between devices  19.7 us (4%)
    pallas_call x12, Pallas kernels, project(): pl.pallas_call(body, in_specs=[pl.BlockSpec(memory_space=pltpu.SMEM)] + [...  268 us
    ppermute x11, waiting for transfers between devices, inner(): near.append(lax.ppermute(m, 'tp', across))  128 us
    pallas_call x1, Pallas kernels, normalize_all(): pl.pallas_call(body, grid=(block // step,), in_specs=[pl.BlockSpec((step,...  22.7 us
    ppermute x11, starting transfers between devices, inner(): near.append(lax.ppermute(m, 'tp', across))  17.9 us
    pallas_call x1, Pallas kernels, join_weights(): pl.pallas_call(body, in_specs=[pl.BlockSpec(memory_space=pl.ANY)] * 3, ou...  15.7 us
    ppermute x11, waiting for transfers between devices, arrive(): far[i] = lax.ppermute(a, 'tp', beside)  10.1 us
  transfers between devices with their start and end apart: 23, of which 13 were waited for; matrix products, arithmetic and copies ran while one was open for 0% of the time, Pallas kernels for 60%

profile of v6, /device:TPU:0, one launch (start us, length us, event | category | flops | bytes accessed | tf_op | source)
XLA Modules:
  0.0 471.3 jit_solution(13665955958125812334)
XLA Ops:
  0.6 22.7 %normalize_all.1 = (bf16[2048,4096]{1,0:T(8,128)(2,1)}, bf16[256,4096]{1,0:T(8,128)(2,1)}, bf16[256,4096]{1,0:T(8,128)(2,1)}, bf16[256,4096]{1,0:T(8,128)(2,1)},...) custom-call(bf16[2048,4096]{1,0:T(8,128)(2,1)} %x_ref.3, ...), custom_call_target="tpu_custom_call" | custom-call | flops 67108864 | bytes 50331648 | tf_op jit(solution)/shard_map/normalize_all/pallas_call | solution.py:130
  26.7 2.8 collective-permute-start.7
  29.6 3.8 normalize_some.1
  35.5 15.7 %join_weights.1.refs_1_.refs_4_.refs_2_ = bf16[6,4096,512]{2,1,0:T(8,128)(2,1)S(1)} custom-call(bf16[4096,8,128]{2,1,0:T(8,128)(2,1)} %a_ref.1, bf16[4096,8,128]{2,1,0:T(8,128)(2,1)} %b_ref.1, bf16[4096,8,128]{2,1,0:T(8,128)(2,1)} %c_ref.1), custom_call_target="tpu_custom_call" | custom-call | flops 25165824 | bytes 25165824 | tf_op jit(solution)/shard_map/join_weights/pallas_call | solution.py:177
  51.2 62.7 %project.12 = (bf16[8192,8,128]{2,1,0:T(8,128)(2,1)}, bf16[8192,8,128]{2,1,0:T(8,128)(2,1)}, bf16[8192,8,128]{2,1,0:T(8,128)(2,1)}) custom-call(s32[4]{0:T(128)S(1)} %iota_xor_fusion.owners_ref, bf16[2048,4096]{1,0:T(8,128)(2,1)} %get-tuple-element.92.refs_0_, bf16[6,4096,512]{2,1,0:T(8,128)(2,1)S(1)} %join_weights.1.refs_1_.refs_4_.refs_2_), custom_call_target="tpu_custom_call" | custom-call | flops 51539607552 | bytes 29360128 | tf_op jit(solution)/shard_map/project/pallas_call | solution.py:274
  116.0 50.0 %collective-permute-done.9.refs_0_ = bf16[256,4096]{1,0:T(8,128)(2,1)S(1)} collective-permute-done((bf16[256,4096]{1,0:T(8,128)(2,1)}, bf16[256,4096]{1,0:T(8,128)(2,1)S(1)}, u32[]{:S(2)}, u32[]{:S(2)}) %collective-permute-start.9) | collective-permute-done | bytes 2097184 | tf_op jit(solution)/shard_map/ppermute | solution.py:318
  166.5 62.6 %project.13 = (bf16[8192,8,128]{2,1,0:T(8,128)(2,1)}, bf16[8192,8,128]{2,1,0:T(8,128)(2,1)}, bf16[8192,8,128]{2,1,0:T(8,128)(2,1)}) custom-call(s32[4]{0:T(128)S(1)} %iota_xor_fusion.owners_ref, bf16[2048,4096]{1,0:T(8,128)(2,1)} %collective-permute-done.14.refs_0_, ...), custom_call_target="tpu_custom_call", output_to_operand_aliasing={{0}: (3, {}), {1}: (4, {}), {2}: (5, {})} | custom-call | flops 51539607552 | bytes 29360128 | tf_op jit(solution)/shard_map/project/pallas_call | solution.py:274
  229.7 18.0 %project.14 = (bf16[8192,8,128]{2,1,0:T(8,128)(2,1)}, bf16[8192,8,128]{2,1,0:T(8,128)(2,1)}, bf16[8192,8,128]{2,1,0:T(8,128)(2,1)}) custom-call(s32[4]{0:T(128)S(1)} %iota_xor_fusion.owners_ref, bf16[64,4096]{1,0:T(8,128)(2,1)S(1)} %collective-permute-done.7.refs_0_, ...), custom_call_target="tpu_custom_call", output_to_operand_aliasing={{0}: (6, {}), {1}: (7, {}), {2}: (8, {})} | custom-call | flops 12884901888 | bytes 7340032 | tf_op jit(solution)/shard_map/project/pallas_call | solution.py:274
  247.7 16.8 %project.15 = (bf16[8192,8,128]{2,1,0:T(8,128)(2,1)}, bf16[8192,8,128]{2,1,0:T(8,128)(2,1)}, bf16[8192,8,128]{2,1,0:T(8,128)(2,1)}) custom-call(s32[4]{0:T(128)S(1)} %iota_xor_fusion.owners_ref, bf16[256,4096]{1,0:T(8,128)(2,1)S(1)} %collective-permute-done.9.refs_0_, ...), custom_call_target="tpu_custom_call", output_to_operand_aliasing={{0}: (4, {}), {1}: (5, {}), {2}: (6, {})} | custom-call | flops 12884901888 | bytes 7340032 | tf_op jit(solution)/shard_map/project/pallas_call | solution.py:274
  266.6 16.8 %project.16 = (bf16[8192,8,128]{2,1,0:T(8,128)(2,1)}, bf16[8192,8,128]{2,1,0:T(8,128)(2,1)}, bf16[8192,8,128]{2,1,0:T(8,128)(2,1)}) custom-call(s32[4]{0:T(128)S(1)} %iota_xor_fusion.owners_ref, bf16[256,4096]{1,0:T(8,128)(2,1)S(1)} %collective-permute-done.13.refs_0_, ...), custom_call_target="tpu_custom_call", output_to_operand_aliasing={{0}: (4, {}), {1}: (5, {}), {2}: (6, {})} | custom-call | flops 12884901888 | bytes 7340032 | tf_op jit(solution)/shard_map/project/pallas_call | solution.py:274
  283.4 18.1 %project.17 = (bf16[8192,8,128]{2,1,0:T(8,128)(2,1)}, bf16[8192,8,128]{2,1,0:T(8,128)(2,1)}, bf16[8192,8,128]{2,1,0:T(8,128)(2,1)}) custom-call(s32[4]{0:T(128)S(1)} %iota_xor_fusion.owners_ref, bf16[256,4096]{1,0:T(8,128)(2,1)} %collective-permute-done.6.refs_0_, ...), custom_call_target="tpu_custom_call", output_to_operand_aliasing={{0}: (4, {}), {1}: (5, {}), {2}: (6, {})} | custom-call | flops 12884901888 | bytes 7340032 | tf_op jit(solution)/shard_map/project/pallas_call | solution.py:274
  301.6 11.3 %collective-permute-done.5.refs_0_ = bf16[256,4096]{1,0:T(8,128)(2,1)S(1)} collective-permute-done((bf16[256,4096]{1,0:T(8,128)(2,1)S(1)}, bf16[256,4096]{1,0:T(8,128)(2,1)S(1)}, u32[]{:S(2)}, u32[]{:S(2)}) %collective-permute-start.5) | collective-permute-done | bytes 2097184 | tf_op jit(solution)/shard_map/ppermute | solution.py:318
  317.0 16.8 %project.18 = (bf16[8192,8,128]{2,1,0:T(8,128)(2,1)}, bf16[8192,8,128]{2,1,0:T(8,128)(2,1)}, bf16[8192,8,128]{2,1,0:T(8,128)(2,1)}) custom-call(s32[4]{0:T(128)S(1)} %iota_xor_fusion.owners_ref, bf16[256,4096]{1,0:T(8,128)(2,1)S(1)} %collective-permute-done.5.refs_0_, ...), custom_call_target="tpu_custom_call", output_to_operand_aliasing={{0}: (4, {}), {1}: (5, {}), {2}: (6, {})} | custom-call | flops 12884901888 | bytes 7340032 | tf_op jit(solution)/shard_map/project/pallas_call | solution.py:274
  333.8 27.1 %collective-permute-done.4.refs_0_ = bf16[256,4096]{1,0:T(8,128)(2,1)S(1)} collective-permute-done((bf16[256,4096]{1,0:T(8,128)(2,1)S(1)}, bf16[256,4096]{1,0:T(8,128)(2,1)S(1)}, u32[]{:S(2)}, u32[]{:S(2)}) %collective-permute-start.4) | collective-permute-done | bytes 2097184 | tf_op jit(solution)/shard_map/ppermute | solution.py:318
  362.7 2.4 collective-permute-done.18.refs_1_
  365.1 17.0 %project.19 = (bf16[8192,8,128]{2,1,0:T(8,128)(2,1)}, bf16[8192,8,128]{2,1,0:T(8,128)(2,1)}, bf16[8192,8,128]{2,1,0:T(8,128)(2,1)}) custom-call(s32[4]{0:T(128)S(1)} %iota_xor_fusion.owners_ref, bf16[256,4096]{1,0:T(8,128)(2,1)S(1)} %collective-permute-done.4.refs_0_, ...), custom_call_target="tpu_custom_call", output_to_operand_aliasing={{0}: (4, {}), {1}: (5, {}), {2}: (6, {})} | custom-call | flops 12884901888 | bytes 7340032 | tf_op jit(solution)/shard_map/project/pallas_call | solution.py:274
  382.0 24.1 %collective-permute-done.3.refs_0_ = bf16[240,4096]{1,0:T(8,128)(2,1)S(1)} collective-permute-done((bf16[240,4096]{1,0:T(8,128)(2,1)S(1)}, bf16[240,4096]{1,0:T(8,128)(2,1)S(1)}, u32[]{:S(2)}, u32[]{:S(2)}) %collective-permute-start.3) | collective-permute-done | bytes 1966112 | tf_op jit(solution)/shard_map/ppermute | solution.py:318
  410.1 16.2 %project.20 = (bf16[8192,8,128]{2,1,0:T(8,128)(2,1)}, bf16[8192,8,128]{2,1,0:T(8,128)(2,1)}, bf16[8192,8,128]{2,1,0:T(8,128)(2,1)}) custom-call(s32[4]{0:T(128)S(1)} %iota_xor_fusion.owners_ref, bf16[240,4096]{1,0:T(8,128)(2,1)S(1)} %collective-permute-done.3.refs_0_, ...), custom_call_target="tpu_custom_call", output_to_operand_aliasing={{0}: (4, {}), {1}: (5, {}), {2}: (6, {})} | custom-call | flops 12079595520 | bytes 6881280 | tf_op jit(solution)/shard_map/project/pallas_call | solution.py:274
  426.3 5.4 %collective-permute-done.2.refs_0_ = bf16[128,4096]{1,0:T(8,128)(2,1)S(1)} collective-permute-done((bf16[128,4096]{1,0:T(8,128)(2,1)S(1)}, bf16[128,4096]{1,0:T(8,128)(2,1)S(1)}, u32[]{:S(2)}, u32[]{:S(2)}) %collective-permute-start.2) | collective-permute-done | bytes 1048608 | tf_op jit(solution)/shard_map/ppermute | solution.py:318
  434.4 9.5 %project.21 = (bf16[8192,8,128]{2,1,0:T(8,128)(2,1)}, bf16[8192,8,128]{2,1,0:T(8,128)(2,1)}, bf16[8192,8,128]{2,1,0:T(8,128)(2,1)}) custom-call(s32[4]{0:T(128)S(1)} %iota_xor_fusion.owners_ref, bf16[128,4096]{1,0:T(8,128)(2,1)S(1)} %collective-permute-done.2.refs_0_, ...), custom_call_target="tpu_custom_call", output_to_operand_aliasing={{0}: (4, {}), {1}: (5, {}), {2}: (6, {})} | custom-call | flops 6442450944 | bytes 3670016 | tf_op jit(solution)/shard_map/project/pallas_call | solution.py:274
  443.9 5.0 %collective-permute-done.1.refs_0_ = bf16[80,4096]{1,0:T(8,128)(2,1)S(1)} collective-permute-done((bf16[80,4096]{1,0:T(8,128)(2,1)S(1)}, bf16[80,4096]{1,0:T(8,128)(2,1)S(1)}, u32[]{:S(2)}, u32[]{:S(2)}) %collective-permute-start.1) | collective-permute-done | bytes 655392 | tf_op jit(solution)/shard_map/ppermute | solution.py:318
  451.0 7.2 %project.22 = (bf16[8192,8,128]{2,1,0:T(8,128)(2,1)}, bf16[8192,8,128]{2,1,0:T(8,128)(2,1)}, bf16[8192,8,128]{2,1,0:T(8,128)(2,1)}) custom-call(s32[4]{0:T(128)S(1)} %iota_xor_fusion.owners_ref, bf16[80,4096]{1,0:T(8,128)(2,1)S(1)} %collective-permute-done.1.refs_0_, ...), custom_call_target="tpu_custom_call", output_to_operand_aliasing={{0}: (4, {}), {1}: (5, {}), {2}: (6, {})} | custom-call | flops 4026531840 | bytes 2293760 | tf_op jit(solution)/shard_map/project/pallas_call | solution.py:274
  458.2 5.1 %collective-permute-done.refs_0_ = bf16[64,4096]{1,0:T(8,128)(2,1)S(1)} collective-permute-done((bf16[64,4096]{1,0:T(8,128)(2,1)S(1)}, bf16[64,4096]{1,0:T(8,128)(2,1)S(1)}, u32[]{:S(2)}, u32[]{:S(2)}) %collective-permute-start) | collective-permute-done | bytes 524320 | tf_op jit(solution)/shard_map/ppermute | solution.py:318
  465.1 6.0 %project.23 = (bf16[8192,8,128]{2,1,0:T(8,128)(2,1)}, bf16[8192,8,128]{2,1,0:T(8,128)(2,1)}, bf16[8192,8,128]{2,1,0:T(8,128)(2,1)}) custom-call(s32[4]{0:T(128)S(1)} %iota_xor_fusion.owners_ref, bf16[64,4096]{1,0:T(8,128)(2,1)S(1)} %collective-permute-done.refs_0_, ...), custom_call_target="tpu_custom_call", output_to_operand_aliasing={{0}: (4, {}), {1}: (5, {}), {2}: (6, {})} | custom-call | flops 3221225472 | bytes 1835008 | tf_op jit(solution)/shard_map/project/pallas_call | solution.py:274
  (61 shorter events, 27.3 us)
Async XLA Ops:
  24.7 141.8 %collective-permute-start.14 = (bf16[2048,4096]{1,0:T(8,128)(2,1)}, bf16[2048,4096]{1,0:T(8,128)(2,1)}, u32[]{:S(2)}, u32[]{:S(2)}) collective-permute-start(bf16[2048,4096]{1,0:T(8,128)(2,1)} %get-tuple-element.92.refs_0_), channel_id=1, source_target_pairs={{0,1},{1,0},{2,3},{3,2},{4,5},{5,4},{6,7},{7,6},{8,9},{9,8},{10,11... | collective-permute-start | bytes 50331656 | tf_op jit(solution)/shard_map/ppermute | solution.py:319
  26.7 87.2 %collective-permute-start.7 = (bf16[64,4096]{1,0:T(8,128)(2,1)S(1)}, bf16[64,4096]{1,0:T(8,128)(2,1)S(1)}, u32[]{:S(2)}, u32[]{:S(2)}) collective-permute-start(bf16[64,4096]{1,0:T(8,128)(2,1)S(1)} %normalize_first.1), channel_id=1, source_target_pairs={{0,2},{1,3},{2,0},{3,1},{4,6},{5,7},{6,4},{7,5},{8,10},{9,11},{10,... | collective-permute-start | bytes 1572872 | tf_op jit(solution)/shard_map/ppermute | solution.py:315
  33.3 82.6 %collective-permute-start.8 = (bf16[192,4096]{1,0:T(8,128)(2,1)}, bf16[192,4096]{1,0:T(8,128)(2,1)}, u32[]{:S(2)}, u32[]{:S(2)}) collective-permute-start(bf16[192,4096]{1,0:T(8,128)(2,1)} %normalize_some.1), channel_id=1, source_target_pairs={{0,2},{1,3},{2,0},{3,1},{4,6},{5,7},{6,4},{7,5},{8,10},{9,11},{10,... | collective-permute-start | bytes 4718600 | tf_op jit(solution)/shard_map/ppermute | solution.py:315
  33.4 231.1 %collective-permute-start.6 = (bf16[256,4096]{1,0:T(8,128)(2,1)}, bf16[256,4096]{1,0:T(8,128)(2,1)}, u32[]{:S(2)}, u32[]{:S(2)}) collective-permute-start(bf16[256,4096]{1,0:T(8,128)(2,1)} %get-tuple-element.90), channel_id=1, source_target_pairs={{0,2},{1,3},{2,0},{3,1},{4,6},{5,7},{6,4},{7,5},{8,10},{9,11},{10,... | collective-permute-start | bytes 6291464 | tf_op jit(solution)/shard_map/ppermute | solution.py:318
  35.4 130.5 %collective-permute-start.9 = (bf16[256,4096]{1,0:T(8,128)(2,1)}, bf16[256,4096]{1,0:T(8,128)(2,1)S(1)}, u32[]{:S(2)}, u32[]{:S(2)}) collective-permute-start(bf16[256,4096]{1,0:T(8,128)(2,1)} %get-tuple-element.91), channel_id=1, source_target_pairs={{0,2},{1,3},{2,0},{3,1},{4,6},{5,7},{6,4},{7,5},{8,10},{9,11},{10,... | collective-permute-start | bytes 6291464 | tf_op jit(solution)/shard_map/ppermute | solution.py:318
  51.2 62.8 %copy-start.10 = (bf16[256,4096]{1,0:T(8,128)(2,1)S(1)}, bf16[256,4096]{1,0:T(8,128)(2,1)}, u32[]{:S(2)}) copy-start(bf16[256,4096]{1,0:T(8,128)(2,1)} %get-tuple-element.99) | copy-start | bytes 6291460
  114.0 115.2 %collective-permute-start.13 = (bf16[256,4096]{1,0:T(8,128)(2,1)S(1)}, bf16[256,4096]{1,0:T(8,128)(2,1)S(1)}, u32[]{:S(2)}, u32[]{:S(2)}) collective-permute-start(bf16[256,4096]{1,0:T(8,128)(2,1)S(1)} %copy-done.10), channel_id=1, source_target_pairs={{0,2},{1,3},{2,0},{3,1},{4,6},{5,7},{6,4},{7,5},{8,10},{9,11},{10,... | collective-permute-start | bytes 6291464 | tf_op jit(solution)/shard_map/ppermute | solution.py:318
  165.9 63.7 %collective-permute-start.11 = (bf16[64,4096]{1,0:T(8,128)(2,1)S(1)}, bf16[64,4096]{1,0:T(8,128)(2,1)S(1)}, u32[]{:S(2)}, u32[]{:S(2)}) collective-permute-start(bf16[64,4096]{1,0:T(8,128)(2,1)S(1)} %collective-permute-done.7.refs_0_), channel_id=1, source_target_pairs={{0,1},{1,0},{2,3},{3,2},{4,5},{5,4},{6,7},{7,6},{8,9},{9,8},{10,11... | collective-permute-start | bytes 1572872 | tf_op jit(solution)/shard_map/ppermute | solution.py:328
  165.9 63.7 %collective-permute-start.12 = (bf16[192,4096]{1,0:T(8,128)(2,1)}, bf16[192,4096]{1,0:T(8,128)(2,1)S(1)}, u32[]{:S(2)}, u32[]{:S(2)}) collective-permute-start(bf16[192,4096]{1,0:T(8,128)(2,1)} %collective-permute-done.8.refs_1_), channel_id=1, source_target_pairs={{0,1},{1,0},{2,3},{3,2},{4,5},{5,4},{6,7},{7,6},{8,9},{9,8},{10,11... | collective-permute-start | bytes 4718600 | tf_op jit(solution)/shard_map/ppermute | solution.py:328
  166.4 81.2 %collective-permute-start.10 = (bf16[256,4096]{1,0:T(8,128)(2,1)S(1)}, bf16[256,4096]{1,0:T(8,128)(2,1)S(1)}, u32[]{:S(2)}, u32[]{:S(2)}) collective-permute-start(bf16[256,4096]{1,0:T(8,128)(2,1)S(1)} %collective-permute-done.9.refs_0_), channel_id=1, source_target_pairs={{0,1},{1,0},{2,3},{3,2},{4,5},{5,4},{6,7},{7,6},{8,9},{9,8},{10,11... | collective-permute-start | bytes 6291464 | tf_op jit(solution)/shard_map/ppermute | solution.py:328
  229.1 37.5 %collective-permute-start.16 = (bf16[256,4096]{1,0:T(8,128)(2,1)S(1)}, bf16[256,4096]{1,0:T(8,128)(2,1)S(1)}, u32[]{:S(2)}, u32[]{:S(2)}) collective-permute-start(bf16[256,4096]{1,0:T(8,128)(2,1)S(1)} %collective-permute-done.13.refs_0_), channel_id=1, source_target_pairs={{0,1},{1,0},{2,3},{3,2},{4,5},{5,4},{6,7},{7,6},{8,9},{9,8},{10,11... | collective-permute-start | bytes 6291464 | tf_op jit(solution)/shard_map/ppermute | solution.py:328
  264.5 18.9 %collective-permute-start.15 = (bf16[256,4096]{1,0:T(8,128)(2,1)}, bf16[256,4096]{1,0:T(8,128)(2,1)S(1)}, u32[]{:S(2)}, u32[]{:S(2)}) collective-permute-start(bf16[256,4096]{1,0:T(8,128)(2,1)} %collective-permute-done.6.refs_0_), channel_id=1, source_target_pairs={{0,1},{1,0},{2,3},{3,2},{4,5},{5,4},{6,7},{7,6},{8,9},{9,8},{10,11... | collective-permute-start | bytes 6291464 | tf_op jit(solution)/shard_map/ppermute | solution.py:328
  264.6 48.3 %collective-permute-start.5 = (bf16[256,4096]{1,0:T(8,128)(2,1)S(1)}, bf16[256,4096]{1,0:T(8,128)(2,1)S(1)}, u32[]{:S(2)}, u32[]{:S(2)}) collective-permute-start(bf16[256,4096]{1,0:T(8,128)(2,1)S(1)} %copy-done.9), channel_id=1, source_target_pairs={{0,2},{1,3},{2,0},{3,1},{4,6},{5,7},{6,4},{7,5},{8,10},{9,11},{10,... | collective-permute-start | bytes 6291464 | tf_op jit(solution)/shard_map/ppermute | solution.py:318
  312.9 4.2 collective-permute-start.17
  312.9 48.0 %collective-permute-start.4 = (bf16[256,4096]{1,0:T(8,128)(2,1)S(1)}, bf16[256,4096]{1,0:T(8,128)(2,1)S(1)}, u32[]{:S(2)}, u32[]{:S(2)}) collective-permute-start(bf16[256,4096]{1,0:T(8,128)(2,1)S(1)} %copy-done.8), channel_id=1, source_target_pairs={{0,2},{1,3},{2,0},{3,1},{4,6},{5,7},{6,4},{7,5},{8,10},{9,11},{10,... | collective-permute-start | bytes 6291464 | tf_op jit(solution)/shard_map/ppermute | solution.py:318
  360.9 4.2 collective-permute-start.18
  360.9 45.2 %collective-permute-start.3 = (bf16[240,4096]{1,0:T(8,128)(2,1)S(1)}, bf16[240,4096]{1,0:T(8,128)(2,1)S(1)}, u32[]{:S(2)}, u32[]{:S(2)}) collective-permute-start(bf16[240,4096]{1,0:T(8,128)(2,1)S(1)} %copy-done.1), channel_id=1, source_target_pairs={{0,2},{1,3},{2,0},{3,1},{4,6},{5,7},{6,4},{7,5},{8,10},{9,11},{10,... | collective-permute-start | bytes 5898248 | tf_op jit(solution)/shard_map/ppermute | solution.py:318
  406.2 4.0 collective-permute-start.19
  406.2 25.6 %collective-permute-start.2 = (bf16[128,4096]{1,0:T(8,128)(2,1)S(1)}, bf16[128,4096]{1,0:T(8,128)(2,1)S(1)}, u32[]{:S(2)}, u32[]{:S(2)}) collective-permute-start(bf16[128,4096]{1,0:T(8,128)(2,1)S(1)} %copy-done.3), channel_id=1, source_target_pairs={{0,2},{1,3},{2,0},{3,1},{4,6},{5,7},{6,4},{7,5},{8,10},{9,11},{10,... | collective-permute-start | bytes 3145736 | tf_op jit(solution)/shard_map/ppermute | solution.py:318
  431.7 2.7 collective-permute-start.20
  431.8 17.1 %collective-permute-start.1 = (bf16[80,4096]{1,0:T(8,128)(2,1)S(1)}, bf16[80,4096]{1,0:T(8,128)(2,1)S(1)}, u32[]{:S(2)}, u32[]{:S(2)}) collective-permute-start(bf16[80,4096]{1,0:T(8,128)(2,1)S(1)} %copy-done.5), channel_id=1, source_target_pairs={{0,2},{1,3},{2,0},{3,1},{4,6},{5,7},{6,4},{7,5},{8,10},{9,11},{10,... | collective-permute-start | bytes 1966088 | tf_op jit(solution)/shard_map/ppermute | solution.py:318
  448.9 2.1 collective-permute-start.21
  448.9 14.3 %collective-permute-start = (bf16[64,4096]{1,0:T(8,128)(2,1)S(1)}, bf16[64,4096]{1,0:T(8,128)(2,1)S(1)}, u32[]{:S(2)}, u32[]{:S(2)}) collective-permute-start(bf16[64,4096]{1,0:T(8,128)(2,1)S(1)} %copy-done.7), channel_id=1, source_target_pairs={{0,2},{1,3},{2,0},{3,1},{4,6},{5,7},{6,4},{7,5},{8,10},{9,11},{10,... | collective-permute-start | bytes 1572872 | tf_op jit(solution)/shard_map/ppermute | solution.py:318
  463.2 1.9 collective-permute-start.22
  (10 other events, 209.7 us)
